TPU v7x, 32 devices: a whole 2x2x4 slice. The times are simulated.
32 devices in a mesh: freq: 8 (over z, core), rows: 4 (over y, x).
Axes of the slice: x: 2, y: 2, z: 4, core: 2. Of those that a mesh axis runs over, the one named last changes fastest.
Arguments:
- wavefield: float32 [2, 8, 1024, 2048], P(None, 'freq', 'rows'), may hold values from -28 to 28
- block_inverse: bfloat16 [2, 8, 16, 128, 128], P(None, 'freq'), may hold values from -0.19921875 to 0.19921875
- coefficient: bfloat16 [1024, 2048], P('rows'), may hold values from 0.049804688 to 0.29882812
- correction_factor: float32 [2, 8], P(None, 'freq'), may hold values from -4 to 4
- frequencies: float32 [8], P('freq'), may hold values from 1.5 to 4.5
- slowness: float32 [2], replicated, may hold values from 0.7 to 1
Outputs:
- depth_image: float32 [2, 1024, 2048], P(None, 'rows', 'freq')
- final_field: float32 [2, 8, 1024, 2048], P(None, 'freq', 'rows')
All inputs are finite; a program needn't handle non-finite values.
Results may differ from a plain program's by a relative error of at most 0.023.
Values may be sent and summed in bfloat16 or wider, within the bound.
No kernel may reach another device: no remote copies, remote signals or barrier semaphores. Data moves between devices by JAX's collectives and lax.ppermute only.
A program may use at most 64 MiB of HBM per device.

v0:
```python
import math

import jax
import jax.numpy as jnp
from jax import lax
from jax.sharding import PartitionSpec as P

DEPTHS = 2


epsilon = 1e-06


def with_halo(cells, sides, width):
    for axis, dim in sides:
        count = lax.axis_size(axis)
        ends = count - 1
        head = lax.slice_in_dim(cells, 0, width, axis=dim)
        tail = lax.slice_in_dim(cells, cells.shape[dim] - width, cells.shape[dim], axis=dim)
        cells = jnp.concatenate(
            [
                lax.ppermute(tail, axis, [(i, (i + 1) % count) for i in range(ends)]),
                cells,
                lax.ppermute(head, axis, [((i + 1) % count, i) for i in range(ends)]),
            ],
            axis=dim,
        )
    return cells


def wavenumbers(length, offset, count):
    indices = offset + jnp.arange(count, dtype=jnp.int32)
    signed = jnp.where(2 * indices < length, indices, indices - length)
    return signed.astype(jnp.float32) * (2.0 * jnp.pi / length)


def split_factor(length):
    factor_small = 1
    while (
        factor_small * 2 <= 128 and factor_small * 2 < length and (length % (factor_small * 2) == 0)
    ):
        factor_small = factor_small * 2
    return factor_small


def rotation_table(count_rows, count_cols, stride, length, sign_value, scaling):
    row_index = jnp.arange(count_rows, dtype=jnp.int32)[:, None]
    col_index = jnp.arange(count_cols, dtype=jnp.int32)[None, :]
    residue = row_index * col_index * stride % length
    angle = residue.astype(jnp.float32) * (sign_value * 2.0 * math.pi / length)
    cosine = jnp.cos(angle) * scaling
    sine = jnp.sin(angle) * scaling
    return jnp.stack([jnp.stack([cosine, -sine]), jnp.stack([sine, cosine])])


def transform(pair, along_axis, inverse, accuracy):
    length = pair.shape[along_axis]
    factor_small = split_factor(length)
    factor_large = length // factor_small
    sign_value = 1.0 if inverse else -1.0
    initial_shape = pair.shape
    split_shape = (
        initial_shape[:along_axis] + (factor_large, factor_small) + initial_shape[along_axis + 1 :]
    )
    pair = pair.reshape(split_shape)
    lead_axes = "cdeg"[: along_axis - 1]
    tail_axes = "pqr"[: len(split_shape) - along_axis - 2]
    first_form = "s" + lead_axes + "ba" + tail_axes + ",zsbk->z" + lead_axes + "ka" + tail_axes
    second_form = "s" + lead_axes + "ka" + tail_axes + ",zsaj->z" + lead_axes + "jk" + tail_axes
    outer_table = rotation_table(factor_large, factor_large, factor_small, length, sign_value, 1.0)
    mixed = jnp.einsum(first_form, pair, outer_table, precision=accuracy)
    twist_angle = (
        jnp.arange(factor_large, dtype=jnp.int32)[:, None]
        * jnp.arange(factor_small, dtype=jnp.int32)[None, :]
        % length
    )
    twist_angle = twist_angle.astype(jnp.float32) * (sign_value * 2.0 * math.pi / length)
    twist_shape = (factor_large, factor_small) + (1,) * len(tail_axes)
    twist_real = jnp.cos(twist_angle).reshape(twist_shape)
    twist_imag = jnp.sin(twist_angle).reshape(twist_shape)
    turned = jnp.stack(
        [
            mixed[0] * twist_real - mixed[1] * twist_imag,
            mixed[0] * twist_imag + mixed[1] * twist_real,
        ]
    )
    scaling = 1.0 / length if inverse else 1.0
    inner_table = rotation_table(
        factor_small, factor_small, factor_large, length, sign_value, scaling
    )
    result = jnp.einsum(second_form, turned, inner_table, precision=accuracy)
    return result.reshape(initial_shape)


def blockwise(left_rows, right_blocks):
    return jnp.einsum(
        "fybi,fbij->fybj", left_rows, right_blocks, preferred_element_type=jnp.float32
    )


def shards(wavefield, block_inverse, coefficient, correction_factor, frequencies, slowness):
    freq_local = wavefield.shape[1]
    rows_local = wavefield.shape[2]
    width_x = wavefield.shape[3]
    row_devices = lax.axis_size("rows")
    height_y = rows_local * row_devices
    cols_local = width_x // row_devices
    block_size = block_inverse.shape[-1]
    block_count = width_x // block_size
    kappa_y = wavenumbers(height_y, 0, height_y)
    kappa_x = wavenumbers(width_x, lax.axis_index("rows") * cols_local, cols_local)
    coef_full = coefficient.astype(jnp.float32)
    factor_real = correction_factor[0][:, None, None]
    factor_imag = correction_factor[1][:, None, None]
    highest = lax.Precision.HIGHEST
    higher = lax.Precision.HIGH
    field = wavefield
    partials = []
    for depth_step in range(DEPTHS):
        spectra = transform(field, 3, False, highest)
        spectra = lax.all_to_all(
            spectra.astype(jnp.bfloat16), "rows", split_axis=3, concat_axis=2, tiled=True
        )
        spectra = transform(spectra.astype(jnp.float32), 2, False, higher)
        vertical = (
            (frequencies * slowness[depth_step])[:, None, None] ** 2
            - kappa_y[None, :, None] ** 2
            - kappa_x[None, None, :] ** 2
        )
        root_value = jnp.sqrt(jnp.abs(vertical))
        upward = vertical >= 0.0
        prop_real = jnp.where(upward, jnp.cos(root_value), jnp.exp(-root_value))
        prop_imag = jnp.where(upward, jnp.sin(root_value), 0.0)
        turned = jnp.stack(
            [
                spectra[0] * prop_real - spectra[1] * prop_imag,
                spectra[0] * prop_imag + spectra[1] * prop_real,
            ]
        )
        turned = transform(turned, 2, True, higher)
        turned = lax.all_to_all(
            turned.astype(jnp.bfloat16), "rows", split_axis=2, concat_axis=3, tiled=True
        )
        stacked_field = transform(turned.astype(jnp.float32), 3, True, higher)
        padded = with_halo(stacked_field.astype(jnp.bfloat16), (("rows", 2),), 1).astype(
            stacked_field.dtype
        )
        curvature = padded[:, :, 2:] - 2.0 * stacked_field + padded[:, :, :-2]
        corrected_real = stacked_field[0] + coef_full * (
            factor_real * curvature[0] - factor_imag * curvature[1]
        )
        corrected_imag = stacked_field[1] + coef_full * (
            factor_real * curvature[1] + factor_imag * curvature[0]
        )
        rounded_real = corrected_real.astype(jnp.bfloat16).reshape(
            freq_local, rows_local, block_count, block_size
        )
        rounded_imag = corrected_imag.astype(jnp.bfloat16).reshape(
            freq_local, rows_local, block_count, block_size
        )
        new_real = corrected_real + (
            blockwise(rounded_real, block_inverse[0]) - blockwise(rounded_imag, block_inverse[1])
        ).reshape(freq_local, rows_local, width_x)
        new_imag = corrected_imag + (
            blockwise(rounded_real, block_inverse[1]) + blockwise(rounded_imag, block_inverse[0])
        ).reshape(freq_local, rows_local, width_x)
        partials.append(jnp.sum(new_real, axis=0))
        field = jnp.stack([new_real, new_imag])
    total_pixels = height_y * width_x
    shares = lax.psum_scatter(
        jnp.stack(partials).astype(jnp.bfloat16), "freq", scatter_dimension=2, tiled=True
    ).astype(jnp.float32)
    energy = lax.psum(jnp.sum(shares * shares, axis=(1, 2)), ("freq", "rows"))
    depth_image = shares / jnp.sqrt(energy / total_pixels + epsilon)[:, None, None]
    return (depth_image, field)


def solution(mesh):
    placed = (
        P(None, "freq", "rows", None),
        P(None, "freq", None, None, None),
        P("rows", None),
        P(None, "freq"),
        P("freq"),
        P(),
    )
    return jax.shard_map(
        shards,
        mesh=mesh,
        in_specs=placed,
        out_specs=(P(None, "rows", "freq"), P(None, "freq", "rows", None)),
        check_vma=False,
    )
```

profile of v0, /device:TPU:10, one launch (start us, length us, event | category | flops | bytes accessed | tf_op | source)
XLA Modules:
  0.0 465.1 jit_solution(8962835039749148515)
XLA Ops:
  7.9 3.1 copy.373
  11.1 3.7 fusion.36
  15.6 6.0 %fusion.80 = bf16[2,1,256,128,16]{2,3,4,0,1:T(8,128)(2,1)S(1)} fusion(f32[2,256,16,128]{3,2,1,0:T(8,128)S(1)} %maximum_bitcast_fusion, f32[1,2,128,128]{2,3,1,0:T(8,128)S(1)} %get-tuple-element.69, f32[1,2,128,128]{2,3,1,0:T(8,128)S(1)} %get-tuple-element.68), kind=kOutput, calls=%fused_computation.104 | convolution fusion | flops 3222339584 | bytes 6553600 | tf_op jit(solution)/shard_map/scdka,zsaj->zcdjk/dot_general | solution.py:91
  22.7 14.0 %copy.260 = bf16[2,1,256,2048]{2,0,1,3:T(2,128)(2,1)} copy(bf16[2,1,256,2048]{2,3,0,1:T(8,128)(2,1)S(1)} %bitcast.453) | data formatting | bytes 4194304 | tf_op jit(solution)/shard_map/convert_element_type | solution.py:122
  36.7 4.4 all-to-all-start
  45.6 19.9 %all-to-all-done = bf16[2,1,256,2048]{2,0,1,3:T(2,128)(2,1)S(1)} async-done(((bf16[2,1,256,2048]{2,0,1,3:T(2,128)(2,1)}), bf16[2,1,256,2048]{2,0,1,3:T(2,128)(2,1)S(1)}, u32[]{:S(2)}, u32[]{:S(2)}) %all-to-all-start) | async-done | bytes 2097184 | tf_op jit(solution)/shard_map/all_to_all | solution.py:121
  67.1 3.0 copy.262
  73.2 4.1 fusion.39
  80.4 10.0 %fusion.65 = (f32[1,8,128,512]{3,1,0,2:T(8,128)S(1)}, f32[1,8,128,512]{3,1,0,2:T(8,128)S(1)}) fusion(f32[1,8,128,512]{3,2,1,0:T(8,128)S(1)} %bitcast.446, f32[1,8,128,512]{3,2,1,0:T(8,128)S(1)} %bitcast.444, f32[512]{0:T(512)S(1)} %fusion.146, f32[8,128]{0,1:T(8,128)S(1)} %copy.268), kind=kLoop, calls=%fused_computation.89 | loop fusion | flops 6291456 | bytes 8394752 | tf_op jit(solution)/shard_map/sub | solution.py:136
  93.5 4.1 bitcast_convert_fusion.2
  98.9 3.5 copy.278
  102.3 4.3 all-to-all-start.1
  109.5 20.9 %all-to-all-done.1 = bf16[2,1,1024,512]{3,0,1,2:T(2,128)(2,1)S(1)} async-done(((bf16[2,1,1024,512]{3,0,1,2:T(2,128)(2,1)}), bf16[2,1,1024,512]{3,0,1,2:T(2,128)(2,1)S(1)}, u32[]{:S(2)}, u32[]{:S(2)}) %all-to-all-start.1) | async-done | bytes 2097184 | tf_op jit(solution)/shard_map/all_to_all | solution.py:141
  130.8 2.9 copy.280
  133.7 2.7 reshape.1521
  138.5 6.8 %broadcast_multiply_fusion.1 = (f32[2,1,256,128,16]{2,3,4,0,1:T(8,128)}, bf16[2,1,256,128,16]{2,3,4,0,1:T(8,128)(2,1)S(1)}, f32[2,1,256,128,16]{2,3,4,0,1:T(8,128)}) fusion(f32[2,256,16,128]{3,2,1,0:T(8,128)S(1)} %maximum_bitcast_fusion.5, f32[1,2,128,128]{2,3,1,0:T(8,128)S(1)} %get-tuple-element.63, f32[1,2,128,128]{2,3,1,0:T(8,128)S(1)} %get-tuple-element.62), kind=kOutput, calls=%fused_computation.126 | convolution fusion | flops 1612775424 | bytes 14942208 | tf_op jit(solution)/shard_map/scdka,zsaj->zcdjk/dot_general | solution.py:91
  150.2 3.4 collective-permute-start
  154.6 3.4 collective-permute-start.1
  158.0 2.7 fusion.175
  161.5 4.4 copy.290
  165.9 2.5 copy.282
  168.4 2.6 copy.294
  174.3 3.0 maximum_convert_fusion
  178.6 5.9 %fusion.171 = (bf16[256,2048]{0,1:T(8,128)(2,1)S(1)}, f32[256,2048]{0,1:T(8,128)S(1)}, bf16[256,2048]{0,1:T(8,128)(2,1)S(1)}, f32[256,2048]{0,1:T(8,128)}) fusion(f32[2,1,256,2048]{2,3,1,0:T(8,128)S(1)} %slice_add_fusion.1, f32[]{:T(128)} %bitcast.90, f32[]{:T(128)} %bitcast.84, bf16[256,2048]{0,1:T(8,128)(2,1)S(1)} %copy-done.5, ...), kind=kLoop, calls=%fused_computation.289 | loop fusion | flops 6815744 | bytes 15728648 | tf_op jit(solution)/shard_map/convert_element_type | solution.py:155
  189.2 3.2 copy.369
  197.0 5.4 %fusion.52 = f32[2,1,256,16,128]{4,3,2,0,1:T(8,128)S(1)} fusion(f32[1,1,256,16,128]{4,3,0,2,1:T(8,128)} %copy.370, f32[1,1,256,16,128]{4,3,0,2,1:T(8,128)} %copy.369, f32[1,2,16,16]{2,3,1,0:T(8,128)} %copy-done.34, f32[1,2,16,16]{2,3,1,0:T(8,128)S(1)} %get-tuple-element.72), kind=kOutput, calls=%fused_computation.72 | convolution fusion | flops 403702784 | bytes 8392704 | tf_op jit(solution)/shard_map/scdba,zsbk->zcdka/dot_general | solution.py:71
  203.8 5.5 %fusion.81 = bf16[2,1,256,128,16]{2,3,4,0,1:T(8,128)(2,1)S(1)} fusion(f32[2,256,16,128]{3,2,1,0:T(8,128)S(1)} %maximum_bitcast_fusion.8, f32[1,2,128,128]{2,3,1,0:T(8,128)S(1)} %copy-done.18, f32[1,2,128,128]{2,3,1,0:T(8,128)S(1)} %copy-done.16), kind=kOutput, calls=%fused_computation.105 | convolution fusion | flops 3222339584 | bytes 6553600 | tf_op jit(solution)/shard_map/scdka,zsaj->zcdjk/dot_general | solution.py:91
  210.5 14.0 %copy.303 = bf16[2,1,256,2048]{2,0,1,3:T(2,128)(2,1)} copy(bf16[2,1,256,2048]{2,3,0,1:T(8,128)(2,1)S(1)} %bitcast.457) | data formatting | bytes 4194304 | tf_op jit(solution)/shard_map/convert_element_type | solution.py:122
  224.5 3.7 all-to-all-start.2
  229.5 21.6 %all-to-all-done.2 = bf16[2,1,256,2048]{2,0,1,3:T(2,128)(2,1)S(1)} async-done(((bf16[2,1,256,2048]{2,0,1,3:T(2,128)(2,1)}), bf16[2,1,256,2048]{2,0,1,3:T(2,128)(2,1)S(1)}, u32[]{:S(2)}, u32[]{:S(2)}) %all-to-all-start.2) | async-done | bytes 2097184 | tf_op jit(solution)/shard_map/all_to_all | solution.py:121
  252.7 3.0 copy.305
  258.8 4.1 fusion.45
  266.0 10.1 %fusion.74 = (f32[1,8,128,512]{3,1,0,2:T(8,128)S(1)}, f32[1,8,128,512]{3,1,0,2:T(8,128)S(1)}) fusion(f32[1,8,128,512]{3,2,1,0:T(8,128)S(1)} %bitcast.445, f32[1,8,128,512]{3,2,1,0:T(8,128)S(1)} %bitcast.443, f32[8,128]{0,1:T(8,128)S(1)} %copy-done.33, f32[512]{0:T(512)S(1)} %copy-done.56), kind=kLoop, calls=%fused_computation.98 | loop fusion | flops 6291456 | bytes 8394752 | tf_op jit(solution)/shard_map/sub | solution.py:136
  279.8 4.0 bitcast_convert_fusion
  287.1 27.7 %all_to_all.60 = bf16[2,1,1024,512]{3,0,1,2:T(2,128)(2,1)S(1)} all-to-all(bf16[2,1,1024,512]{3,0,1,2:T(2,128)(2,1)S(1)} %copy.317), channel_id=1, replica_groups=mesh['freq'=8,'rows'=4] {'rows'}, dimensions={2} | all-to-all | bytes 4194304 | tf_op jit(solution)/shard_map/all_to_all | solution.py:141
  315.2 2.9 copy.319
  318.1 2.8 reshape.1538
  323.6 6.8 %broadcast_multiply_fusion = (f32[2,1,256,128,16]{2,3,4,0,1:T(8,128)}, bf16[2,1,256,128,16]{2,3,4,0,1:T(8,128)(2,1)S(1)}, f32[2,1,256,128,16]{2,3,4,0,1:T(8,128)}) fusion(f32[2,256,16,128]{3,2,1,0:T(8,128)S(1)} %maximum_bitcast_fusion.13, f32[1,2,128,128]{2,3,1,0:T(8,128)S(1)} %copy-done.14, f32[1,2,128,128]{2,3,1,0:T(8,128)S(1)} %get-tuple-element.62), kind=kOutput, calls=%fused_computation.125 | convolution fusion | flops 1612775424 | bytes 14942208 | tf_op jit(solution)/shard_map/scdka,zsaj->zcdjk/dot_general | solution.py:91
  335.0 3.4 collective-permute-start.2
  339.9 2.7 collective-permute-start.3
  342.6 2.7 fusion.173
  346.1 4.4 copy.328
  350.5 2.6 copy.321
  358.4 3.4 maximum_convert_fusion.1
  363.0 5.8 %fusion.165 = (bf16[256,2048]{0,1:T(8,128)(2,1)S(1)}, f32[256,2048]{0,1:T(8,128)}, bf16[256,2048]{0,1:T(8,128)(2,1)S(1)}, f32[256,2048]{0,1:T(8,128)S(1)}) fusion(f32[2,1,256,2048]{2,3,1,0:T(8,128)S(1)} %slice_add_fusion, f32[]{:T(128)} %bitcast.90, f32[]{:T(128)} %bitcast.84, bf16[256,2048]{0,1:T(8,128)(2,1)S(1)} %copy-done.6, ...), kind=kLoop, calls=%fused_computation.286 | loop fusion | flops 6815744 | bytes 15728648 | tf_op jit(solution)/shard_map/convert_element_type | solution.py:158
  379.7 26.6 %reduce-scatter.2.cloned.1.call-done = bf16[2,256,256]{1,2,0:T(8,128)(2,1)} async-done(((bf16[2,256,2048]{1,2,0:T(8,128)(2,1)}), bf16[2,256,256]{1,2,0:T(8,128)(2,1)}) %reduce-scatter.2.cloned.1.call-update) | async-done | bytes 262160 | tf_op jit(solution)/shard_map/reduce_scatter | solution.py:170
  407.4 5.4 %copy.336 = f32[2,1,256,2048]{3,2,1,0:T(8,128)} copy(f32[2,1,256,2048]{2,3,1,0:T(8,128)} %pad_maximum_fusion) | data formatting | bytes 8388608
  412.8 44.0 %psum.7 = f32[2]{0:T(128)S(1)} all-reduce(f32[2]{0:T(128)S(1)} %fusion.94), channel_id=1, replica_groups=mesh['freq'=8,'rows'=4] {'freq','rows'}, use_global_device_ids=true, to_apply=%region_2.3 | all-reduce | flops 2 | bytes 16 | tf_op jit(solution)/shard_map/psum | solution.py:173
  (241 shorter events, 90.4 us)
Async XLA Ops:
  7.4 7.4 %copy-start.43 = (f32[16,128]{1,0:T(8,128)}, f32[16,128]{1,0:T(8,128)S(1)}, u32[]{:S(2)}) copy-start(f32[16,128]{1,0:T(8,128)S(1)} %get-tuple-element.86) | copy-start | bytes 24580
  7.4 7.4 %copy-start.45 = (f32[16,128]{1,0:T(8,128)}, f32[16,128]{1,0:T(8,128)S(1)}, u32[]{:S(2)}) copy-start(f32[16,128]{1,0:T(8,128)S(1)} %get-tuple-element.87) | copy-start | bytes 24580
  11.1 3.7 copy-start.34
  15.6 6.0 %copy-start.15 = (f32[1,2,128,128]{2,3,1,0:T(8,128)}, f32[1,2,128,128]{2,3,1,0:T(8,128)S(1)}, u32[]{:S(2)}) copy-start(f32[1,2,128,128]{2,3,1,0:T(8,128)S(1)} %get-tuple-element.68) | copy-start | bytes 393220
  15.6 6.0 %copy-start.17 = (f32[1,2,128,128]{2,3,1,0:T(8,128)}, f32[1,2,128,128]{2,3,1,0:T(8,128)S(1)}, u32[]{:S(2)}) copy-start(f32[1,2,128,128]{2,3,1,0:T(8,128)S(1)} %get-tuple-element.69) | copy-start | bytes 393220
  36.7 5.6 %copy-start.57 = (f32[2]{0:T(128)S(1)}, f32[2]{0:T(128)}, u32[]{:S(2)}) copy-start(f32[2]{0:T(128)} %param.11) | copy-start | bytes 28
  36.7 28.8 %all-to-all-start = ((bf16[2,1,256,2048]{2,0,1,3:T(2,128)(2,1)}), bf16[2,1,256,2048]{2,0,1,3:T(2,128)(2,1)S(1)}, u32[]{:S(2)}, u32[]{:S(2)}) async-start(bf16[2,1,256,2048]{2,0,1,3:T(2,128)(2,1)} %copy.260), calls=%async_computation | async-start | bytes 4194304 | tf_op jit(solution)/shard_map/all_to_all | solution.py:121
  41.4 28.7 %copy-start.39 = (f32[1,2,8,8]{2,3,1,0:T(8,128)}, f32[1,2,8,8]{2,3,1,0:T(8,128)S(1)}, u32[]{:S(2)}) copy-start(f32[1,2,8,8]{2,3,1,0:T(8,128)S(1)} %copy.255) | copy-start | bytes 1540
  41.5 28.6 %copy-start.41 = (f32[1,2,8,8]{2,3,1,0:T(8,128)}, f32[1,2,8,8]{2,3,1,0:T(8,128)S(1)}, u32[]{:S(2)}) copy-start(f32[1,2,8,8]{2,3,1,0:T(8,128)S(1)} %copy.256) | copy-start | bytes 1540
  41.6 30.5 %copy-start.25 = (f32[8,128]{0,1:T(8,128)}, f32[8,128]{0,1:T(8,128)S(1)}, u32[]{:S(2)}) copy-start(f32[8,128]{0,1:T(8,128)S(1)} %copy.264) | copy-start | bytes 12292
  41.7 30.4 %copy-start.27 = (f32[8,128]{0,1:T(8,128)}, f32[8,128]{0,1:T(8,128)S(1)}, u32[]{:S(2)}) copy-start(f32[8,128]{0,1:T(8,128)S(1)} %copy.265) | copy-start | bytes 12292
  44.0 46.4 %copy-start.47 = (f32[1,2,8,8]{2,3,1,0:T(8,128)}, f32[1,2,8,8]{2,3,1,0:T(8,128)S(1)}, u32[]{:S(2)}) copy-start(f32[1,2,8,8]{2,3,1,0:T(8,128)S(1)} %copy.253) | copy-start | bytes 1540
  44.1 46.4 %copy-start.49 = (f32[1,2,8,8]{2,3,1,0:T(8,128)}, f32[1,2,8,8]{2,3,1,0:T(8,128)S(1)}, u32[]{:S(2)}) copy-start(f32[1,2,8,8]{2,3,1,0:T(8,128)S(1)} %copy.254) | copy-start | bytes 1540
  44.2 48.3 %copy-start.29 = (f32[8,128]{0,1:T(8,128)}, f32[8,128]{0,1:T(8,128)S(1)}, u32[]{:S(2)}) copy-start(f32[8,128]{0,1:T(8,128)S(1)} %copy.274) | copy-start | bytes 12292
  44.4 48.1 %copy-start.31 = (f32[8,128]{0,1:T(8,128)}, f32[8,128]{0,1:T(8,128)S(1)}, u32[]{:S(2)}) copy-start(f32[8,128]{0,1:T(8,128)S(1)} %copy.275) | copy-start | bytes 12292
  44.4 36.0 %copy-start.55 = (f32[512]{0:T(512)}, f32[512]{0:T(512)S(1)}, u32[]{:S(2)}) copy-start(f32[512]{0:T(512)S(1)} %fusion.146) | copy-start | bytes 6148
  45.6 47.9 %copy-start.19 = (f32[1,2,128,128]{2,3,1,0:T(8,128)}, f32[1,2,128,128]{2,3,1,0:T(8,128)S(1)}, u32[]{:S(2)}) copy-start(f32[1,2,128,128]{2,3,1,0:T(8,128)S(1)} %get-tuple-element.64) | copy-start | bytes 393220
  45.6 47.9 %copy-start.21 = (f32[1,2,128,128]{2,3,1,0:T(8,128)}, f32[1,2,128,128]{2,3,1,0:T(8,128)S(1)}, u32[]{:S(2)}) copy-start(f32[1,2,128,128]{2,3,1,0:T(8,128)S(1)} %get-tuple-element.65) | copy-start | bytes 393220
  102.3 4.3 copy-start.23
  102.3 28.1 %all-to-all-start.1 = ((bf16[2,1,1024,512]{3,0,1,2:T(2,128)(2,1)}), bf16[2,1,1024,512]{3,0,1,2:T(2,128)(2,1)S(1)}, u32[]{:S(2)}, u32[]{:S(2)}) async-start(bf16[2,1,1024,512]{3,0,1,2:T(2,128)(2,1)} %copy.278), calls=%async_computation.1 | async-start | bytes 4194304 | tf_op jit(solution)/shard_map/all_to_all | solution.py:141
  108.8 29.0 %copy-start.51 = (f32[16,128]{1,0:T(8,128)}, f32[16,128]{1,0:T(8,128)S(1)}, u32[]{:S(2)}) copy-start(f32[16,128]{1,0:T(8,128)S(1)} %get-tuple-element.100) | copy-start | bytes 24580
  108.8 29.0 %copy-start.53 = (f32[16,128]{1,0:T(8,128)}, f32[16,128]{1,0:T(8,128)S(1)}, u32[]{:S(2)}) copy-start(f32[16,128]{1,0:T(8,128)S(1)} %get-tuple-element.101) | copy-start | bytes 24580
  108.9 27.6 %copy-start.35 = (f32[1,2,16,16]{2,3,1,0:T(8,128)}, f32[1,2,16,16]{2,3,1,0:T(8,128)S(1)}, u32[]{:S(2)}) copy-start(f32[1,2,16,16]{2,3,1,0:T(8,128)S(1)} %get-tuple-element.70) | copy-start | bytes 6148
  108.9 27.6 %copy-start.37 = (f32[1,2,16,16]{2,3,1,0:T(8,128)}, f32[1,2,16,16]{2,3,1,0:T(8,128)S(1)}, u32[]{:S(2)}) copy-start(f32[1,2,16,16]{2,3,1,0:T(8,128)S(1)} %get-tuple-element.71) | copy-start | bytes 6148
  109.5 29.1 %copy-start.13 = (f32[1,2,128,128]{2,3,1,0:T(8,128)}, f32[1,2,128,128]{2,3,1,0:T(8,128)S(1)}, u32[]{:S(2)}) copy-start(f32[1,2,128,128]{2,3,1,0:T(8,128)S(1)} %get-tuple-element.63) | copy-start | bytes 393220
  150.2 20.8 %collective-permute-start = (bf16[2,1,1,2048]{3,0,2,1:T(2,128)(2,1)}, bf16[2,1,1,2048]{3,0,2,1:T(2,128)(2,1)}, u32[]{:S(2)}, u32[]{:S(2)}) collective-permute-start(bf16[2,1,1,2048]{3,0,2,1:T(2,128)(2,1)} %copy.285), channel_id=1, source_target_pairs={{0,1},{1,2},{2,3},{4,5},{5,6},{6,7},{8,9},{9,10},{10,11},{12,13},{... | collective-permute-start | bytes 24584 | tf_op jit(solution)/shard_map/ppermute | solution.py:22
  154.6 17.6 %collective-permute-start.1 = (bf16[2,1,1,2048]{3,0,2,1:T(2,128)(2,1)}, bf16[2,1,1,2048]{3,0,2,1:T(2,128)(2,1)}, u32[]{:S(2)}, u32[]{:S(2)}) collective-permute-start(bf16[2,1,1,2048]{3,0,2,1:T(2,128)(2,1)} %copy.286), channel_id=1, source_target_pairs={{1,0},{2,1},{3,2},{5,4},{6,5},{7,6},{9,8},{10,9},{11,10},{13,12},{... | collective-permute-start | bytes 24584 | tf_op jit(solution)/shard_map/ppermute | solution.py:24
  158.0 3.5 copy-start.1
  174.3 3.0 copy-start.2
  178.6 5.9 %copy-start.4 = (bf16[2,1,16,128,128]{4,3,2,1,0:T(8,128)(2,1)S(1)}, bf16[2,1,16,128,128]{4,3,2,1,0:T(8,128)(2,1)}, u32[]{:S(2)}) copy-start(bf16[2,1,16,128,128]{4,3,2,1,0:T(8,128)(2,1)} %param.7) | copy-start | bytes 3145732
  192.5 2.2 copy-start.10
  197.0 5.4 %copy-start.44 = (f32[16,128]{1,0:T(8,128)S(1)}, f32[16,128]{1,0:T(8,128)}, u32[]{:S(2)}) copy-start(f32[16,128]{1,0:T(8,128)} %copy-done.43) | copy-start | bytes 24580
  197.0 5.4 %copy-start.46 = (f32[16,128]{1,0:T(8,128)S(1)}, f32[16,128]{1,0:T(8,128)}, u32[]{:S(2)}) copy-start(f32[16,128]{1,0:T(8,128)} %copy-done.45) | copy-start | bytes 24580
  224.5 26.6 %all-to-all-start.2 = ((bf16[2,1,256,2048]{2,0,1,3:T(2,128)(2,1)}), bf16[2,1,256,2048]{2,0,1,3:T(2,128)(2,1)S(1)}, u32[]{:S(2)}, u32[]{:S(2)}) async-start(bf16[2,1,256,2048]{2,0,1,3:T(2,128)(2,1)} %copy.303), calls=%async_computation.2 | async-start | bytes 4194304 | tf_op jit(solution)/shard_map/all_to_all | solution.py:121
  228.1 178.2 %reduce-scatter.2.cloned.1.call-start = ((), (), s32[]{:S(2)}) async-start(), calls=%async_computation.5 | async-start | bytes 2359296 | tf_op jit(solution)/shard_map/reduce_scatter | solution.py:170
  252.7 3.0 copy-start.40
  252.7 3.1 copy-start.42
  266.0 10.1 %copy-start.48 = (f32[1,2,8,8]{2,3,1,0:T(8,128)S(1)}, f32[1,2,8,8]{2,3,1,0:T(8,128)}, u32[]{:S(2)}) copy-start(f32[1,2,8,8]{2,3,1,0:T(8,128)} %copy-done.47) | copy-start | bytes 1540
  266.0 10.1 %copy-start.50 = (f32[1,2,8,8]{2,3,1,0:T(8,128)S(1)}, f32[1,2,8,8]{2,3,1,0:T(8,128)}, u32[]{:S(2)}) copy-start(f32[1,2,8,8]{2,3,1,0:T(8,128)} %copy-done.49) | copy-start | bytes 1540
  276.2 2.1 copy-start.30
  276.2 2.1 copy-start.32
  318.1 2.8 copy-start.36
  318.1 2.8 copy-start.38
  335.0 20.6 %collective-permute-start.2 = (bf16[2,1,1,2048]{3,0,2,1:T(2,128)(2,1)S(1)}, bf16[2,1,1,2048]{3,0,2,1:T(2,128)(2,1)S(1)}, u32[]{:S(2)}, u32[]{:S(2)}) collective-permute-start(bf16[2,1,1,2048]{3,0,2,1:T(2,128)(2,1)S(1)} %copy.323), channel_id=1, source_target_pairs={{0,1},{1,2},{2,3},{4,5},{5,6},{6,7},{8,9},{9,10},{10,11},{12,13},{... | collective-permute-start | bytes 24584 | tf_op jit(solution)/shard_map/ppermute | solution.py:22
  339.9 17.0 %collective-permute-start.3 = (bf16[2,1,1,2048]{3,0,2,1:T(2,128)(2,1)S(1)}, bf16[2,1,1,2048]{3,0,2,1:T(2,128)(2,1)S(1)}, u32[]{:S(2)}, u32[]{:S(2)}) collective-permute-start(bf16[2,1,1,2048]{3,0,2,1:T(2,128)(2,1)S(1)} %copy.324), channel_id=1, source_target_pairs={{1,0},{2,1},{3,2},{5,4},{6,5},{7,6},{9,8},{10,9},{11,10},{13,12},{... | collective-permute-start | bytes 24584 | tf_op jit(solution)/shard_map/ppermute | solution.py:24
  342.6 3.5 copy-start
  358.4 3.4 copy-start.3
  407.4 49.4 %copy-start.24 = (bf16[2,256,256]{1,2,0:T(8,128)(2,1)S(1)}, bf16[2,256,256]{1,2,0:T(8,128)(2,1)}, u32[]{:S(2)}) copy-start(bf16[2,256,256]{1,2,0:T(8,128)(2,1)} %reduce-scatter.2.cloned.1.call-done) | copy-start | bytes 786436
  (19 other events, 24.9 us)
Sparse Core Ops, SparseCore 0:
  373.2 33.0 reduce-scatter.1
where the time goes:
time: 471 us; the launch traced here: 465 us
  local copies, waits for them, and re-layouts  134 us (28%)
  waiting for transfers between devices  89 us (19%)
  blocking collectives  71.7 us (15%)
  matrix products  68.2 us (14%)
  other arithmetic  59.5 us (13%)
  starting transfers between devices  25.2 us (5%)
  between operations  17.6 us (4%)
    psum x1, blocking collectives, shards(): energy = lax.psum(jnp.sum(shares * shares, axis=(1, 2)), ('freq', 'rows'))  44 us
    all_to_all x2, waiting for transfers between devices, shards(): lax.all_to_all(spectra.astype(jnp.bfloat16), 'rows', split_axis=3, concat...  41.5 us
    dot_general x8, matrix products, transform(): result = jnp.einsum(second_form, turned, inner_table, precision=accuracy)  41.4 us
    convert_element_type x4, local copies, waits for them, and re-layouts, shards(): spectra.astype(jnp.bfloat16)  30.4 us
    all_to_all x1, blocking collectives, shards(): lax.all_to_all(turned.astype(jnp.bfloat16), 'rows', split_axis=2, concat_...  27.7 us
    reduce_scatter x1, waiting for transfers between devices, shards(): lax.psum_scatter(jnp.stack(partials).astype(jnp.bfloat16), 'freq', scatte...  26.6 us
    all_to_all x1, waiting for transfers between devices, shards(): lax.all_to_all(turned.astype(jnp.bfloat16), 'rows', split_axis=2, concat_...  20.9 us
    sub x2, other arithmetic, shards(): spectra[0] * prop_real - spectra[1] * prop_imag  20.1 us
  transfers between devices with their start and end apart: 8, of which 4 were waited for; matrix products, arithmetic and copies ran while one was open for 9% of the time, Pallas kernels for 0%

commit v1 on v0

v1 whole, which is shorter than its diff:
```python
import functools
import math

import jax
import jax.numpy as jnp
import numpy as np
from jax import lax
from jax.experimental import pallas as pl
from jax.experimental.pallas import tpu as pltpu
from jax.sharding import PartitionSpec as P

DEPTHS = 2
epsilon = 1e-06
F32 = jnp.float32
BF16 = jnp.bfloat16
VMEM_LIMIT = 36 * 1024 * 1024
EXTRA = 16


def small_dft(real, imag, sign):
    count = len(real)
    if count == 1:
        return list(real), list(imag)
    even_r, even_i = small_dft(real[0::2], imag[0::2], sign)
    odd_r, odd_i = small_dft(real[1::2], imag[1::2], sign)
    half = count // 2
    out_r, out_i = [None] * count, [None] * count
    for k in range(half):
        br, bi = odd_r[k], odd_i[k]
        if k == 0:
            tr, ti = br, bi
        elif 4 * k == count:
            tr, ti = (-bi, br) if sign > 0 else (bi, -br)
            if sign > 0:
                out_r[k], out_i[k] = even_r[k] - bi, even_i[k] + br
                out_r[k + half], out_i[k + half] = even_r[k] + bi, even_i[k] - br
            else:
                out_r[k], out_i[k] = even_r[k] + bi, even_i[k] - br
                out_r[k + half], out_i[k + half] = even_r[k] - bi, even_i[k] + br
            continue
        else:
            angle = sign * 2.0 * math.pi * k / count
            c, s = math.cos(angle), math.sin(angle)
            if abs(abs(c) - abs(s)) < 1e-12:
                h = abs(c)
                cs, ss = math.copysign(1.0, c), math.copysign(1.0, s)
                re = (br if cs > 0 else -br) + (-bi if ss > 0 else bi)
                im = (bi if cs > 0 else -bi) + (br if ss > 0 else -br)
                tr, ti = re * h, im * h
            else:
                tr, ti = br * c - bi * s, br * s + bi * c
        out_r[k], out_i[k] = even_r[k] + tr, even_i[k] + ti
        out_r[k + half], out_i[k + half] = even_r[k] - tr, even_i[k] - ti
    return out_r, out_i


def lane_tables(width, lane):
    blocks = width // lane
    a = np.arange(lane)
    forward = np.exp(-2j * np.pi * np.outer(a, a) / lane)
    inverse = np.exp(2j * np.pi * np.outer(a, a) / lane) / width

    def embed(m):
        return np.block([[m.real, m.imag], [-m.imag, m.real]])

    twist = np.exp(-2j * np.pi * np.outer(np.arange(blocks), a) / width)
    return (
        jnp.asarray(embed(forward), BF16),
        jnp.asarray(embed(inverse), BF16),
        jnp.asarray(np.stack([twist.real, twist.imag]), F32),
    )


def row_tables(height, lane):
    count = height // lane
    a = np.arange(lane)
    forward, inverse = [], []
    for k in range(count):
        j = a if 2 * k <= count else lane - 1 - a
        ky = count * j + k
        table = np.exp(-2j * np.pi * np.outer(ky, a) / height)
        forward.append(np.block([[table.real, -table.imag], [table.imag, table.real]]))
        back = np.conj(table.T) / height
        inverse.append(np.block([[back.real, -back.imag], [back.imag, back.real]]))
    return jnp.asarray(np.stack(forward), BF16), jnp.asarray(np.stack(inverse), BF16)


def dot(left, right):
    return jnp.dot(left, right, preferred_element_type=F32)

ANY = pl.BlockSpec(memory_space=pltpu.HBM)
SMEM = pl.BlockSpec(memory_space=pltpu.SMEM)
FULL = pl.BlockSpec(memory_space=pltpu.VMEM)


def cost(flops, moved):
    return pl.CostEstimate(flops=flops, bytes_accessed=moved, transcendentals=0)


def params():
    return pltpu.CompilerParams(vmem_limit_bytes=VMEM_LIMIT)


def forward_lanes(load, rows, blocks, lane, twist_ref, left_ref, base=0):
    sub = 16

    def body(i, carry):
        at = pl.ds(pl.multiple_of(i * sub, sub), sub)
        to = pl.ds(pl.multiple_of(i * sub + base, sub), sub)
        real = [load(0, at, b) for b in range(blocks)]
        imag = [load(1, at, b) for b in range(blocks)]
        real, imag = small_dft(real, imag, -1)
        for k in range(blocks):
            if k:
                c, s = twist_ref[0, k : k + 1, :], twist_ref[1, k : k + 1, :]
                re, im = real[k] * c - imag[k] * s, real[k] * s + imag[k] * c
            else:
                re, im = real[k], imag[k]
            left_ref[k, to, 0:lane] = re.astype(BF16)
            left_ref[k, to, lane : 2 * lane] = im.astype(BF16)
        return carry

    lax.fori_loop(0, rows // sub, body, 0)


def slot_products(left_ref, table_ref, me, slot, per_device):
    owner = lax.bitwise_xor(me, slot)
    left = left_ref[pl.ds(owner * per_device, per_device)]
    count, rows, wide = left.shape
    part = dot(left.reshape(count * rows, wide), table_ref[...]).astype(BF16)
    return [part[place * rows : (place + 1) * rows] for place in range(per_device)]


def first_kernel(me_ref, field_hbm, twist_ref, table_ref, *refs, lane, per_device, chunk, parts):
    outs, (field_ref, left_ref, sem) = refs[:-3], refs[-3:]
    rows, width = field_ref.shape[1], field_ref.shape[2]
    tile = rows // parts
    arriving = [
        pltpu.make_async_copy(
            field_hbm.at[:, pl.ds(chunk * rows + t * tile, tile), :],
            field_ref.at[:, pl.ds(t * tile, tile), :],
            sem.at[t],
        )
        for t in range(parts)
    ]
    for copy in arriving:
        copy.start()
    for t in range(parts):
        arriving[t].wait()

        def load(part, at, b, t=t):
            return field_ref[part, pl.ds(at.start + t * tile, at.size), b * lane : (b + 1) * lane]

        forward_lanes(load, tile, width // lane, lane, twist_ref, left_ref, t * tile)
    for slot, out_ref in enumerate(outs):
        made = slot_products(left_ref, table_ref, me_ref[0], slot, per_device)
        for place, part in enumerate(made):
            out_ref[:, place * 2 * lane : (place + 1) * 2 * lane] = part


def forward_x(me, field, tables, lane, devices, chunk, chunks):
    _, rows, width = field.shape
    blocks = width // lane
    per_device = blocks // devices
    rows = rows // chunks
    parts = max(rows // 32, 1)
    wide = per_device * 2 * lane
    return pl.pallas_call(
        functools.partial(
            first_kernel, lane=lane, per_device=per_device, chunk=chunk, parts=parts
        ),
        in_specs=[SMEM, ANY, FULL, FULL],
        out_specs=[FULL] * devices,
        out_shape=[jax.ShapeDtypeStruct((rows, wide), BF16)] * devices,
        scratch_shapes=[
            pltpu.VMEM((2, rows, width), F32),
            pltpu.VMEM((blocks, rows, 2 * lane), BF16),
            pltpu.SemaphoreType.DMA((parts,)),
        ],
        compiler_params=params(),
        cost_estimate=cost(rows * width * 4000, rows * width * 12),
        name="forward_x",
    )(me, field, tables[2], tables[0])


def poly(coefficients, t):
    acc = jnp.full_like(t, coefficients[-1])
    for c in coefficients[-2::-1]:
        acc = acc * t + c
    return acc


@functools.lru_cache(maxsize=None)
def wave_series(limit):
    from numpy.polynomial import chebyshev

    nodes = np.cos(np.pi * (np.arange(64) + 0.5) / 64)
    root = np.sqrt((nodes + 1.0) * 0.5 * limit)
    out = []
    for values in (np.cos(root), np.sinc(root / np.pi)):
        fitted = chebyshev.chebfit(nodes, values, 7)
        out.append(tuple(float(c) for c in chebyshev.cheb2poly(fitted)))
    return tuple(out)


def propagator(q, limit):
    root = jnp.sqrt(jnp.abs(q))
    t = q * (2.0 / limit) - 1.0
    cosine, sinc = wave_series(limit)
    upward = q >= 0.0
    t = jnp.where(upward, t, 0.0)
    real = jnp.where(upward, poly(cosine, t), jnp.exp(-root))
    imag = jnp.where(upward, root * poly(sinc, t), 0.0)
    return real, imag


def wave_kernel(me_ref, squared_ref, after_ref, *u_refs, lane, width, height, columns, limit):
    me = me_ref[0]
    depths = len(u_refs)
    count = height // lane
    blocks = width // lane
    sub = 8
    col = lax.broadcasted_iota(jnp.int32, (sub, lane), 1)
    row_id = lax.broadcasted_iota(jnp.int32, (sub, lane), 0)

    def kappa_squared(index, length):
        signed = jnp.where(2 * index < length, index, index - length)
        kappa = signed.astype(F32) * (2.0 * math.pi / length)
        return kappa * kappa

    def wave_body(i, carry):
        at = pl.multiple_of(i * sub, sub)
        ky2 = [
            kappa_squared(count * (row_id + at) + k, height) for k in range(count // 2 + 1)
        ]
        for c in range(columns):
            kx2 = kappa_squared(blocks * col + me * columns + c, width)
            here = slice(c * lane, (c + 1) * lane)
            for k in range(count // 2 + 1):
                for depth in range(depths):
                    real, imag = propagator((squared_ref[depth] - ky2[k]) - kx2, limit)
                    u_refs[depth][k, pl.ds(at, sub), here] = real
                    u_refs[depth][k, pl.ds(lane + at, sub), here] = imag
        return carry

    lax.fori_loop(0, lane // sub, wave_body, 0)


def waves(me, squared, after, lane, width, height, columns, limit):
    shape = (height // lane // 2 + 1, 2 * lane, columns * lane)
    return pl.pallas_call(
        functools.partial(
            wave_kernel, lane=lane, width=width, height=height, columns=columns, limit=limit
        ),
        in_specs=[SMEM, SMEM, ANY],
        out_specs=[FULL] * squared.shape[0],
        out_shape=[jax.ShapeDtypeStruct(shape, F32)] * squared.shape[0],
        compiler_params=params(),
        cost_estimate=cost(height * columns * lane * 8000, height * columns * lane * 16),
        name="waves",
    )(me, squared, after)


def spectral_kernel(*refs, lane, width, rows, devices, chunks):
    me_ref, u_ref, forward_ref, inverse_ref = refs[:4]
    ins = refs[4 : 4 + chunks * devices]
    outs = refs[4 + chunks * devices : 4 + 2 * chunks * devices]
    (
        in_ref, out_ref, edge_ref, x_ref, z_ref, w_ref, in_sem, out_sem, edge_sem,
    ) = refs[4 + 2 * chunks * devices :]
    me = me_ref[0]
    height = devices * rows
    part_rows = rows // chunks
    count = height // lane
    blocks = width // lane
    columns = blocks // devices
    sub = 16
    pair = 2 * lane

    def place_of(slot, h):
        start = lax.bitwise_xor(me, slot) * rows + h * part_rows
        return pl.multiple_of(start, 16)

    def copies(c):
        made = []
        for h in range(chunks):
            for slot in range(devices):
                made.append(
                    pltpu.make_async_copy(
                        ins[h * devices + slot].at[:, pl.ds(c * pair, pair)],
                        in_ref.at[c, pl.ds(place_of(slot, h), part_rows), :],
                        in_sem.at[c, h, slot],
                    )
                )
        return made

    arriving = [copies(c) for c in range(columns)]
    for group in arriving:
        for copy in group:
            copy.start()

    for c in range(columns):
        for copy in arriving[c]:
            copy.wait()
        here = slice(c * lane, (c + 1) * lane)

        def load_body(i, carry, c=c, here=here):
            at = pl.multiple_of(i * sub, sub)
            real, imag = [], []
            for b in range(count):
                row = pl.multiple_of(at + b * lane, sub)
                real.append(in_ref[c, pl.ds(row, sub), 0:lane].astype(F32))
                imag.append(in_ref[c, pl.ds(row, sub), lane:pair].astype(F32))
            real, imag = small_dft(real, imag, -1)
            for k in range(count):
                x_ref[k, pl.ds(at, sub), here] = real[k].astype(BF16)
                x_ref[k, pl.ds(lane + at, sub), here] = imag[k].astype(BF16)
            return carry

        lax.fori_loop(0, lane // sub, load_body, 0)

    for k in range(count):
        same = k if 2 * k <= count else count - k
        y = dot(forward_ref[k], x_ref[k])
        yr, yi = y[:lane], y[lane:]
        ur, ui = u_ref[same, 0:lane, :], u_ref[same, lane:pair, :]
        z_ref[k, 0:lane, :] = (yr * ur - yi * ui).astype(BF16)
        z_ref[k, lane:pair, :] = (yr * ui + yi * ur).astype(BF16)
    for k in range(count):
        w_ref[k] = dot(inverse_ref[k], z_ref[k])

    leaving = []
    edge = lax.broadcasted_iota(jnp.int32, (EXTRA, pair), 0)
    for c in range(columns):
        here = slice(c * lane, (c + 1) * lane)

        def store_body(i, carry, c=c, here=here):
            at = pl.multiple_of(i * sub, sub)
            real = [w_ref[k, pl.ds(at, sub), here] for k in range(count)]
            imag = [w_ref[k, pl.ds(lane + at, sub), here] for k in range(count)]
            real, imag = small_dft(real, imag, 1)
            for b in range(count):
                row = pl.multiple_of(at + b * lane, sub)
                out_ref[c, pl.ds(row, sub), 0:lane] = real[b].astype(BF16)
                out_ref[c, pl.ds(row, sub), lane:pair] = imag[b].astype(BF16)
            return carry

        lax.fori_loop(0, lane // sub, store_body, 0)

        def place(tile, row, source):
            return jnp.where(edge == row, jnp.broadcast_to(source.astype(F32), edge.shape), tile)

        for slab in range(devices):
            tile = jnp.zeros(edge.shape, F32)
            start = slab * rows
            after = out_ref[c, start + part_rows : start + part_rows + EXTRA, :].astype(F32)
            tile = place(tile, 0, after[0:1])
            if slab + 1 < devices:
                after = out_ref[c, start + rows : start + rows + EXTRA, :].astype(F32)
                tile = place(tile, 8, after[0:1])
            if slab:
                before = out_ref[c, start - EXTRA : start, :].astype(F32)
                tile = place(tile, EXTRA - 1, before[EXTRA - 1 :])
            edge_ref[c, slab] = tile.astype(BF16)
        for h in range(chunks):
            for slot in range(devices):
                target = outs[h * devices + slot]
                owner = lax.bitwise_xor(me, slot)
                leaving.append(
                    pltpu.make_async_copy(
                        out_ref.at[c, pl.ds(place_of(slot, h), part_rows), :],
                        target.at[pl.ds(0, part_rows), pl.ds(c * pair, pair)],
                        out_sem.at[c, h, slot],
                    )
                )
                leaving[-1].start()
                if h == 0:
                    leaving.append(
                        pltpu.make_async_copy(
                            edge_ref.at[c, owner],
                            target.at[pl.ds(part_rows, EXTRA), pl.ds(c * pair, pair)],
                            edge_sem.at[c, slot],
                        )
                    )
                    leaving[-1].start()
    for copy in leaving:
        copy.wait()


def spectral(me, waves, pieces, tables, lane, width):
    chunks, devices = len(pieces), len(pieces[0])
    part_rows, wide = pieces[0][0].shape
    rows = part_rows * chunks
    columns = wide // (2 * lane)
    height = devices * rows
    count = height // lane
    shapes = []
    for h in range(chunks):
        extra = EXTRA if h == 0 else 0
        shapes += [jax.ShapeDtypeStruct((part_rows + extra, wide), BF16)] * devices
    sent = pl.pallas_call(
        functools.partial(
            spectral_kernel, lane=lane, width=width, rows=rows, devices=devices, chunks=chunks
        ),
        in_specs=[SMEM, FULL, FULL, FULL] + [FULL] * (chunks * devices),
        out_specs=[FULL] * (chunks * devices),
        out_shape=shapes,
        scratch_shapes=[
            pltpu.VMEM((columns, height, 2 * lane), BF16),
            pltpu.VMEM((columns, height, 2 * lane), BF16),
            pltpu.VMEM((columns, devices, EXTRA, 2 * lane), BF16),
            pltpu.VMEM((count, 2 * lane, columns * lane), BF16),
            pltpu.VMEM((count, 2 * lane, columns * lane), BF16),
            pltpu.VMEM((count, 2 * lane, columns * lane), F32),
            pltpu.SemaphoreType.DMA((columns, chunks, devices)),
            pltpu.SemaphoreType.DMA((columns, chunks, devices)),
            pltpu.SemaphoreType.DMA((columns, devices)),
        ],
        compiler_params=params(),
        cost_estimate=cost(height * columns * lane * 8000, height * columns * lane * 16),
        name="spectral",
    )(me, waves, *tables, *[piece for part in pieces for piece in part])
    return [sent[h * devices : (h + 1) * devices] for h in range(chunks)]


def space_kernel(*refs, lane, devices, chunk, first, last):
    me_ref, factor_ref, coef_hbm, block_hbm, twist_ref, inverse_ref, forward_ref = refs[:7]
    ins = refs[7 : 7 + devices]
    at = 7 + devices
    if not first:
        carried_ref = refs[at]
        at += 1
    if last and not first:
        at += 1
    outs = refs[at : at + (1 if last else devices)]
    at += len(outs)
    kept_ref, sent_ref = refs[at : at + 2]
    at += 2
    if first:
        carry_ref = refs[at]
        at += 1
    (
        coef_ref, block_ref, y_ref, s_ref, left_ref, p_ref, fixed_sem, out_sem,
    ) = refs[at:]
    me = me_ref[0]
    padded, wide = ins[0].shape
    per_device = wide // (2 * lane)
    rows, width = coef_ref.shape
    blocks = width // lane
    pair = 2 * lane
    coef_copy = pltpu.make_async_copy(
        coef_hbm.at[pl.ds(chunk * rows, rows), :], coef_ref, fixed_sem.at[0]
    )
    block_copy = pltpu.make_async_copy(block_hbm, block_ref, fixed_sem.at[1])
    coef_copy.start()
    block_copy.start()

    for slot in range(devices):
        left = jnp.concatenate(
            [ins[slot][:, place * pair : (place + 1) * pair] for place in range(per_device)],
            axis=0,
        )
        owner = lax.bitwise_xor(me, slot)
        y_ref[pl.ds(owner * per_device, per_device)] = dot(left, inverse_ref[...]).reshape(
            per_device, padded, pair
        )

    def back(start, target):
        real, imag = [], []
        for k in range(blocks):
            re = y_ref[k, pl.ds(start, 8), 0:lane]
            im = y_ref[k, pl.ds(start, 8), lane:pair]
            if k:
                c, s = twist_ref[0, k : k + 1, :], twist_ref[1, k : k + 1, :]
                re, im = re * c + im * s, im * c - re * s
            real.append(re)
            imag.append(im)
        real, imag = small_dft(real, imag, 1)
        for b in range(blocks):
            here = slice(b * lane, (b + 1) * lane)
            s_ref[0, pl.ds(target, 8), here] = real[b]
            s_ref[1, pl.ds(target, 8), here] = imag[b]

    def back_body(i, carry):
        start = pl.multiple_of(i * 8, 8)
        back(start, pl.multiple_of(start + 8, 8))
        return carry

    if first:
        lax.fori_loop(0, rows // 8 + 1, back_body, 0)
        back(rows + 8, 0)
        carry_ref[:, 0:8, :] = s_ref[:, rows : rows + 8, :]
        carry_ref[:, 8:16, :] = s_ref[:, 0:8, :]
    else:
        lax.fori_loop(0, rows // 8, back_body, 0)
        s_ref[:, 0:8, :] = carried_ref[:, 0:8, :]
        s_ref[:, rows + 8 : rows + 16, :] = carried_ref[:, 8:16, :]

    coef_copy.wait()
    gr, gi = factor_ref[0], factor_ref[1]
    sub = 16

    def correct(i, carry):
        at = pl.multiple_of(i * sub, sub)
        for b in range(blocks):
            here = slice(b * lane, (b + 1) * lane)
            weight = coef_ref[pl.ds(at, sub), here].astype(F32)
            centre, curve = [], []
            for part in range(2):
                near = s_ref[part, pl.ds(at, sub + 16), here]
                mid, up, down = near[8 : 8 + sub], near[9 : 9 + sub], near[7 : 7 + sub]
                centre.append(mid)
                curve.append(up - 2.0 * mid + down)
            re = centre[0] + weight * (gr * curve[0] - gi * curve[1])
            im = centre[1] + weight * (gr * curve[1] + gi * curve[0])
            p_ref[0, pl.ds(at, sub), here] = re
            p_ref[1, pl.ds(at, sub), here] = im
            left_ref[b, pl.ds(at, sub), 0:lane] = re.astype(BF16)
            left_ref[b, pl.ds(at, sub), lane:pair] = im.astype(BF16)
        return carry

    lax.fori_loop(0, rows // sub, correct, 0)
    block_copy.wait()
    leaving = []
    half, _, share = kept_ref.shape
    stride = share // lane
    if stride:
        order = [
            (2 * z + parity) * stride + offset
            for z in range(half) for offset in range(stride) for parity in range(2)
        ]
    else:
        order = list(range(blocks))
    even = None
    for b in order:
        here = slice(b * lane, (b + 1) * lane)
        br, bi = block_ref[0, b], block_ref[1, b]
        square = jnp.concatenate(
            [jnp.concatenate([br, bi], axis=1), jnp.concatenate([-bi, br], axis=1)], axis=0
        )
        change = dot(left_ref[b], square)
        re = p_ref[0, :, here] + change[:, 0:lane]
        im = p_ref[1, :, here] + change[:, lane:pair]
        if not stride:
            per_tile = lane // share
            for piece in range(per_tile):
                owner = b * per_tile + piece
                value = re[:, piece * share : (piece + 1) * share].astype(BF16)
                place = lax.bitwise_xor(jnp.int32(owner // 2), me_ref[2])

                @pl.when(me_ref[1] == owner % 2)
                def _(place=place, value=value):
                    kept_ref[place] = value

                @pl.when(me_ref[1] != owner % 2)
                def _(place=place, value=value):
                    sent_ref[place] = value
        elif (b // stride) % 2 == 0:
            even = re
        else:
            place = lax.bitwise_xor(jnp.int32(b // stride // 2), me_ref[2])
            cols = slice((b % stride) * lane, (b % stride + 1) * lane)
            kept_ref[place, :, cols] = jnp.where(me_ref[1] == 0, even, re).astype(BF16)
            sent_ref[place, :, cols] = jnp.where(me_ref[1] == 0, re, even).astype(BF16)
        p_ref[0, :, here] = re
        p_ref[1, :, here] = im
        if last:
            leaving.append(
                pltpu.make_async_copy(
                    p_ref.at[:, :, pl.ds(b * lane, lane)],
                    outs[0].at[:, pl.ds(chunk * rows, rows), pl.ds(b * lane, lane)],
                    out_sem.at[b],
                )
            )
            leaving[-1].start()
    if not last:

        def load(part, at, b):
            return p_ref[part, at, b * lane : (b + 1) * lane]

        forward_lanes(load, rows, blocks, lane, twist_ref, left_ref)
        for slot in range(devices):
            parts = slot_products(left_ref, forward_ref, me, slot, per_device)
            for place, part in enumerate(parts):
                outs[slot][:, place * pair : (place + 1) * pair] = part
    for copy in leaving:
        copy.wait()


def space(me, pieces, coefficient, factor, inverse_blocks, tables, lane, chunk, carried, field,
          last):
    devices = len(pieces)
    padded, wide = pieces[0].shape
    first = chunk == 0
    rows = padded - EXTRA if first else padded
    all_rows, width = coefficient.shape
    blocks = width // lane
    if last:
        shapes = [jax.ShapeDtypeStruct((2, all_rows, width), F32)]
    else:
        shapes = [jax.ShapeDtypeStruct((rows, wide), BF16)] * devices
    specs = [ANY if last else FULL] * len(shapes)
    groups = lax.axis_size("freq")
    half = jax.ShapeDtypeStruct((groups // 2, rows, width // groups), BF16)
    shapes = shapes + [half, half]
    specs = specs + [FULL, FULL]
    if first:
        shapes = shapes + [jax.ShapeDtypeStruct((2, 16, width), F32)]
        specs = specs + [FULL]
    operands = [me, factor, coefficient, inverse_blocks, tables[2], tables[1], tables[0], *pieces]
    in_specs = [SMEM, SMEM, ANY, ANY, FULL, FULL, FULL] + [FULL] * devices
    aliases = {}
    if not first:
        operands.append(carried)
        in_specs.append(FULL)
        if last:
            aliases = {len(operands): 0}
            operands.append(field)
            in_specs.append(ANY)
    got = pl.pallas_call(
        functools.partial(
            space_kernel, lane=lane, devices=devices, chunk=chunk, first=first, last=last
        ),
        in_specs=in_specs,
        out_specs=specs,
        out_shape=shapes,
        scratch_shapes=[
            pltpu.VMEM((rows, width), BF16),
            pltpu.VMEM(inverse_blocks.shape, BF16),
            pltpu.VMEM((blocks, padded, 2 * lane), F32),
            pltpu.VMEM((2, rows + 16, width), F32),
            pltpu.VMEM((blocks, rows, 2 * lane), BF16),
            pltpu.VMEM((2, rows, width), F32),
            pltpu.SemaphoreType.DMA((2,)),
            pltpu.SemaphoreType.DMA((blocks,)),
        ],
        input_output_aliases=aliases,
        compiler_params=params(),
        cost_estimate=cost(rows * width * 8000, rows * width * 12),
        name="space_last" if last else "space",
    )(*operands)
    got = list(got)
    carry = got.pop() if first else None
    sent, kept = got.pop(), got.pop()
    image = (kept, sent)
    return (got[0] if last else got), image, carry


def swap(value, axis, distance):
    count = lax.axis_size(axis)
    return lax.ppermute(value, axis, [(i, i ^ distance) for i in range(count)])


def exchange(pieces):
    return [pieces[0]] + [swap(piece, "rows", k) for k, piece in enumerate(pieces) if k]


def add_all(value, axis, distances):
    return value + sum(swap(value, axis, distance) for distance in distances)


def collect(image):
    kept, sent = image
    joined = (kept.astype(F32) + swap(sent, "freq", 1).astype(F32)).astype(BF16)
    parts = [joined[0]]
    for j in range(1, joined.shape[0]):
        parts.append(swap(joined[j], "freq", 2 * j))
    return sum(part.astype(F32) for part in parts)


def total(value):
    groups, rows = lax.axis_size("freq"), lax.axis_size("rows")
    value = add_all(value, "freq", [1])
    value = add_all(value, "freq", range(2, groups, 2))
    return add_all(value, "rows", range(1, rows))


def shards(wavefield, block_inverse, coefficient, correction_factor, frequencies, slowness):
    freq_local, rows_local, width = wavefield.shape[1:]
    devices = lax.axis_size("rows")
    groups = lax.axis_size("freq")
    height = rows_local * devices
    lane = block_inverse.shape[-1]
    chunks = 2
    limit = (4.5 * 1.0) ** 2 * 1.0001
    x_tables = lane_tables(width, lane)
    y_tables = row_tables(height, lane)
    place = lax.axis_index("freq")
    me = jnp.stack([lax.axis_index("rows"), place % 2, place // 2]).astype(jnp.int32)
    partials = [[None] * chunks for _ in range(DEPTHS)]
    columns = width // lane // devices
    fields = []
    for f in range(freq_local):
        factor = correction_factor[:, f]
        made = [
            forward_x(me, wavefield[:, f], x_tables, lane, devices, h, chunks)
            for h in range(chunks)
        ]
        squared = (frequencies[f] * slowness) ** 2
        table = waves(me, squared, made[-1][0], lane, width, height, columns, limit)
        pieces = [exchange(part) for part in made]
        for depth_step in range(DEPTHS):
            last = depth_step == DEPTHS - 1
            sent = spectral(me, table[depth_step], pieces, y_tables, lane, width)
            arrived = [exchange(part) for part in sent]
            pieces, carry, field = [], None, None
            for h in range(chunks):
                made, image, carried = space(
                    me, arrived[h], coefficient, factor, block_inverse[:, f], x_tables, lane, h,
                    carry, field, last,
                )
                carry = carry if carried is None else carried
                if last:
                    field = made
                else:
                    pieces.append(exchange(made))
                before = partials[depth_step][h]
                if before is not None:
                    image = [
                        (a.astype(F32) + b.astype(F32)).astype(BF16)
                        for a, b in zip(before, image)
                    ]
                partials[depth_step][h] = image
        fields.append(field)
    shares = jnp.stack(
        [jnp.concatenate([collect(image) for image in images]) for images in partials]
    )
    energy = total(jnp.sum(shares * shares, axis=(1, 2)))
    scale = 1.0 / jnp.sqrt(energy / (height * width) + epsilon)
    return shares * scale[:, None, None], jnp.stack(fields, axis=1)


def solution(mesh):
    placed = (
        P(None, "freq", "rows", None),
        P(None, "freq", None, None, None),
        P("rows", None),
        P(None, "freq"),
        P("freq"),
        P(),
    )
    return jax.shard_map(
        shards,
        mesh=mesh,
        in_specs=placed,
        out_specs=(P(None, "rows", "freq"), P(None, "freq", "rows", None)),
        check_vma=False,
    )
```

time: 471 us -> 172 us (0.37)
  local copies, waits for them, and re-layouts: 134 us -> 3.91 us
  blocking collectives: 71.7 us -> 0 us
  matrix products: 68.2 us -> 0 us
  other arithmetic: 59.5 us -> 1.62 us
  Pallas kernels: 0 us -> 45.2 us
  starting transfers between devices: 25.2 us -> 54.6 us
  waiting for transfers between devices: 89 us -> 63.5 us
  between operations: 17.6 us -> 1.65 us
    dot_general x24 -> x0, matrix products: 68.2 us -> none  [the longest x8 41.4 us: transform(): result = jnp.einsum(second_form, turned, inner_table, precision=accuracy)]
    ppermute x4 -> x47, waiting for transfers between devices: 0.01 us -> 63.5 us  [swap(): return lax.ppermute(value, axis, [(i, i ^ distance) for i in range(count)])]
    all_to_all x3 -> x0, waiting for transfers between devices: 62.5 us -> none  [the longest x2 41.5 us: shards(): lax.all_to_all(spectra.astype(jnp.bfloat16), 'rows', split_axis=3, concat...]
    pallas_call x0 -> x9, Pallas kernels: none -> 45.2 us  [the longest x4 24.1 us: space(): pl.pallas_call(functools.partial(space_kernel, lane=lane, devices=devices...]
    psum x1 -> x0, blocking collectives: 44 us -> none  [shards(): energy = lax.psum(jnp.sum(shares * shares, axis=(1, 2)), ('freq', 'rows'))]
    ppermute x4 -> x47, starting transfers between devices: 12.9 us -> 54.6 us  [swap(): return lax.ppermute(value, axis, [(i, i ^ distance) for i in range(count)])]
    convert_element_type x10 -> x0, local copies, waits for them, and re-layouts: 40.7 us -> none  [the longest x4 30.4 us: shards(): spectra.astype(jnp.bfloat16)]
    slice x20 -> x0, local copies, waits for them, and re-layouts: 32.6 us -> none  [the longest x3 7.82 us: shards(): stacked_field[1]]
  transfers between devices with their start and end apart: 8 -> 47, of which waited for: 4 -> 23; matrix products, arithmetic and copies ran while one was open for 9% -> 0% of each run, Pallas kernels for 0% -> 22%
where the time goes in v1:
time: 172 us; the launch traced here: 171 us
  waiting for transfers between devices  63.5 us (37%)
  starting transfers between devices  54.6 us (32%)
  Pallas kernels  45.2 us (26%)
  local copies, waits for them, and re-layouts  3.91 us (2%)
    ppermute x47, waiting for transfers between devices, swap(): return lax.ppermute(value, axis, [(i, i ^ distance) for i in range(count)])  63.5 us
    ppermute x47, starting transfers between devices, swap(): return lax.ppermute(value, axis, [(i, i ^ distance) for i in range(count)])  54.6 us
    pallas_call x4, Pallas kernels, space(): pl.pallas_call(functools.partial(space_kernel, lane=lane, devices=devices...  24.1 us
    pallas_call x2, Pallas kernels, spectral(): pl.pallas_call(functools.partial(spectral_kernel, lane=lane, width=width,...  12.4 us
    pallas_call x1, Pallas kernels, waves(): pl.pallas_call(functools.partial(wave_kernel, lane=lane, width=width, hei...  4.96 us
    unnamed x24, local copies, waits for them, and re-layouts  3.85 us
    pallas_call x2, Pallas kernels, forward_x(): pl.pallas_call(functools.partial(first_kernel, lane=lane, per_device=per_...  3.79 us
  transfers between devices with their start and end apart: 47, of which 23 were waited for; matrix products, arithmetic and copies ran while one was open for 0% of the time, Pallas kernels for 22%

profile of v1, /device:TPU:10, one launch (start us, length us, event | category | flops | bytes accessed | tf_op | source)
XLA Modules:
  0.0 170.6 jit_solution(13644371046444862640)
XLA Ops:
  0.7 2.2 %copy-done = f32[2,1,256,2048]{3,2,1,0:T(8,128)S(1)} copy-done((f32[2,1,256,2048]{3,2,1,0:T(8,128)S(1)}, f32[2,1,256,2048]{3,2,1,0:T(8,128)}, u32[]{:S(2)}) %copy-start) | copy-done | bytes 4194328
  4.5 1.9 %forward_x.3 = (bf16[128,1024]{1,0:T(8,128)(2,1)S(1)}, bf16[128,1024]{1,0:T(8,128)(2,1)S(1)}, bf16[128,1024]{1,0:T(8,128)(2,1)S(1)}, bf16[128,1024]{1,0:T(8,128)(2,1)S(1)}) custom-call(s32[3]{0:T(128)S(1)} %pad_add_fusion.me_ref.refs_0_, f32[2,256,2048]{2,1,0:T(8,128)S(1)} %bitcast.59, f32[2,16,128]{2,1,0:T(8,128)S(1)} %copy-done.5, ...), custom_call_target="tpu_custom_call" | custom-call | flops 1048576000 | bytes 3145728 | tf_op jit(solution)/shard_map/forward_x/pallas_call | solution.py:168
  7.0 1.5 collective-permute-start.1
  8.6 1.4 collective-permute-start.2
  10.0 1.9 %forward_x.2 = (bf16[128,1024]{1,0:T(8,128)(2,1)S(1)}, bf16[128,1024]{1,0:T(8,128)(2,1)S(1)}, bf16[128,1024]{1,0:T(8,128)(2,1)S(1)}, bf16[128,1024]{1,0:T(8,128)(2,1)S(1)}) custom-call(s32[3]{0:T(128)S(1)} %pad_add_fusion.me_ref.refs_0_, f32[2,256,2048]{2,1,0:T(8,128)S(1)} %bitcast.60, f32[2,16,128]{2,1,0:T(8,128)S(1)} %copy-done.5, ...), custom_call_target="tpu_custom_call" | custom-call | flops 1048576000 | bytes 3145728 | tf_op jit(solution)/shard_map/forward_x/pallas_call | solution.py:168
  12.5 1.5 collective-permute-start.4
  15.7 1.5 collective-permute-start.5
  17.2 5.0 %waves.1 = (f32[5,256,512]{2,1,0:T(8,128)S(1)}, f32[5,256,512]{2,1,0:T(8,128)S(1)}) custom-call(s32[3]{0:T(128)S(1)} %pad_add_fusion.me_ref.refs_0_, f32[2]{0:T(128)S(1)} %multiply_multiply_fusion.squared_ref, bf16[128,1024]{1,0:T(8,128)(2,1)S(1)} %get-tuple-element.48.after_ref.refs_8_), custom_call_target="tpu_custom_call" | custom-call | flops 4194304000 | bytes 8388608 | tf_op jit(solution)/shard_map/waves/pallas_call | solution.py:251
  22.3 4.7 %collective-permute-done.3.refs_9_ = bf16[128,1024]{1,0:T(8,128)(2,1)S(1)} collective-permute-done((bf16[128,1024]{1,0:T(8,128)(2,1)S(1)}, bf16[128,1024]{1,0:T(8,128)(2,1)S(1)}, u32[]{:S(2)}, u32[]{:S(2)}) %collective-permute-start.3) | collective-permute-done | bytes 262176 | tf_op jit(solution)/shard_map/ppermute | solution.py:651
  27.0 5.4 %collective-permute-done.5.refs_11_ = bf16[128,1024]{1,0:T(8,128)(2,1)S(1)} collective-permute-done((bf16[128,1024]{1,0:T(8,128)(2,1)S(1)}, bf16[128,1024]{1,0:T(8,128)(2,1)S(1)}, u32[]{:S(2)}, u32[]{:S(2)}) %collective-permute-start.5) | collective-permute-done | bytes 262176 | tf_op jit(solution)/shard_map/ppermute | solution.py:651
  32.5 6.1 %spectral.2 = (bf16[144,1024]{1,0:T(8,128)(2,1)S(1)}, bf16[144,1024]{1,0:T(8,128)(2,1)S(1)}, bf16[144,1024]{1,0:T(8,128)(2,1)S(1)}, bf16[144,1024]{1,0:T(8,128)(...) custom-call(s32[3]{0:T(128)S(1)} %pad_add_fusion.me_ref.refs_0_, ...), custom_call_target="tpu_custom_call" | custom-call | flops 4194304000 | bytes 8388608 | tf_op jit(solution)/shard_map/spectral/pallas_call | solution.py:401
  39.4 1.5 collective-permute-start.7
  40.9 1.2 collective-permute-start.8
  42.9 1.5 collective-permute-start.14
  44.4 4.1 %collective-permute-done.6.refs_8_ = bf16[144,1024]{1,0:T(8,128)(2,1)S(1)} collective-permute-done((bf16[144,1024]{1,0:T(8,128)(2,1)S(1)}, bf16[144,1024]{1,0:T(8,128)(2,1)S(1)}, u32[]{:S(2)}, u32[]{:S(2)}) %collective-permute-start.6) | collective-permute-done | bytes 294944 | tf_op jit(solution)/shard_map/ppermute | solution.py:651
  48.5 1.7 %collective-permute-start.15 = (bf16[128,1024]{1,0:T(8,128)(2,1)S(1)}, bf16[128,1024]{1,0:T(8,128)(2,1)S(1)}, u32[]{:S(2)}, u32[]{:S(2)}) collective-permute-start(bf16[128,1024]{1,0:T(8,128)(2,1)S(1)} %get-tuple-element.66), channel_id=1, source_target_pairs={{0,3},{1,2},{2,1},{3,0},{4,7},{5,6},{6,5},{7,4},{8,11},{9,10},{10,... | collective-permute-start | bytes 786440 | tf_op jit(solution)/shard_map/ppermute | solution.py:651
  50.3 5.4 %collective-permute-done.7.refs_9_ = bf16[144,1024]{1,0:T(8,128)(2,1)S(1)} collective-permute-done((bf16[144,1024]{1,0:T(8,128)(2,1)S(1)}, bf16[144,1024]{1,0:T(8,128)(2,1)S(1)}, u32[]{:S(2)}, u32[]{:S(2)}) %collective-permute-start.7) | collective-permute-done | bytes 294944 | tf_op jit(solution)/shard_map/ppermute | solution.py:651
  55.7 5.1 %space.2 = (bf16[128,1024]{1,0:T(8,128)(2,1)S(1)}, bf16[128,1024]{1,0:T(8,128)(2,1)S(1)}, bf16[128,1024]{1,0:T(8,128)(2,1)S(1)}, bf16[128,1024]{1,0:T(8,128)(2,1...) custom-call(s32[3]{0:T(128)S(1)} %pad_add_fusion.me_ref.refs_0_, ...), custom_call_target="tpu_custom_call" | custom-call | flops 2097152000 | bytes 3145728 | tf_op jit(solution)/shard_map/space/pallas_call | solution.py:620
  60.9 3.5 %collective-permute-done.14.refs_9_ = bf16[128,1024]{1,0:T(8,128)(2,1)S(1)} collective-permute-done((bf16[128,1024]{1,0:T(8,128)(2,1)S(1)}, bf16[128,1024]{1,0:T(8,128)(2,1)S(1)}, u32[]{:S(2)}, u32[]{:S(2)}) %collective-permute-start.14) | collective-permute-done | bytes 262176 | tf_op jit(solution)/shard_map/ppermute | solution.py:651
  64.4 5.0 %space.3 = (bf16[128,1024]{1,0:T(8,128)(2,1)S(1)}, bf16[128,1024]{1,0:T(8,128)(2,1)S(1)}, bf16[128,1024]{1,0:T(8,128)(2,1)S(1)}, bf16[128,1024]{1,0:T(8,128)(2,1...) custom-call(s32[3]{0:T(128)S(1)} %pad_add_fusion.me_ref.refs_0_, f32[2]{0:T(128)S(1)} %bitcast.66, ...), custom_call_target="tpu_custom_call" | custom-call | flops 2097152000 | bytes 3145728 | tf_op jit(solution)/shard_map/space/pallas_call | solution.py:620
  69.5 1.5 collective-permute-start.20
  71.5 1.5 collective-permute-start.22
  73.0 1.4 collective-permute-start.23
  75.3 3.5 %collective-permute-done.20.refs_5_ = bf16[128,1024]{1,0:T(8,128)(2,1)S(1)} collective-permute-done((bf16[128,1024]{1,0:T(8,128)(2,1)S(1)}, bf16[128,1024]{1,0:T(8,128)(2,1)S(1)}, u32[]{:S(2)}, u32[]{:S(2)}) %collective-permute-start.20) | collective-permute-done | bytes 262176 | tf_op jit(solution)/shard_map/ppermute | solution.py:651
  78.7 1.4 collective-permute-start.25
  80.2 5.6 %collective-permute-done.21.refs_6_ = bf16[128,1024]{1,0:T(8,128)(2,1)S(1)} collective-permute-done((bf16[128,1024]{1,0:T(8,128)(2,1)S(1)}, bf16[128,1024]{1,0:T(8,128)(2,1)S(1)}, u32[]{:S(2)}, u32[]{:S(2)}) %collective-permute-start.21) | collective-permute-done | bytes 262176 | tf_op jit(solution)/shard_map/ppermute | solution.py:651
  86.2 2.7 %collective-permute-start.12 = (bf16[128,256]{1,0:T(8,128)(2,1)S(1)}, bf16[128,256]{1,0:T(8,128)(2,1)S(1)}, u32[]{:S(2)}, u32[]{:S(2)}) collective-permute-start(bf16[128,256]{1,0:T(8,128)(2,1)S(1)} %get-tuple-element.97), channel_id=1, source_target_pairs={{0,24},{4,28},{8,16},{12,20},{16,8},{20,12},{24,0},{28,4},{1,25},{... | collective-permute-start | bytes 196616 | tf_op jit(solution)/shard_map/ppermute | solution.py:651
  90.0 2.6 %collective-permute-start.11 = (bf16[128,256]{1,0:T(8,128)(2,1)S(1)}, bf16[128,256]{1,0:T(8,128)(2,1)S(1)}, u32[]{:S(2)}, u32[]{:S(2)}) collective-permute-start(bf16[128,256]{1,0:T(8,128)(2,1)S(1)} %get-tuple-element.98), channel_id=1, source_target_pairs={{0,16},{4,20},{8,24},{12,28},{16,0},{20,4},{24,8},{28,12},{1,17},{... | collective-permute-start | bytes 196616 | tf_op jit(solution)/shard_map/ppermute | solution.py:651
  92.6 3.6 %collective-permute-done.24.refs_10_ = bf16[128,1024]{1,0:T(8,128)(2,1)S(1)} collective-permute-done((bf16[128,1024]{1,0:T(8,128)(2,1)S(1)}, bf16[128,1024]{1,0:T(8,128)(2,1)S(1)}, u32[]{:S(2)}, u32[]{:S(2)}) %collective-permute-start.24) | collective-permute-done | bytes 262176 | tf_op jit(solution)/shard_map/ppermute | solution.py:651
  96.7 2.7 %collective-permute-start.19 = (bf16[128,256]{1,0:T(8,128)(2,1)S(1)}, bf16[128,256]{1,0:T(8,128)(2,1)S(1)}, u32[]{:S(2)}, u32[]{:S(2)}) collective-permute-start(bf16[128,256]{1,0:T(8,128)(2,1)S(1)} %get-tuple-element.100), channel_id=1, source_target_pairs={{0,24},{4,28},{8,16},{12,20},{16,8},{20,12},{24,0},{28,4},{1,25},{... | collective-permute-start | bytes 196616 | tf_op jit(solution)/shard_map/ppermute | solution.py:651
  99.4 6.2 %spectral.3 = (bf16[144,1024]{1,0:T(8,128)(2,1)S(1)}, bf16[144,1024]{1,0:T(8,128)(2,1)S(1)}, bf16[144,1024]{1,0:T(8,128)(2,1)S(1)}, bf16[144,1024]{1,0:T(8,128)(...) custom-call(s32[3]{0:T(128)S(1)} %pad_add_fusion.me_ref.refs_0_, ...), custom_call_target="tpu_custom_call" | custom-call | flops 4194304000 | bytes 8388608 | tf_op jit(solution)/shard_map/spectral/pallas_call | solution.py:401
  105.6 1.3 collective-permute-start.18
  107.6 2.9 %collective-permute-start.28 = (bf16[144,1024]{1,0:T(8,128)(2,1)S(1)}, bf16[144,1024]{1,0:T(8,128)(2,1)S(1)}, u32[]{:S(2)}, u32[]{:S(2)}) collective-permute-start(bf16[144,1024]{1,0:T(8,128)(2,1)S(1)} %get-tuple-element.82), channel_id=1, source_target_pairs={{0,3},{1,2},{2,1},{3,0},{4,7},{5,6},{6,5},{7,4},{8,11},{9,10},{10,... | collective-permute-start | bytes 884744 | tf_op jit(solution)/shard_map/ppermute | solution.py:651
  111.5 5.3 %collective-permute-done.26.refs_8_ = bf16[144,1024]{1,0:T(8,128)(2,1)S(1)} collective-permute-done((bf16[144,1024]{1,0:T(8,128)(2,1)S(1)}, bf16[144,1024]{1,0:T(8,128)(2,1)S(1)}, u32[]{:S(2)}, u32[]{:S(2)}) %collective-permute-start.26) | collective-permute-done | bytes 294944 | tf_op jit(solution)/shard_map/ppermute | solution.py:651
  116.8 6.8 %collective-permute-done.27.refs_9_ = bf16[144,1024]{1,0:T(8,128)(2,1)S(1)} collective-permute-done((bf16[144,1024]{1,0:T(8,128)(2,1)S(1)}, bf16[144,1024]{1,0:T(8,128)(2,1)S(1)}, u32[]{:S(2)}, u32[]{:S(2)}) %collective-permute-start.27) | collective-permute-done | bytes 294944 | tf_op jit(solution)/shard_map/ppermute | solution.py:651
  123.6 7.1 %space_last.2 = (f32[2,256,2048]{2,1,0:T(8,128)}, bf16[4,128,256]{2,1,0:T(8,128)(2,1)S(1)}, bf16[4,128,256]{2,1,0:T(8,128)(2,1)S(1)}, f32[2,16,2048]{2,1,0:T(8,128)S(1)}) custom-call(s32[3]{0:T(128)S(1)} %pad_add_fusion.me_ref.refs_0_, f32[2]{0:T(128)S(1)} %bitcast.67, bf16[256,2048]{1,0:T(8,128)(2,1)S(1)} %copy-done.3, ...), custom_call_target="tpu_custom_call" | custom-call | flops 2097152000 | bytes 3145728 | tf_op jit(solution)/shard_map/space_last/pallas_call | solution.py:620
  131.0 6.9 %space_last.3 = (f32[2,256,2048]{2,1,0:T(8,128)}, bf16[4,128,256]{2,1,0:T(8,128)(2,1)S(1)}, bf16[4,128,256]{2,1,0:T(8,128)(2,1)S(1)}) custom-call(s32[3]{0:T(128)S(1)} %pad_add_fusion.me_ref.refs_0_, f32[2]{0:T(128)S(1)} %bitcast.68, bf16[256,2048]{1,0:T(8,128)(2,1)S(1)} %copy-done.3, ...), custom_call_target="tpu_custom_call", output_to_operand_aliasing={{0}: (12, {})} | custom-call | flops 2097152000 | bytes 3145728 | tf_op jit(solution)/shard_map/space_last/pallas_call | solution.py:620
  138.4 1.3 collective-permute-start.30
  140.9 2.0 %collective-permute-start.31 = (bf16[128,256]{1,0:T(8,128)(2,1)S(1)}, bf16[128,256]{1,0:T(8,128)(2,1)S(1)}, u32[]{:S(2)}, u32[]{:S(2)}) collective-permute-start(bf16[128,256]{1,0:T(8,128)(2,1)S(1)} %get-tuple-element.104), channel_id=1, source_target_pairs={{0,16},{4,20},{8,24},{12,28},{16,0},{20,4},{24,8},{28,12},{1,17},{... | collective-permute-start | bytes 196616 | tf_op jit(solution)/shard_map/ppermute | solution.py:651
  143.9 1.5 collective-permute-start.39
  145.5 2.0 %collective-permute-start.38 = (bf16[128,256]{1,0:T(8,128)(2,1)S(1)}, bf16[128,256]{1,0:T(8,128)(2,1)S(1)}, u32[]{:S(2)}, u32[]{:S(2)}) collective-permute-start(bf16[128,256]{1,0:T(8,128)(2,1)S(1)} %get-tuple-element.107), channel_id=1, source_target_pairs={{0,16},{4,20},{8,24},{12,28},{16,0},{20,4},{24,8},{28,12},{1,17},{... | collective-permute-start | bytes 196616 | tf_op jit(solution)/shard_map/ppermute | solution.py:651
  148.1 1.3 collective-permute-done.37
  149.3 3.9 %collective-permute-done.39 = bf16[128,256]{1,0:T(8,128)(2,1)S(1)} collective-permute-done((bf16[128,256]{1,0:T(8,128)(2,1)S(1)}, bf16[128,256]{1,0:T(8,128)(2,1)S(1)}, u32[]{:S(2)}, u32[]{:S(2)}) %collective-permute-start.39) | collective-permute-done | bytes 65568 | tf_op jit(solution)/shard_map/ppermute | solution.py:651
  154.7 1.2 collective-permute-start.43
  155.9 3.9 %collective-permute-start.42 = (f32[2]{0:T(128)S(1)}, f32[2]{0:T(128)S(1)}, u32[]{:S(2)}, u32[]{:S(2)}) collective-permute-start(f32[2]{0:T(128)S(1)} %add.94), channel_id=1, source_target_pairs={{0,16},{4,20},{8,24},{12,28},{16,0},{20,4},{24,8},{28,12},{1,17},{... | collective-permute-start | bytes 32 | tf_op jit(solution)/shard_map/ppermute | solution.py:651
  159.8 1.5 collective-permute-done.42
  161.3 2.0 %collective-permute-done.41 = f32[2]{0:T(128)S(1)} collective-permute-done((f32[2]{0:T(128)S(1)}, f32[2]{0:T(128)S(1)}, u32[]{:S(2)}, u32[]{:S(2)}) %collective-permute-start.41) | collective-permute-done | bytes 40 | tf_op jit(solution)/shard_map/ppermute | solution.py:651
  163.4 1.5 collective-permute-start.46
  (100 shorter events, 21.6 us)
Async XLA Ops:
  6.4 9.2 %collective-permute-start = (bf16[128,1024]{1,0:T(8,128)(2,1)S(1)}, bf16[128,1024]{1,0:T(8,128)(2,1)S(1)}, u32[]{:S(2)}, u32[]{:S(2)}) collective-permute-start(bf16[128,1024]{1,0:T(8,128)(2,1)S(1)} %get-tuple-element.51), channel_id=1, source_target_pairs={{0,1},{1,0},{2,3},{3,2},{4,5},{5,4},{6,7},{7,6},{8,9},{9,8},{10,11... | collective-permute-start | bytes 786440 | tf_op jit(solution)/shard_map/ppermute | solution.py:651
  7.0 15.1 %collective-permute-start.1 = (bf16[128,1024]{1,0:T(8,128)(2,1)S(1)}, bf16[128,1024]{1,0:T(8,128)(2,1)S(1)}, u32[]{:S(2)}, u32[]{:S(2)}) collective-permute-start(bf16[128,1024]{1,0:T(8,128)(2,1)S(1)} %get-tuple-element.52), channel_id=1, source_target_pairs={{0,2},{1,3},{2,0},{3,1},{4,6},{5,7},{6,4},{7,5},{8,10},{9,11},{10,... | collective-permute-start | bytes 786440 | tf_op jit(solution)/shard_map/ppermute | solution.py:651
  8.6 13.7 %collective-permute-start.2 = (bf16[128,1024]{1,0:T(8,128)(2,1)S(1)}, bf16[128,1024]{1,0:T(8,128)(2,1)S(1)}, u32[]{:S(2)}, u32[]{:S(2)}) collective-permute-start(bf16[128,1024]{1,0:T(8,128)(2,1)S(1)} %get-tuple-element.53), channel_id=1, source_target_pairs={{0,3},{1,2},{2,1},{3,0},{4,7},{5,6},{6,5},{7,4},{8,11},{9,10},{10,... | collective-permute-start | bytes 786440 | tf_op jit(solution)/shard_map/ppermute | solution.py:651
  11.9 15.1 %collective-permute-start.3 = (bf16[128,1024]{1,0:T(8,128)(2,1)S(1)}, bf16[128,1024]{1,0:T(8,128)(2,1)S(1)}, u32[]{:S(2)}, u32[]{:S(2)}) collective-permute-start(bf16[128,1024]{1,0:T(8,128)(2,1)S(1)} %get-tuple-element.54), channel_id=1, source_target_pairs={{0,1},{1,0},{2,3},{3,2},{4,5},{5,4},{6,7},{7,6},{8,9},{9,8},{10,11... | collective-permute-start | bytes 786440 | tf_op jit(solution)/shard_map/ppermute | solution.py:651
  12.5 14.5 %collective-permute-start.4 = (bf16[128,1024]{1,0:T(8,128)(2,1)S(1)}, bf16[128,1024]{1,0:T(8,128)(2,1)S(1)}, u32[]{:S(2)}, u32[]{:S(2)}) collective-permute-start(bf16[128,1024]{1,0:T(8,128)(2,1)S(1)} %get-tuple-element.55), channel_id=1, source_target_pairs={{0,2},{1,3},{2,0},{3,1},{4,6},{5,7},{6,4},{7,5},{8,10},{9,11},{10,... | collective-permute-start | bytes 786440 | tf_op jit(solution)/shard_map/ppermute | solution.py:651
  15.7 16.7 %collective-permute-start.5 = (bf16[128,1024]{1,0:T(8,128)(2,1)S(1)}, bf16[128,1024]{1,0:T(8,128)(2,1)S(1)}, u32[]{:S(2)}, u32[]{:S(2)}) collective-permute-start(bf16[128,1024]{1,0:T(8,128)(2,1)S(1)} %get-tuple-element.56), channel_id=1, source_target_pairs={{0,3},{1,2},{2,1},{3,0},{4,7},{5,6},{6,5},{7,4},{8,11},{9,10},{10,... | collective-permute-start | bytes 786440 | tf_op jit(solution)/shard_map/ppermute | solution.py:651
  32.4 23.2 %copy-start.3 = (bf16[256,2048]{1,0:T(8,128)(2,1)S(1)}, bf16[256,2048]{1,0:T(8,128)(2,1)}, u32[]{:S(2)}) copy-start(bf16[256,2048]{1,0:T(8,128)(2,1)} %refs_2_.9) | copy-start | bytes 3145732
  38.6 9.9 %collective-permute-start.6 = (bf16[144,1024]{1,0:T(8,128)(2,1)S(1)}, bf16[144,1024]{1,0:T(8,128)(2,1)S(1)}, u32[]{:S(2)}, u32[]{:S(2)}) collective-permute-start(bf16[144,1024]{1,0:T(8,128)(2,1)S(1)} %get-tuple-element.58), channel_id=1, source_target_pairs={{0,1},{1,0},{2,3},{3,2},{4,5},{5,4},{6,7},{7,6},{8,9},{9,8},{10,11... | collective-permute-start | bytes 884744 | tf_op jit(solution)/shard_map/ppermute | solution.py:651
  39.4 16.2 %collective-permute-start.7 = (bf16[144,1024]{1,0:T(8,128)(2,1)S(1)}, bf16[144,1024]{1,0:T(8,128)(2,1)S(1)}, u32[]{:S(2)}, u32[]{:S(2)}) collective-permute-start(bf16[144,1024]{1,0:T(8,128)(2,1)S(1)} %get-tuple-element.59), channel_id=1, source_target_pairs={{0,2},{1,3},{2,0},{3,1},{4,6},{5,7},{6,4},{7,5},{8,10},{9,11},{10,... | collective-permute-start | bytes 884744 | tf_op jit(solution)/shard_map/ppermute | solution.py:651
  40.9 14.7 %collective-permute-start.8 = (bf16[144,1024]{1,0:T(8,128)(2,1)S(1)}, bf16[144,1024]{1,0:T(8,128)(2,1)S(1)}, u32[]{:S(2)}, u32[]{:S(2)}) collective-permute-start(bf16[144,1024]{1,0:T(8,128)(2,1)S(1)} %get-tuple-element.60), channel_id=1, source_target_pairs={{0,3},{1,2},{2,1},{3,0},{4,7},{5,6},{6,5},{7,4},{8,11},{9,10},{10,... | collective-permute-start | bytes 884744 | tf_op jit(solution)/shard_map/ppermute | solution.py:651
  42.2 18.7 %collective-permute-start.13 = (bf16[128,1024]{1,0:T(8,128)(2,1)S(1)}, bf16[128,1024]{1,0:T(8,128)(2,1)S(1)}, u32[]{:S(2)}, u32[]{:S(2)}) collective-permute-start(bf16[128,1024]{1,0:T(8,128)(2,1)S(1)} %get-tuple-element.64), channel_id=1, source_target_pairs={{0,1},{1,0},{2,3},{3,2},{4,5},{5,4},{6,7},{7,6},{8,9},{9,8},{10,11... | collective-permute-start | bytes 786440 | tf_op jit(solution)/shard_map/ppermute | solution.py:651
  42.9 21.5 %collective-permute-start.14 = (bf16[128,1024]{1,0:T(8,128)(2,1)S(1)}, bf16[128,1024]{1,0:T(8,128)(2,1)S(1)}, u32[]{:S(2)}, u32[]{:S(2)}) collective-permute-start(bf16[128,1024]{1,0:T(8,128)(2,1)S(1)} %get-tuple-element.65), channel_id=1, source_target_pairs={{0,2},{1,3},{2,0},{3,1},{4,6},{5,7},{6,4},{7,5},{8,10},{9,11},{10,... | collective-permute-start | bytes 786440 | tf_op jit(solution)/shard_map/ppermute | solution.py:651
  48.5 15.9 %collective-permute-start.15 = (bf16[128,1024]{1,0:T(8,128)(2,1)S(1)}, bf16[128,1024]{1,0:T(8,128)(2,1)S(1)}, u32[]{:S(2)}, u32[]{:S(2)}) collective-permute-start(bf16[128,1024]{1,0:T(8,128)(2,1)S(1)} %get-tuple-element.66), channel_id=1, source_target_pairs={{0,3},{1,2},{2,1},{3,0},{4,7},{5,6},{6,5},{7,4},{8,11},{9,10},{10,... | collective-permute-start | bytes 786440 | tf_op jit(solution)/shard_map/ppermute | solution.py:651
  60.8 12.2 %collective-permute-start.9 = (bf16[4,128,256]{2,1,0:T(8,128)(2,1)S(1)}, bf16[4,128,256]{2,1,0:T(8,128)(2,1)S(1)}, u32[]{:S(2)}, u32[]{:S(2)}) collective-permute-start(bf16[4,128,256]{2,1,0:T(8,128)(2,1)S(1)} %get-tuple-element.62), channel_id=1, source_target_pairs={{0,4},{4,0},{8,12},{12,8},{16,20},{20,16},{24,28},{28,24},{1,5},{5... | collective-permute-start | bytes 786440 | tf_op jit(solution)/shard_map/ppermute | solution.py:651
  69.4 5.2 %collective-permute-start.16 = (bf16[4,128,256]{2,1,0:T(8,128)(2,1)S(1)}, bf16[4,128,256]{2,1,0:T(8,128)(2,1)S(1)}, u32[]{:S(2)}, u32[]{:S(2)}) collective-permute-start(bf16[4,128,256]{2,1,0:T(8,128)(2,1)S(1)} %get-tuple-element.69), channel_id=1, source_target_pairs={{0,4},{4,0},{8,12},{12,8},{16,20},{20,16},{24,28},{28,24},{1,5},{5... | collective-permute-start | bytes 786440 | tf_op jit(solution)/shard_map/ppermute | solution.py:651
  69.5 9.2 %collective-permute-start.20 = (bf16[128,1024]{1,0:T(8,128)(2,1)S(1)}, bf16[128,1024]{1,0:T(8,128)(2,1)S(1)}, u32[]{:S(2)}, u32[]{:S(2)}) collective-permute-start(bf16[128,1024]{1,0:T(8,128)(2,1)S(1)} %get-tuple-element.72), channel_id=1, source_target_pairs={{0,1},{1,0},{2,3},{3,2},{4,5},{5,4},{6,7},{7,6},{8,9},{9,8},{10,11... | collective-permute-start | bytes 786440 | tf_op jit(solution)/shard_map/ppermute | solution.py:651
  71.0 14.8 %collective-permute-start.21 = (bf16[128,1024]{1,0:T(8,128)(2,1)S(1)}, bf16[128,1024]{1,0:T(8,128)(2,1)S(1)}, u32[]{:S(2)}, u32[]{:S(2)}) collective-permute-start(bf16[128,1024]{1,0:T(8,128)(2,1)S(1)} %get-tuple-element.73), channel_id=1, source_target_pairs={{0,2},{1,3},{2,0},{3,1},{4,6},{5,7},{6,4},{7,5},{8,10},{9,11},{10,... | collective-permute-start | bytes 786440 | tf_op jit(solution)/shard_map/ppermute | solution.py:651
  71.5 14.7 %collective-permute-start.22 = (bf16[128,1024]{1,0:T(8,128)(2,1)S(1)}, bf16[128,1024]{1,0:T(8,128)(2,1)S(1)}, u32[]{:S(2)}, u32[]{:S(2)}) collective-permute-start(bf16[128,1024]{1,0:T(8,128)(2,1)S(1)} %get-tuple-element.74), channel_id=1, source_target_pairs={{0,3},{1,2},{2,1},{3,0},{4,7},{5,6},{6,5},{7,4},{8,11},{9,10},{10,... | collective-permute-start | bytes 786440 | tf_op jit(solution)/shard_map/ppermute | solution.py:651
  73.0 17.0 %collective-permute-start.23 = (bf16[128,1024]{1,0:T(8,128)(2,1)S(1)}, bf16[128,1024]{1,0:T(8,128)(2,1)S(1)}, u32[]{:S(2)}, u32[]{:S(2)}) collective-permute-start(bf16[128,1024]{1,0:T(8,128)(2,1)S(1)} %get-tuple-element.76), channel_id=1, source_target_pairs={{0,1},{1,0},{2,3},{3,2},{4,5},{5,4},{6,7},{7,6},{8,9},{9,8},{10,11... | collective-permute-start | bytes 786440 | tf_op jit(solution)/shard_map/ppermute | solution.py:651
  74.6 21.6 %collective-permute-start.24 = (bf16[128,1024]{1,0:T(8,128)(2,1)S(1)}, bf16[128,1024]{1,0:T(8,128)(2,1)S(1)}, u32[]{:S(2)}, u32[]{:S(2)}) collective-permute-start(bf16[128,1024]{1,0:T(8,128)(2,1)S(1)} %get-tuple-element.77), channel_id=1, source_target_pairs={{0,2},{1,3},{2,0},{3,1},{4,6},{5,7},{6,4},{7,5},{8,10},{9,11},{10,... | collective-permute-start | bytes 786440 | tf_op jit(solution)/shard_map/ppermute | solution.py:651
  78.7 17.9 %collective-permute-start.25 = (bf16[128,1024]{1,0:T(8,128)(2,1)S(1)}, bf16[128,1024]{1,0:T(8,128)(2,1)S(1)}, u32[]{:S(2)}, u32[]{:S(2)}) collective-permute-start(bf16[128,1024]{1,0:T(8,128)(2,1)S(1)} %get-tuple-element.78), channel_id=1, source_target_pairs={{0,3},{1,2},{2,1},{3,0},{4,7},{5,6},{6,5},{7,4},{8,11},{9,10},{10,... | collective-permute-start | bytes 786440 | tf_op jit(solution)/shard_map/ppermute | solution.py:651
  85.8 19.8 %collective-permute-start.10 = (bf16[128,256]{1,0:T(8,128)(2,1)S(1)}, bf16[128,256]{1,0:T(8,128)(2,1)S(1)}, u32[]{:S(2)}, u32[]{:S(2)}) collective-permute-start(bf16[128,256]{1,0:T(8,128)(2,1)S(1)} %get-tuple-element.96), channel_id=1, source_target_pairs={{0,8},{4,12},{8,0},{12,4},{16,24},{20,28},{24,16},{28,20},{1,9},{5... | collective-permute-start | bytes 196616 | tf_op jit(solution)/shard_map/ppermute | solution.py:651
  86.2 20.7 %collective-permute-start.12 = (bf16[128,256]{1,0:T(8,128)(2,1)S(1)}, bf16[128,256]{1,0:T(8,128)(2,1)S(1)}, u32[]{:S(2)}, u32[]{:S(2)}) collective-permute-start(bf16[128,256]{1,0:T(8,128)(2,1)S(1)} %get-tuple-element.97), channel_id=1, source_target_pairs={{0,24},{4,28},{8,16},{12,20},{16,8},{20,12},{24,0},{28,4},{1,25},{... | collective-permute-start | bytes 196616 | tf_op jit(solution)/shard_map/ppermute | solution.py:651
  90.0 17.5 %collective-permute-start.11 = (bf16[128,256]{1,0:T(8,128)(2,1)S(1)}, bf16[128,256]{1,0:T(8,128)(2,1)S(1)}, u32[]{:S(2)}, u32[]{:S(2)}) collective-permute-start(bf16[128,256]{1,0:T(8,128)(2,1)S(1)} %get-tuple-element.98), channel_id=1, source_target_pairs={{0,16},{4,20},{8,24},{12,28},{16,0},{20,4},{24,8},{28,12},{1,17},{... | collective-permute-start | bytes 196616 | tf_op jit(solution)/shard_map/ppermute | solution.py:651
  96.2 11.3 %collective-permute-start.17 = (bf16[128,256]{1,0:T(8,128)(2,1)S(1)}, bf16[128,256]{1,0:T(8,128)(2,1)S(1)}, u32[]{:S(2)}, u32[]{:S(2)}) collective-permute-start(bf16[128,256]{1,0:T(8,128)(2,1)S(1)} %get-tuple-element.99), channel_id=1, source_target_pairs={{0,8},{4,12},{8,0},{12,4},{16,24},{20,28},{24,16},{28,20},{1,9},{5... | collective-permute-start | bytes 196616 | tf_op jit(solution)/shard_map/ppermute | solution.py:651
  96.7 13.8 %collective-permute-start.19 = (bf16[128,256]{1,0:T(8,128)(2,1)S(1)}, bf16[128,256]{1,0:T(8,128)(2,1)S(1)}, u32[]{:S(2)}, u32[]{:S(2)}) collective-permute-start(bf16[128,256]{1,0:T(8,128)(2,1)S(1)} %get-tuple-element.100), channel_id=1, source_target_pairs={{0,24},{4,28},{8,16},{12,20},{16,8},{20,12},{24,0},{28,4},{1,25},{... | collective-permute-start | bytes 196616 | tf_op jit(solution)/shard_map/ppermute | solution.py:651
  105.6 5.5 %collective-permute-start.18 = (bf16[128,256]{1,0:T(8,128)(2,1)S(1)}, bf16[128,256]{1,0:T(8,128)(2,1)S(1)}, u32[]{:S(2)}, u32[]{:S(2)}) collective-permute-start(bf16[128,256]{1,0:T(8,128)(2,1)S(1)} %get-tuple-element.101), channel_id=1, source_target_pairs={{0,16},{4,20},{8,24},{12,28},{16,0},{20,4},{24,8},{28,12},{1,17},{... | collective-permute-start | bytes 196616 | tf_op jit(solution)/shard_map/ppermute | solution.py:651
  106.9 9.9 %collective-permute-start.26 = (bf16[144,1024]{1,0:T(8,128)(2,1)S(1)}, bf16[144,1024]{1,0:T(8,128)(2,1)S(1)}, u32[]{:S(2)}, u32[]{:S(2)}) collective-permute-start(bf16[144,1024]{1,0:T(8,128)(2,1)S(1)} %get-tuple-element.80), channel_id=1, source_target_pairs={{0,1},{1,0},{2,3},{3,2},{4,5},{5,4},{6,7},{7,6},{8,9},{9,8},{10,11... | collective-permute-start | bytes 884744 | tf_op jit(solution)/shard_map/ppermute | solution.py:651
  107.5 16.1 %collective-permute-start.27 = (bf16[144,1024]{1,0:T(8,128)(2,1)S(1)}, bf16[144,1024]{1,0:T(8,128)(2,1)S(1)}, u32[]{:S(2)}, u32[]{:S(2)}) collective-permute-start(bf16[144,1024]{1,0:T(8,128)(2,1)S(1)} %get-tuple-element.81), channel_id=1, source_target_pairs={{0,2},{1,3},{2,0},{3,1},{4,6},{5,7},{6,4},{7,5},{8,10},{9,11},{10,... | collective-permute-start | bytes 884744 | tf_op jit(solution)/shard_map/ppermute | solution.py:651
  107.6 16.0 %collective-permute-start.28 = (bf16[144,1024]{1,0:T(8,128)(2,1)S(1)}, bf16[144,1024]{1,0:T(8,128)(2,1)S(1)}, u32[]{:S(2)}, u32[]{:S(2)}) collective-permute-start(bf16[144,1024]{1,0:T(8,128)(2,1)S(1)} %get-tuple-element.82), channel_id=1, source_target_pairs={{0,3},{1,2},{2,1},{3,0},{4,7},{5,6},{6,5},{7,4},{8,11},{9,10},{10,... | collective-permute-start | bytes 884744 | tf_op jit(solution)/shard_map/ppermute | solution.py:651
  110.5 20.3 %collective-permute-start.33 = (bf16[128,1024]{1,0:T(8,128)(2,1)S(1)}, bf16[128,1024]{1,0:T(8,128)(2,1)S(1)}, u32[]{:S(2)}, u32[]{:S(2)}) collective-permute-start(bf16[128,1024]{1,0:T(8,128)(2,1)S(1)} %get-tuple-element.86), channel_id=1, source_target_pairs={{0,1},{1,0},{2,3},{3,2},{4,5},{5,4},{6,7},{7,6},{8,9},{9,8},{10,11... | collective-permute-start | bytes 786440 | tf_op jit(solution)/shard_map/ppermute | solution.py:651
  111.1 19.8 %collective-permute-start.34 = (bf16[128,1024]{1,0:T(8,128)(2,1)S(1)}, bf16[128,1024]{1,0:T(8,128)(2,1)S(1)}, u32[]{:S(2)}, u32[]{:S(2)}) collective-permute-start(bf16[128,1024]{1,0:T(8,128)(2,1)S(1)} %get-tuple-element.87), channel_id=1, source_target_pairs={{0,2},{1,3},{2,0},{3,1},{4,6},{5,7},{6,4},{7,5},{8,10},{9,11},{10,... | collective-permute-start | bytes 786440 | tf_op jit(solution)/shard_map/ppermute | solution.py:651
  116.8 14.2 %collective-permute-start.35 = (bf16[128,1024]{1,0:T(8,128)(2,1)S(1)}, bf16[128,1024]{1,0:T(8,128)(2,1)S(1)}, u32[]{:S(2)}, u32[]{:S(2)}) collective-permute-start(bf16[128,1024]{1,0:T(8,128)(2,1)S(1)} %get-tuple-element.88), channel_id=1, source_target_pairs={{0,3},{1,2},{2,1},{3,0},{4,7},{5,6},{6,5},{7,4},{8,11},{9,10},{10,... | collective-permute-start | bytes 786440 | tf_op jit(solution)/shard_map/ppermute | solution.py:651
  130.7 7.7 %collective-permute-start.29 = (bf16[4,128,256]{2,1,0:T(8,128)(2,1)S(1)}, bf16[4,128,256]{2,1,0:T(8,128)(2,1)S(1)}, u32[]{:S(2)}, u32[]{:S(2)}) collective-permute-start(bf16[4,128,256]{2,1,0:T(8,128)(2,1)S(1)} %get-tuple-element.84), channel_id=1, source_target_pairs={{0,4},{4,0},{8,12},{12,8},{16,20},{20,16},{24,28},{28,24},{1,5},{5... | collective-permute-start | bytes 786440 | tf_op jit(solution)/shard_map/ppermute | solution.py:651
  137.9 4.9 %collective-permute-start.36 = (bf16[4,128,256]{2,1,0:T(8,128)(2,1)S(1)}, bf16[4,128,256]{2,1,0:T(8,128)(2,1)S(1)}, u32[]{:S(2)}, u32[]{:S(2)}) collective-permute-start(bf16[4,128,256]{2,1,0:T(8,128)(2,1)S(1)} %get-tuple-element.92), channel_id=1, source_target_pairs={{0,4},{4,0},{8,12},{12,8},{16,20},{20,16},{24,28},{28,24},{1,5},{5... | collective-permute-start | bytes 786440 | tf_op jit(solution)/shard_map/ppermute | solution.py:651
  138.4 7.0 %collective-permute-start.30 = (bf16[128,256]{1,0:T(8,128)(2,1)S(1)}, bf16[128,256]{1,0:T(8,128)(2,1)S(1)}, u32[]{:S(2)}, u32[]{:S(2)}) collective-permute-start(bf16[128,256]{1,0:T(8,128)(2,1)S(1)} %get-tuple-element.102), channel_id=1, source_target_pairs={{0,8},{4,12},{8,0},{12,4},{16,24},{20,28},{24,16},{28,20},{1,9},{5... | collective-permute-start | bytes 196616 | tf_op jit(solution)/shard_map/ppermute | solution.py:651
  139.7 7.7 %collective-permute-start.32 = (bf16[128,256]{1,0:T(8,128)(2,1)S(1)}, bf16[128,256]{1,0:T(8,128)(2,1)S(1)}, u32[]{:S(2)}, u32[]{:S(2)}) collective-permute-start(bf16[128,256]{1,0:T(8,128)(2,1)S(1)} %get-tuple-element.103), channel_id=1, source_target_pairs={{0,24},{4,28},{8,16},{12,20},{16,8},{20,12},{24,0},{28,4},{1,25},{... | collective-permute-start | bytes 196616 | tf_op jit(solution)/shard_map/ppermute | solution.py:651
  140.9 7.1 %collective-permute-start.31 = (bf16[128,256]{1,0:T(8,128)(2,1)S(1)}, bf16[128,256]{1,0:T(8,128)(2,1)S(1)}, u32[]{:S(2)}, u32[]{:S(2)}) collective-permute-start(bf16[128,256]{1,0:T(8,128)(2,1)S(1)} %get-tuple-element.104), channel_id=1, source_target_pairs={{0,16},{4,20},{8,24},{12,28},{16,0},{20,4},{24,8},{28,12},{1,17},{... | collective-permute-start | bytes 196616 | tf_op jit(solution)/shard_map/ppermute | solution.py:651
  143.0 6.4 %collective-permute-start.37 = (bf16[128,256]{1,0:T(8,128)(2,1)S(1)}, bf16[128,256]{1,0:T(8,128)(2,1)S(1)}, u32[]{:S(2)}, u32[]{:S(2)}) collective-permute-start(bf16[128,256]{1,0:T(8,128)(2,1)S(1)} %get-tuple-element.105), channel_id=1, source_target_pairs={{0,8},{4,12},{8,0},{12,4},{16,24},{20,28},{24,16},{28,20},{1,9},{5... | collective-permute-start | bytes 196616 | tf_op jit(solution)/shard_map/ppermute | solution.py:651
  143.9 9.4 %collective-permute-start.39 = (bf16[128,256]{1,0:T(8,128)(2,1)S(1)}, bf16[128,256]{1,0:T(8,128)(2,1)S(1)}, u32[]{:S(2)}, u32[]{:S(2)}) collective-permute-start(bf16[128,256]{1,0:T(8,128)(2,1)S(1)} %get-tuple-element.106), channel_id=1, source_target_pairs={{0,24},{4,28},{8,16},{12,20},{16,8},{20,12},{24,0},{28,4},{1,25},{... | collective-permute-start | bytes 196616 | tf_op jit(solution)/shard_map/ppermute | solution.py:651
  145.5 7.8 %collective-permute-start.38 = (bf16[128,256]{1,0:T(8,128)(2,1)S(1)}, bf16[128,256]{1,0:T(8,128)(2,1)S(1)}, u32[]{:S(2)}, u32[]{:S(2)}) collective-permute-start(bf16[128,256]{1,0:T(8,128)(2,1)S(1)} %get-tuple-element.107), channel_id=1, source_target_pairs={{0,16},{4,20},{8,24},{12,28},{16,0},{20,4},{24,8},{28,12},{1,17},{... | collective-permute-start | bytes 196616 | tf_op jit(solution)/shard_map/ppermute | solution.py:651
  153.5 1.2 collective-permute-start.40
  154.7 5.1 %collective-permute-start.43 = (f32[2]{0:T(128)S(1)}, f32[2]{0:T(128)S(1)}, u32[]{:S(2)}, u32[]{:S(2)}) collective-permute-start(f32[2]{0:T(128)S(1)} %add.94), channel_id=1, source_target_pairs={{0,24},{4,28},{8,16},{12,20},{16,8},{20,12},{24,0},{28,4},{1,25},{... | collective-permute-start | bytes 32 | tf_op jit(solution)/shard_map/ppermute | solution.py:651
  155.9 5.4 %collective-permute-start.42 = (f32[2]{0:T(128)S(1)}, f32[2]{0:T(128)S(1)}, u32[]{:S(2)}, u32[]{:S(2)}) collective-permute-start(f32[2]{0:T(128)S(1)} %add.94), channel_id=1, source_target_pairs={{0,16},{4,20},{8,24},{12,28},{16,0},{20,4},{24,8},{28,12},{1,17},{... | collective-permute-start | bytes 32 | tf_op jit(solution)/shard_map/ppermute | solution.py:651
  159.8 3.6 %collective-permute-start.41 = (f32[2]{0:T(128)S(1)}, f32[2]{0:T(128)S(1)}, u32[]{:S(2)}, u32[]{:S(2)}) collective-permute-start(f32[2]{0:T(128)S(1)} %add.94), channel_id=1, source_target_pairs={{0,8},{4,12},{8,0},{12,4},{16,24},{20,28},{24,16},{28,20},{1,9},{5... | collective-permute-start | bytes 32 | tf_op jit(solution)/shard_map/ppermute | solution.py:651
  163.4 4.5 %collective-permute-start.46 = (f32[2]{0:T(128)S(1)}, f32[2]{0:T(128)S(1)}, u32[]{:S(2)}, u32[]{:S(2)}) collective-permute-start(f32[2]{0:T(128)S(1)} %add_add_fusion), channel_id=1, source_target_pairs={{0,3},{1,2},{2,1},{3,0},{4,7},{5,6},{6,5},{7,4},{8,11},{9,10},{10,... | collective-permute-start | bytes 32 | tf_op jit(solution)/shard_map/ppermute | solution.py:651
  164.9 3.6 %collective-permute-start.45 = (f32[2]{0:T(128)S(1)}, f32[2]{0:T(128)S(1)}, u32[]{:S(2)}, u32[]{:S(2)}) collective-permute-start(f32[2]{0:T(128)S(1)} %add_add_fusion), channel_id=1, source_target_pairs={{0,2},{1,3},{2,0},{3,1},{4,6},{5,7},{6,4},{7,5},{8,10},{9,11},{10,... | collective-permute-start | bytes 32 | tf_op jit(solution)/shard_map/ppermute | solution.py:651
  166.1 3.6 %collective-permute-start.44 = (f32[2]{0:T(128)S(1)}, f32[2]{0:T(128)S(1)}, u32[]{:S(2)}, u32[]{:S(2)}) collective-permute-start(f32[2]{0:T(128)S(1)} %add_add_fusion), channel_id=1, source_target_pairs={{0,1},{1,0},{2,3},{3,2},{4,5},{5,4},{6,7},{7,6},{8,9},{9,8},{10,11... | collective-permute-start | bytes 32 | tf_op jit(solution)/shard_map/ppermute | solution.py:651
  (11 other events, 160.5 us)

commit v2 on v1

--- a/solution.py
+++ b/solution.py
@@ -8,6 +8,7 @@
 from jax.experimental import pallas as pl
 from jax.experimental.pallas import tpu as pltpu
 from jax.sharding import PartitionSpec as P
+
 
 DEPTHS = 2
 epsilon = 1e-06
@@ -88,6 +89,7 @@
 def dot(left, right):
     return jnp.dot(left, right, preferred_element_type=F32)
 
+
 ANY = pl.BlockSpec(memory_space=pltpu.HBM)
 SMEM = pl.BlockSpec(memory_space=pltpu.SMEM)
 FULL = pl.BlockSpec(memory_space=pltpu.VMEM)
@@ -97,8 +99,8 @@
     return pl.CostEstimate(flops=flops, bytes_accessed=moved, transcendentals=0)
 
 
-def params():
-    return pltpu.CompilerParams(vmem_limit_bytes=VMEM_LIMIT)
+def params(limit=VMEM_LIMIT):
+    return pltpu.CompilerParams(vmem_limit_bytes=limit)
 
 
 def forward_lanes(load, rows, blocks, lane, twist_ref, left_ref, base=0):
@@ -131,8 +133,21 @@
     return [part[place * rows : (place + 1) * rows] for place in range(per_device)]
 
 
-def first_kernel(me_ref, field_hbm, twist_ref, table_ref, *refs, lane, per_device, chunk, parts):
-    outs, (field_ref, left_ref, sem) = refs[:-3], refs[-3:]
+def store_slots(outs, left_ref, table_ref, me, per_device, lane):
+    pair = 2 * lane
+    span = outs[0].shape[1] // pair
+    devices = len(outs) * span // per_device
+    for slot in range(devices):
+        made = slot_products(left_ref, table_ref, me, slot, per_device)
+        for place, part in enumerate(made):
+            target = outs[place // span * devices + slot]
+            target[:, place % span * pair : (place % span + 1) * pair] = part
+
+
+def first_kernel(*refs, lane, per_device, chunk, parts):
+    me_ref, field_hbm, twist_hbm, table_hbm, _ = refs[:5]
+    outs = refs[5:-5]
+    field_ref, left_ref, twist_ref, table_ref, sem = refs[-5:]
     rows, width = field_ref.shape[1], field_ref.shape[2]
     tile = rows // parts
     arriving = [
@@ -143,8 +158,13 @@
         )
         for t in range(parts)
     ]
+    twist_in = pltpu.make_async_copy(twist_hbm, twist_ref, sem.at[parts])
+    table_in = pltpu.make_async_copy(table_hbm, table_ref, sem.at[parts + 1])
+    twist_in.start()
     for copy in arriving:
         copy.start()
+    table_in.start()
+    twist_in.wait()
     for t in range(parts):
         arriving[t].wait()
 
@@ -152,35 +172,36 @@
             return field_ref[part, pl.ds(at.start + t * tile, at.size), b * lane : (b + 1) * lane]
 
         forward_lanes(load, tile, width // lane, lane, twist_ref, left_ref, t * tile)
-    for slot, out_ref in enumerate(outs):
-        made = slot_products(left_ref, table_ref, me_ref[0], slot, per_device)
-        for place, part in enumerate(made):
-            out_ref[:, place * 2 * lane : (place + 1) * 2 * lane] = part
-
-
-def forward_x(me, field, tables, lane, devices, chunk, chunks):
+    table_in.wait()
+    store_slots(outs, left_ref, table_ref, me_ref[0], per_device, lane)
+
+
+def forward_x(me, field, tables, lane, devices, chunk, chunks, pieces, after):
     _, rows, width = field.shape
     blocks = width // lane
     per_device = blocks // devices
     rows = rows // chunks
     parts = max(rows // 32, 1)
-    wide = per_device * 2 * lane
-    return pl.pallas_call(
+    shape = jax.ShapeDtypeStruct((rows, per_device * 2 * lane // pieces), BF16)
+    made = pl.pallas_call(
         functools.partial(
             first_kernel, lane=lane, per_device=per_device, chunk=chunk, parts=parts
         ),
-        in_specs=[SMEM, ANY, FULL, FULL],
-        out_specs=[FULL] * devices,
-        out_shape=[jax.ShapeDtypeStruct((rows, wide), BF16)] * devices,
+        in_specs=[SMEM, ANY, ANY, ANY, pl.BlockSpec(memory_space=pl.ANY)],
+        out_specs=[FULL] * (devices * pieces),
+        out_shape=[shape] * (devices * pieces),
         scratch_shapes=[
             pltpu.VMEM((2, rows, width), F32),
             pltpu.VMEM((blocks, rows, 2 * lane), BF16),
-            pltpu.SemaphoreType.DMA((parts,)),
+            pltpu.VMEM(tables[2].shape, F32),
+            pltpu.VMEM(tables[0].shape, BF16),
+            pltpu.SemaphoreType.DMA((parts + 2,)),
         ],
-        compiler_params=params(),
+        compiler_params=params(60 * 1024 * 1024),
         cost_estimate=cost(rows * width * 4000, rows * width * 12),
         name="forward_x",
-    )(me, field, tables[2], tables[0])
+    )(me, field, tables[2], tables[0], after)
+    return [made[p * devices : (p + 1) * devices] for p in range(pieces)]
 
 
 def poly(coefficients, t):
@@ -216,7 +237,9 @@
 
 def wave_kernel(me_ref, squared_ref, after_ref, *u_refs, lane, width, height, columns, limit):
     me = me_ref[0]
-    depths = len(u_refs)
+    depths = squared_ref.shape[0]
+    parts = len(u_refs) // depths
+    span = columns // parts
     count = height // lane
     blocks = width // lane
     sub = 8
@@ -235,83 +258,131 @@
         ]
         for c in range(columns):
             kx2 = kappa_squared(blocks * col + me * columns + c, width)
-            here = slice(c * lane, (c + 1) * lane)
+            here = slice(c % span * lane, (c % span + 1) * lane)
             for k in range(count // 2 + 1):
                 for depth in range(depths):
                     real, imag = propagator((squared_ref[depth] - ky2[k]) - kx2, limit)
-                    u_refs[depth][k, pl.ds(at, sub), here] = real
-                    u_refs[depth][k, pl.ds(lane + at, sub), here] = imag
+                    u_refs[depth * parts + c // span][k, pl.ds(at, sub), here] = real
+                    u_refs[depth * parts + c // span][k, pl.ds(lane + at, sub), here] = imag
         return carry
 
     lax.fori_loop(0, lane // sub, wave_body, 0)
 
 
-def waves(me, squared, after, lane, width, height, columns, limit):
-    shape = (height // lane // 2 + 1, 2 * lane, columns * lane)
+def waves(me, squared, after, lane, width, height, columns, limit, parts):
+    shape = (height // lane // 2 + 1, 2 * lane, columns * lane // parts)
+    many = squared.shape[0] * parts
     return pl.pallas_call(
         functools.partial(
             wave_kernel, lane=lane, width=width, height=height, columns=columns, limit=limit
         ),
-        in_specs=[SMEM, SMEM, ANY],
-        out_specs=[FULL] * squared.shape[0],
-        out_shape=[jax.ShapeDtypeStruct(shape, F32)] * squared.shape[0],
+        in_specs=[SMEM, SMEM, pl.BlockSpec(memory_space=pl.ANY)],
+        out_specs=[FULL] * many,
+        out_shape=[jax.ShapeDtypeStruct(shape, F32)] * many,
         compiler_params=params(),
         cost_estimate=cost(height * columns * lane * 8000, height * columns * lane * 16),
         name="waves",
     )(me, squared, after)
 
 
-def spectral_kernel(*refs, lane, width, rows, devices, chunks):
+def xor_permute(values, me):
+    values = list(values)
+    bit = 1
+    while bit < len(values):
+        taken = lax.bitwise_and(me, jnp.int32(bit)) != 0
+        values = [jnp.where(taken, values[k ^ bit], values[k]) for k in range(len(values))]
+        bit *= 2
+    return values
+
+
+def spectral_kernel(*refs, lane, width, devices, chunks, part, parts, tiled):
     me_ref, u_ref, forward_ref, inverse_ref = refs[:4]
-    ins = refs[4 : 4 + chunks * devices]
-    outs = refs[4 + chunks * devices : 4 + 2 * chunks * devices]
-    (
-        in_ref, out_ref, edge_ref, x_ref, z_ref, w_ref, in_sem, out_sem, edge_sem,
-    ) = refs[4 + 2 * chunks * devices :]
+    refs = refs[4:]
+    total_in = chunks * devices
+    ins = [refs[h * devices : (h + 1) * devices] for h in range(chunks)]
+    refs = refs[total_in:]
+    joins = part == parts - 1 and parts > 1
+    if joins:
+        priors, refs = refs[:devices], refs[devices:]
+    outs = [refs[h * devices : (h + 1) * devices] for h in range(chunks)]
+    refs = refs[total_in:]
+    x_ref, z_ref, w_ref = refs[:3]
     me = me_ref[0]
+    part_rows = ins[0][0].shape[0]
+    rows = part_rows * chunks
     height = devices * rows
-    part_rows = rows // chunks
     count = height // lane
-    blocks = width // lane
-    columns = blocks // devices
+    pair = 2 * lane
+    columns = outs[0][0].shape[1] // pair
     sub = 16
-    pair = 2 * lane
-
-    def place_of(slot, h):
-        start = lax.bitwise_xor(me, slot) * rows + h * part_rows
-        return pl.multiple_of(start, 16)
-
-    def copies(c):
-        made = []
+    span = columns * pair
+    in_base = [part * span] + [0] * (chunks - 1)
+    out_base = [0] + [part * span if joins else 0] * (chunks - 1)
+    if not tiled:
+        in_ref, out_ref, in_sem, out_sem = refs[3:]
+
+        def place_of(slot, h):
+            start = lax.bitwise_xor(me, slot) * rows + h * part_rows
+            return pl.multiple_of(start, 16)
+
+        def moves(h, slot, inward):
+            near = (in_ref if inward else out_ref).at[pl.ds(place_of(slot, h), part_rows), :]
+            if inward:
+                far = ins[h][slot].at[:, pl.ds(in_base[h], span)]
+                return pltpu.make_async_copy(far, near, in_sem.at[h, slot])
+            far = outs[h][slot].at[pl.ds(0, part_rows), pl.ds(out_base[h], span)]
+            return pltpu.make_async_copy(near, far, out_sem.at[h, slot])
+
+        arriving = [moves(h, k, True) for h in range(chunks) for k in range(devices)]
+        for copy in arriving:
+            copy.start()
+        for copy in arriving:
+            copy.wait()
+    per_chunk = part_rows // lane
+
+    def fetch(at, base):
+        if not tiled:
+            return [
+                in_ref[pl.ds(pl.multiple_of(at + b * lane, sub), sub), base : base + pair]
+                for b in range(count)
+            ]
+        found = [None] * count
         for h in range(chunks):
-            for slot in range(devices):
-                made.append(
-                    pltpu.make_async_copy(
-                        ins[h * devices + slot].at[:, pl.ds(c * pair, pair)],
-                        in_ref.at[c, pl.ds(place_of(slot, h), part_rows), :],
-                        in_sem.at[c, h, slot],
-                    )
+            lanes = slice(in_base[h] + base, in_base[h] + base + pair)
+            for t in range(per_chunk):
+                got = xor_permute(
+                    [ref[pl.ds(pl.multiple_of(at + t * lane, sub), sub), lanes] for ref in ins[h]],
+                    me,
                 )
-        return made
-
-    arriving = [copies(c) for c in range(columns)]
-    for group in arriving:
-        for copy in group:
-            copy.start()
+                for slab in range(devices):
+                    found[(slab * chunks + h) * per_chunk + t] = got[slab]
+        return found
+
+    def leave(at, base, values):
+        if not tiled:
+            for b in range(count):
+                row = pl.multiple_of(at + b * lane, sub)
+                out_ref[pl.ds(row, sub), base : base + pair] = values[b]
+            return
+        for h in range(chunks):
+            lanes = slice(out_base[h] + base, out_base[h] + base + pair)
+            for t in range(per_chunk):
+                got = xor_permute(
+                    [values[(slab * chunks + h) * per_chunk + t] for slab in range(devices)], me
+                )
+                for slot in range(devices):
+                    row = pl.multiple_of(at + t * lane, sub)
+                    outs[h][slot][pl.ds(row, sub), lanes] = got[slot]
 
     for c in range(columns):
-        for copy in arriving[c]:
-            copy.wait()
         here = slice(c * lane, (c + 1) * lane)
 
         def load_body(i, carry, c=c, here=here):
             at = pl.multiple_of(i * sub, sub)
-            real, imag = [], []
-            for b in range(count):
-                row = pl.multiple_of(at + b * lane, sub)
-                real.append(in_ref[c, pl.ds(row, sub), 0:lane].astype(F32))
-                imag.append(in_ref[c, pl.ds(row, sub), lane:pair].astype(F32))
-            real, imag = small_dft(real, imag, -1)
+            tiles = [tile.astype(F32) for tile in fetch(at, c * pair)]
+            real, imag = small_dft(
+                [tile[:, :lane] for tile in tiles], [tile[:, lane:] for tile in tiles], -1
+            )
             for k in range(count):
                 x_ref[k, pl.ds(at, sub), here] = real[k].astype(BF16)
                 x_ref[k, pl.ds(lane + at, sub), here] = imag[k].astype(BF16)
@@ -329,8 +400,6 @@
     for k in range(count):
         w_ref[k] = dot(inverse_ref[k], z_ref[k])
 
-    leaving = []
-    edge = lax.broadcasted_iota(jnp.int32, (EXTRA, pair), 0)
     for c in range(columns):
         here = slice(c * lane, (c + 1) * lane)
 
@@ -339,100 +408,97 @@
             real = [w_ref[k, pl.ds(at, sub), here] for k in range(count)]
             imag = [w_ref[k, pl.ds(lane + at, sub), here] for k in range(count)]
             real, imag = small_dft(real, imag, 1)
-            for b in range(count):
-                row = pl.multiple_of(at + b * lane, sub)
-                out_ref[c, pl.ds(row, sub), 0:lane] = real[b].astype(BF16)
-                out_ref[c, pl.ds(row, sub), lane:pair] = imag[b].astype(BF16)
+            leave(
+                at,
+                c * pair,
+                [
+                    jnp.concatenate([re.astype(BF16), im.astype(BF16)], axis=1)
+                    for re, im in zip(real, imag)
+                ],
+            )
             return carry
 
         lax.fori_loop(0, lane // sub, store_body, 0)
-
-        def place(tile, row, source):
-            return jnp.where(edge == row, jnp.broadcast_to(source.astype(F32), edge.shape), tile)
-
-        for slab in range(devices):
-            tile = jnp.zeros(edge.shape, F32)
-            start = slab * rows
-            after = out_ref[c, start + part_rows : start + part_rows + EXTRA, :].astype(F32)
-            tile = place(tile, 0, after[0:1])
-            if slab + 1 < devices:
-                after = out_ref[c, start + rows : start + rows + EXTRA, :].astype(F32)
-                tile = place(tile, 8, after[0:1])
-            if slab:
-                before = out_ref[c, start - EXTRA : start, :].astype(F32)
-                tile = place(tile, EXTRA - 1, before[EXTRA - 1 :])
-            edge_ref[c, slab] = tile.astype(BF16)
-        for h in range(chunks):
-            for slot in range(devices):
-                target = outs[h * devices + slot]
-                owner = lax.bitwise_xor(me, slot)
-                leaving.append(
-                    pltpu.make_async_copy(
-                        out_ref.at[c, pl.ds(place_of(slot, h), part_rows), :],
-                        target.at[pl.ds(0, part_rows), pl.ds(c * pair, pair)],
-                        out_sem.at[c, h, slot],
-                    )
-                )
-                leaving[-1].start()
-                if h == 0:
-                    leaving.append(
-                        pltpu.make_async_copy(
-                            edge_ref.at[c, owner],
-                            target.at[pl.ds(part_rows, EXTRA), pl.ds(c * pair, pair)],
-                            edge_sem.at[c, slot],
-                        )
-                    )
-                    leaving[-1].start()
-    for copy in leaving:
-        copy.wait()
-
-
-def spectral(me, waves, pieces, tables, lane, width):
+    if joins:
+        for slot in range(devices):
+            for h in range(1, chunks):
+                outs[h][slot][:, 0 : part * span] = priors[slot][...]
+    if not tiled:
+        leaving = [moves(h, k, False) for h in range(chunks) for k in range(devices)]
+        for copy in leaving:
+            copy.start()
+        for copy in leaving:
+            copy.wait()
+
+    edge = lax.broadcasted_iota(jnp.int32, (EXTRA, span), 0)
+    tail = slice(out_base[-1], out_base[-1] + span)
+    starts = [outs[0][k][0:EXTRA, :].astype(F32)[0:1] for k in range(devices)]
+    ends = [
+        outs[-1][k][part_rows - EXTRA : part_rows, tail].astype(F32)[EXTRA - 1 :]
+        for k in range(devices)
+    ]
+    zero = [jnp.zeros((1, span), F32)]
+    nexts = xor_permute(xor_permute(starts, me)[1:] + zero, me)
+    lasts = xor_permute(zero + xor_permute(ends, me)[:-1], me)
+    for k in range(devices):
+        after = outs[1][k][0:EXTRA, out_base[1] : out_base[1] + span].astype(F32)[0:1]
+        tile = jnp.zeros(edge.shape, F32)
+        for row, value in ((0, after), (8, nexts[k]), (EXTRA - 1, lasts[k])):
+            tile = jnp.where(edge == row, jnp.broadcast_to(value, edge.shape), tile)
+        outs[0][k][part_rows : part_rows + EXTRA, :] = tile.astype(BF16)
+
+
+def spectral(me, waves, pieces, priors, tables, lane, width, part, parts):
     chunks, devices = len(pieces), len(pieces[0])
     part_rows, wide = pieces[0][0].shape
     rows = part_rows * chunks
-    columns = wide // (2 * lane)
+    span = wide // parts
+    columns = span // (2 * lane)
     height = devices * rows
     count = height // lane
+    tiled = part_rows % lane == 0
+    joins = part == parts - 1 and parts > 1
     shapes = []
     for h in range(chunks):
-        extra = EXTRA if h == 0 else 0
-        shapes += [jax.ShapeDtypeStruct((part_rows + extra, wide), BF16)] * devices
+        shape = (part_rows, wide if joins else span) if h else (part_rows + EXTRA, span)
+        shapes += [jax.ShapeDtypeStruct(shape, BF16)] * devices
+    operands = [piece for group in pieces for piece in group]
+    if joins:
+        operands += priors
+    scratch = [
+        pltpu.VMEM((count, 2 * lane, columns * lane), BF16),
+        pltpu.VMEM((count, 2 * lane, columns * lane), BF16),
+        pltpu.VMEM((count, 2 * lane, columns * lane), F32),
+    ]
+    if not tiled:
+        scratch += [pltpu.VMEM((height, span), BF16)] * 2
+        scratch += [pltpu.SemaphoreType.DMA((chunks, devices))] * 2
     sent = pl.pallas_call(
         functools.partial(
-            spectral_kernel, lane=lane, width=width, rows=rows, devices=devices, chunks=chunks
+            spectral_kernel, lane=lane, width=width, devices=devices, chunks=chunks, part=part,
+            parts=parts, tiled=tiled,
         ),
-        in_specs=[SMEM, FULL, FULL, FULL] + [FULL] * (chunks * devices),
+        in_specs=[SMEM, FULL, FULL, FULL] + [FULL] * len(operands),
         out_specs=[FULL] * (chunks * devices),
         out_shape=shapes,
-        scratch_shapes=[
-            pltpu.VMEM((columns, height, 2 * lane), BF16),
-            pltpu.VMEM((columns, height, 2 * lane), BF16),
-            pltpu.VMEM((columns, devices, EXTRA, 2 * lane), BF16),
-            pltpu.VMEM((count, 2 * lane, columns * lane), BF16),
-            pltpu.VMEM((count, 2 * lane, columns * lane), BF16),
-            pltpu.VMEM((count, 2 * lane, columns * lane), F32),
-            pltpu.SemaphoreType.DMA((columns, chunks, devices)),
-            pltpu.SemaphoreType.DMA((columns, chunks, devices)),
-            pltpu.SemaphoreType.DMA((columns, devices)),
-        ],
+        scratch_shapes=scratch,
         compiler_params=params(),
         cost_estimate=cost(height * columns * lane * 8000, height * columns * lane * 16),
         name="spectral",
-    )(me, waves, *tables, *[piece for part in pieces for piece in part])
+    )(me, waves, *tables, *operands)
     return [sent[h * devices : (h + 1) * devices] for h in range(chunks)]
 
 
-def space_kernel(*refs, lane, devices, chunk, first, last):
+def space_kernel(*refs, lane, devices, groups_in, groups_out, chunk, first, last):
     me_ref, factor_ref, coef_hbm, block_hbm, twist_ref, inverse_ref, forward_ref = refs[:7]
-    ins = refs[7 : 7 + devices]
-    at = 7 + devices
+    ins = refs[7 : 7 + groups_in * devices]
+    at = 7 + groups_in * devices
     if not first:
         carried_ref = refs[at]
         at += 1
     if last and not first:
         at += 1
-    outs = refs[at : at + (1 if last else devices)]
+    outs = refs[at : at + (1 if last else groups_out * devices)]
     at += len(outs)
     kept_ref, sent_ref = refs[at : at + 2]
     at += 2
@@ -444,7 +510,8 @@
     ) = refs[at:]
     me = me_ref[0]
     padded, wide = ins[0].shape
-    per_device = wide // (2 * lane)
+    span = wide // (2 * lane)
+    per_device = span * groups_in
     rows, width = coef_ref.shape
     blocks = width // lane
     pair = 2 * lane
@@ -457,7 +524,12 @@
 
     for slot in range(devices):
         left = jnp.concatenate(
-            [ins[slot][:, place * pair : (place + 1) * pair] for place in range(per_device)],
+            [
+                ins[place // span * devices + slot][
+                    :, place % span * pair : (place % span + 1) * pair
+                ]
+                for place in range(per_device)
+            ],
             axis=0,
         )
         owner = lax.bitwise_xor(me, slot)
@@ -579,18 +651,17 @@
             return p_ref[part, at, b * lane : (b + 1) * lane]
 
         forward_lanes(load, rows, blocks, lane, twist_ref, left_ref)
-        for slot in range(devices):
-            parts = slot_products(left_ref, forward_ref, me, slot, per_device)
-            for place, part in enumerate(parts):
-                outs[slot][:, place * pair : (place + 1) * pair] = part
+        store_slots(outs, left_ref, forward_ref, me, per_device, lane)
     for copy in leaving:
         copy.wait()
 
 
-def space(me, pieces, coefficient, factor, inverse_blocks, tables, lane, chunk, carried, field,
-          last):
-    devices = len(pieces)
+def space(me, groups_in, coefficient, factor, inverse_blocks, tables, lane, chunk, carried,
+          field, last, groups_out):
+    devices = len(groups_in[0])
+    pieces = [piece for group in groups_in for piece in group]
     padded, wide = pieces[0].shape
+    wide = wide * len(groups_in)
     first = chunk == 0
     rows = padded - EXTRA if first else padded
     all_rows, width = coefficient.shape
@@ -598,7 +669,8 @@
     if last:
         shapes = [jax.ShapeDtypeStruct((2, all_rows, width), F32)]
     else:
-        shapes = [jax.ShapeDtypeStruct((rows, wide), BF16)] * devices
+        shape = jax.ShapeDtypeStruct((rows, wide // groups_out), BF16)
+        shapes = [shape] * (devices * groups_out)
     specs = [ANY if last else FULL] * len(shapes)
     groups = lax.axis_size("freq")
     half = jax.ShapeDtypeStruct((groups // 2, rows, width // groups), BF16)
@@ -608,7 +680,7 @@
         shapes = shapes + [jax.ShapeDtypeStruct((2, 16, width), F32)]
         specs = specs + [FULL]
     operands = [me, factor, coefficient, inverse_blocks, tables[2], tables[1], tables[0], *pieces]
-    in_specs = [SMEM, SMEM, ANY, ANY, FULL, FULL, FULL] + [FULL] * devices
+    in_specs = [SMEM, SMEM, ANY, ANY, FULL, FULL, FULL] + [FULL] * len(pieces)
     aliases = {}
     if not first:
         operands.append(carried)
@@ -619,7 +691,8 @@
             in_specs.append(ANY)
     got = pl.pallas_call(
         functools.partial(
-            space_kernel, lane=lane, devices=devices, chunk=chunk, first=first, last=last
+            space_kernel, lane=lane, devices=devices, groups_in=len(groups_in),
+            groups_out=groups_out, chunk=chunk, first=first, last=last,
         ),
         in_specs=in_specs,
         out_specs=specs,
@@ -643,7 +716,9 @@
     carry = got.pop() if first else None
     sent, kept = got.pop(), got.pop()
     image = (kept, sent)
-    return (got[0] if last else got), image, carry
+    if last:
+        return got[0], image, carry
+    return [got[p * devices : (p + 1) * devices] for p in range(groups_out)], image, carry
 
 
 def swap(value, axis, distance):
@@ -659,12 +734,14 @@
     return value + sum(swap(value, axis, distance) for distance in distances)
 
 
-def collect(image):
-    kept, sent = image
-    joined = (kept.astype(F32) + swap(sent, "freq", 1).astype(F32)).astype(BF16)
-    parts = [joined[0]]
-    for j in range(1, joined.shape[0]):
-        parts.append(swap(joined[j], "freq", 2 * j))
+def collect(images):
+    joined = []
+    for kept, sent in images:
+        other = swap(sent, "freq", 1)
+        joined.append((kept.astype(F32) + other.astype(F32)).astype(BF16))
+    parts = [jnp.concatenate([join[j] for join in joined]) for j in range(joined[0].shape[0])]
+    for j in range(1, len(parts)):
+        parts[j] = swap(parts[j], "freq", 2 * j)
     return sum(part.astype(F32) for part in parts)
 
 
@@ -678,7 +755,6 @@
 def shards(wavefield, block_inverse, coefficient, correction_factor, frequencies, slowness):
     freq_local, rows_local, width = wavefield.shape[1:]
     devices = lax.axis_size("rows")
-    groups = lax.axis_size("freq")
     height = rows_local * devices
     lane = block_inverse.shape[-1]
     chunks = 2
@@ -689,31 +765,47 @@
     me = jnp.stack([lax.axis_index("rows"), place % 2, place // 2]).astype(jnp.int32)
     partials = [[None] * chunks for _ in range(DEPTHS)]
     columns = width // lane // devices
+    parts = 2 if columns % 2 == 0 else 1
     fields = []
     for f in range(freq_local):
         factor = correction_factor[:, f]
-        made = [
-            forward_x(me, wavefield[:, f], x_tables, lane, devices, h, chunks)
-            for h in range(chunks)
-        ]
+        made, behind = [], me
+        for h in range(chunks):
+            made.append(
+                forward_x(
+                    me, wavefield[:, f], x_tables, lane, devices, h, chunks, parts if h else 1,
+                    behind,
+                )
+            )
+            behind = made[-1][0][0]
         squared = (frequencies[f] * slowness) ** 2
-        table = waves(me, squared, made[-1][0], lane, width, height, columns, limit)
-        pieces = [exchange(part) for part in made]
+        table = waves(
+            me, squared, made[-1][0][0], lane, width, height, columns, limit, parts
+        )
+        arrived = [[exchange(group) for group in groups] for groups in made]
         for depth_step in range(DEPTHS):
             last = depth_step == DEPTHS - 1
-            sent = spectral(me, table[depth_step], pieces, y_tables, lane, width)
-            arrived = [exchange(part) for part in sent]
-            pieces, carry, field = [], None, None
+            leaving, priors = [[], []], None
+            for p in range(parts):
+                sent = spectral(
+                    me, table[depth_step * parts + p], [arrived[0][0], arrived[1][p]],
+                    priors, y_tables, lane, width, p, parts,
+                )
+                leaving[0].append(exchange(sent[0]))
+                priors = sent[1]
+            leaving[1].append(exchange(priors))
+            arrived, carry, field = [], None, None
             for h in range(chunks):
+                groups_out = parts if h else 1
                 made, image, carried = space(
-                    me, arrived[h], coefficient, factor, block_inverse[:, f], x_tables, lane, h,
-                    carry, field, last,
+                    me, leaving[h], coefficient, factor, block_inverse[:, f], x_tables, lane,
+                    h, carry, field, last, groups_out,
                 )
                 carry = carry if carried is None else carried
                 if last:
                     field = made
                 else:
-                    pieces.append(exchange(made))
+                    arrived.append([exchange(group) for group in made])
                 before = partials[depth_step][h]
                 if before is not None:
                     image = [
@@ -722,9 +814,13 @@
                     ]
                 partials[depth_step][h] = image
         fields.append(field)
-    shares = jnp.stack(
-        [jnp.concatenate([collect(image) for image in images]) for images in partials]
-    )
+    shares = []
+    for d, images in enumerate(partials):
+        if d < DEPTHS - 1:
+            shares.append(collect(images))
+        else:
+            shares.append(jnp.concatenate([collect([image]) for image in images]))
+    shares = jnp.stack(shares)
     energy = total(jnp.sum(shares * shares, axis=(1, 2)))
     scale = 1.0 / jnp.sqrt(energy / (height * width) + epsilon)
     return shares * scale[:, None, None], jnp.stack(fields, axis=1)
@@ -739,6 +835,7 @@
         P("freq"),
         P(),
     )
+
     return jax.shard_map(
         shards,
         mesh=mesh,

time: 172 us -> 167 us (0.971)
  waiting for transfers between devices: 63.5 us -> 51 us
  starting transfers between devices: 54.6 us -> 60.7 us
  Pallas kernels: 45.2 us -> 48.2 us
  local copies, waits for them, and re-layouts: 3.91 us -> 1.05 us
    ppermute x47 -> x56, waiting for transfers between devices: 63.5 us -> 51 us  [swap(): return lax.ppermute(value, axis, [(i, i ^ distance) for i in range(count)])]
    ppermute x47 -> x56, starting transfers between devices: 54.6 us -> 60.7 us  [swap(): return lax.ppermute(value, axis, [(i, i ^ distance) for i in range(count)])]
    pallas_call x2, Pallas kernels: 3.79 us -> 7.6 us  [forward_x(): pl.pallas_call(functools.partial(first_kernel, lane=lane, per_device=per_...]
    unnamed x24 -> x32, local copies, waits for them, and re-layouts: 3.85 us -> 0.98 us
    pallas_call x2 -> x4, Pallas kernels: 12.4 us -> 11.5 us  [spectral(): pl.pallas_call(functools.partial(spectral_kernel, lane=lane, width=width,...]
  transfers between devices with their start and end apart: 47 -> 56, of which waited for: 23 -> 23; matrix products, arithmetic and copies ran while one was open for 0% -> 0% of each run, Pallas kernels for 22% -> 24%
where the time goes in v2:
time: 167 us; the launch traced here: 165 us
  starting transfers between devices  60.7 us (36%)
  waiting for transfers between devices  51 us (31%)
  Pallas kernels  48.2 us (29%)
  other arithmetic  2.16 us (1%)
  between operations  1.75 us (1%)
    ppermute x56, starting transfers between devices, swap(): return lax.ppermute(value, axis, [(i, i ^ distance) for i in range(count)])  60.7 us
    ppermute x56, waiting for transfers between devices, swap(): return lax.ppermute(value, axis, [(i, i ^ distance) for i in range(count)])  51 us
    pallas_call x4, Pallas kernels, space(): pl.pallas_call(functools.partial(space_kernel, lane=lane, devices=devices...  24.1 us
    pallas_call x4, Pallas kernels, spectral(): pl.pallas_call(functools.partial(spectral_kernel, lane=lane, width=width,...  11.5 us
    pallas_call x2, Pallas kernels, forward_x(): pl.pallas_call(functools.partial(first_kernel, lane=lane, per_device=per_...  7.6 us
    pallas_call x1, Pallas kernels, waves(): pl.pallas_call(functools.partial(wave_kernel, lane=lane, width=width, hei...  4.93 us
  transfers between devices with their start and end apart: 56, of which 23 were waited for; matrix products, arithmetic and copies ran while one was open for 0% of the time, Pallas kernels for 24%

profile of v2, /device:TPU:10, one launch (start us, length us, event | category | flops | bytes accessed | tf_op | source)
XLA Modules:
  0.0 164.8 jit_solution(1855016976634014193)
XLA Ops:
  1.3 3.8 %forward_x.2 = (bf16[128,1024]{1,0:T(8,128)(2,1)}, bf16[128,1024]{1,0:T(8,128)(2,1)}, bf16[128,1024]{1,0:T(8,128)(2,1)}, bf16[128,1024]{1,0:T(8,128)(2,1)}) custom-call(s32[3]{0:T(128)} %pad_add_fusion.refs_0_.refs_4_.me_ref, f32[2,256,2048]{2,1,0:T(8,128)} %bitcast.61, f32[2,16,128]{2,1,0:T(8,128)} %constant.53.clone.refs_2_.refs_4_, ...), custom_call_target="tpu_custom_call" | custom-call | flops 1048576000 | bytes 3145728 | tf_op jit(solution)/shard_map/forward_x/pallas_call | solution.py:186
  5.6 1.5 collective-permute-start.1
  7.1 1.4 collective-permute-start.2
  8.6 3.8 %forward_x.3 = (bf16[128,512]{1,0:T(8,128)(2,1)}, bf16[128,512]{1,0:T(8,128)(2,1)}, bf16[128,512]{1,0:T(8,128)(2,1)}, bf16[128,512]{1,0:T(8,128)(2,1)}, bf16[128...) custom-call(s32[3]{0:T(128)} %pad_add_fusion.refs_0_.refs_4_.me_ref, ...), custom_call_target="tpu_custom_call" | custom-call | flops 1048576000 | bytes 3145728 | tf_op jit(solution)/shard_map/forward_x/pallas_call | solution.py:186
  13.0 1.5 collective-permute-start.4
  15.2 6.6 %collective-permute-done.3.refs_9_ = bf16[128,512]{1,0:T(8,128)(2,1)S(1)} collective-permute-done((bf16[128,512]{1,0:T(8,128)(2,1)}, bf16[128,512]{1,0:T(8,128)(2,1)S(1)}, u32[]{:S(2)}, u32[]{:S(2)}) %collective-permute-start.3) | collective-permute-done | bytes 131104 | tf_op jit(solution)/shard_map/ppermute | solution.py:726
  21.8 1.5 collective-permute-start.5
  24.3 4.9 %waves.1 = (f32[5,256,256]{2,1,0:T(8,128)S(1)}, f32[5,256,256]{2,1,0:T(8,128)S(1)}, f32[5,256,256]{2,1,0:T(8,128)S(1)}, f32[5,256,256]{2,1,0:T(8,128)S(1)}) custom-call(s32[3]{0:T(128)S(1)} %copy-done.6, f32[2]{0:T(128)S(1)} %multiply_multiply_fusion.squared_ref, bf16[128,512]{1,0:T(8,128)(2,1)S(1)} %copy-done.9), custom_call_target="tpu_custom_call" | custom-call | flops 4194304000 | bytes 8388608 | tf_op jit(solution)/shard_map/waves/pallas_call | solution.py:275
  29.2 1.6 collective-permute-start.9
  31.3 1.5 collective-permute-start.11
  32.8 2.8 %spectral.4 = (bf16[144,512]{1,0:T(8,128)(2,1)S(1)}, bf16[144,512]{1,0:T(8,128)(2,1)S(1)}, bf16[144,512]{1,0:T(8,128)(2,1)S(1)}, bf16[144,512]{1,0:T(8,128)(2,1)...) custom-call(s32[3]{0:T(128)S(1)} %copy-done.6, ...), custom_call_target="tpu_custom_call" | custom-call | flops 2097152000 | bytes 4194304 | tf_op jit(solution)/shard_map/spectral/pallas_call | solution.py:476
  35.6 1.6 collective-permute-start.6
  37.7 1.5 collective-permute-start.8
  39.3 2.9 %spectral.5 = (bf16[144,512]{1,0:T(8,128)(2,1)S(1)}, bf16[144,512]{1,0:T(8,128)(2,1)S(1)}, bf16[144,512]{1,0:T(8,128)(2,1)S(1)}, bf16[144,512]{1,0:T(8,128)(2,1)...) custom-call(s32[3]{0:T(128)S(1)} %copy-done.6, ...), custom_call_target="tpu_custom_call" | custom-call | flops 2097152000 | bytes 4194304 | tf_op jit(solution)/shard_map/spectral/pallas_call | solution.py:476
  42.2 1.5 collective-permute-start.12
  44.2 1.5 collective-permute-start.14
  45.7 1.5 collective-permute-start.16
  48.9 1.4 collective-permute-start.18
  50.4 1.9 %collective-permute-done.13.refs_13_ = bf16[144,512]{1,0:T(8,128)(2,1)S(1)} collective-permute-done((bf16[144,512]{1,0:T(8,128)(2,1)S(1)}, bf16[144,512]{1,0:T(8,128)(2,1)S(1)}, u32[]{:S(2)}, u32[]{:S(2)}) %collective-permute-start.13) | collective-permute-done | bytes 147488 | tf_op jit(solution)/shard_map/ppermute | solution.py:726
  52.3 5.1 %space.2 = (bf16[128,1024]{1,0:T(8,128)(2,1)S(1)}, bf16[128,1024]{1,0:T(8,128)(2,1)S(1)}, bf16[128,1024]{1,0:T(8,128)(2,1)S(1)}, bf16[128,1024]{1,0:T(8,128)(2,1...) custom-call(s32[3]{0:T(128)S(1)} %copy-done.6, ...), custom_call_target="tpu_custom_call" | custom-call | flops 2097152000 | bytes 3145728 | tf_op jit(solution)/shard_map/space/pallas_call | solution.py:692
  57.7 4.1 %collective-permute-done.17.refs_9_ = bf16[128,1024]{1,0:T(8,128)(2,1)S(1)} collective-permute-done((bf16[128,1024]{1,0:T(8,128)(2,1)S(1)}, bf16[128,1024]{1,0:T(8,128)(2,1)S(1)}, u32[]{:S(2)}, u32[]{:S(2)}) %collective-permute-start.17) | collective-permute-done | bytes 262176 | tf_op jit(solution)/shard_map/ppermute | solution.py:726
  61.8 5.0 %space.3 = (bf16[128,512]{1,0:T(8,128)(2,1)S(1)}, bf16[128,512]{1,0:T(8,128)(2,1)S(1)}, bf16[128,512]{1,0:T(8,128)(2,1)S(1)}, bf16[128,512]{1,0:T(8,128)(2,1)S(1...) custom-call(s32[3]{0:T(128)S(1)} %copy-done.6, ...), custom_call_target="tpu_custom_call" | custom-call | flops 2097152000 | bytes 3145728 | tf_op jit(solution)/shard_map/space/pallas_call | solution.py:692
  67.1 1.8 %collective-permute-start.23 = (bf16[128,1024]{1,0:T(8,128)(2,1)S(1)}, bf16[128,1024]{1,0:T(8,128)(2,1)S(1)}, u32[]{:S(2)}, u32[]{:S(2)}) collective-permute-start(bf16[128,1024]{1,0:T(8,128)(2,1)S(1)} %get-tuple-element.111), channel_id=1, source_target_pairs={{0,1},{1,0},{2,3},{3,2},{4,5},{5,4},{6,7},{7,6},{8,9},{9,8},{10,11... | collective-permute-start | bytes 786440 | tf_op jit(solution)/shard_map/ppermute | solution.py:726
  70.6 1.4 collective-permute-start.27
  72.0 1.3 collective-permute-done.26.refs_9_
  74.3 11.0 %collective-permute-done.27.refs_10_ = bf16[128,512]{1,0:T(8,128)(2,1)S(1)} collective-permute-done((bf16[128,512]{1,0:T(8,128)(2,1)S(1)}, bf16[128,512]{1,0:T(8,128)(2,1)S(1)}, u32[]{:S(2)}, u32[]{:S(2)}) %collective-permute-start.27) | collective-permute-done | bytes 131104 | tf_op jit(solution)/shard_map/ppermute | solution.py:726
  86.8 1.9 %collective-permute-start.34 = (bf16[128,512]{1,0:T(8,128)(2,1)S(1)}, bf16[128,512]{1,0:T(8,128)(2,1)S(1)}, u32[]{:S(2)}, u32[]{:S(2)}) collective-permute-start(bf16[128,512]{1,0:T(8,128)(2,1)S(1)} %get-tuple-element.126), channel_id=1, source_target_pairs={{0,3},{1,2},{2,1},{3,0},{4,7},{5,6},{6,5},{7,4},{8,11},{9,10},{10,... | collective-permute-start | bytes 393224 | tf_op jit(solution)/shard_map/ppermute | solution.py:726
  88.7 2.8 %spectral.6 = (bf16[144,512]{1,0:T(8,128)(2,1)S(1)}, bf16[144,512]{1,0:T(8,128)(2,1)S(1)}, bf16[144,512]{1,0:T(8,128)(2,1)S(1)}, bf16[144,512]{1,0:T(8,128)(2,1)...) custom-call(s32[3]{0:T(128)S(1)} %copy-done.6, ...), custom_call_target="tpu_custom_call" | custom-call | flops 2097152000 | bytes 4194304 | tf_op jit(solution)/shard_map/spectral/pallas_call | solution.py:476
  91.6 3.0 %collective-permute-done.34.refs_11_ = bf16[128,512]{1,0:T(8,128)(2,1)S(1)} collective-permute-done((bf16[128,512]{1,0:T(8,128)(2,1)S(1)}, bf16[128,512]{1,0:T(8,128)(2,1)S(1)}, u32[]{:S(2)}, u32[]{:S(2)}) %collective-permute-start.34) | collective-permute-done | bytes 131104 | tf_op jit(solution)/shard_map/ppermute | solution.py:726
  94.6 3.0 %spectral.7 = (bf16[144,512]{1,0:T(8,128)(2,1)S(1)}, bf16[144,512]{1,0:T(8,128)(2,1)S(1)}, bf16[144,512]{1,0:T(8,128)(2,1)S(1)}, bf16[144,512]{1,0:T(8,128)(2,1)...) custom-call(s32[3]{0:T(128)S(1)} %copy-done.6, ...), custom_call_target="tpu_custom_call" | custom-call | flops 2097152000 | bytes 4194304 | tf_op jit(solution)/shard_map/spectral/pallas_call | solution.py:476
  102.4 1.3 collective-permute-start.30
  104.4 1.7 %collective-permute-start.31 = (bf16[144,512]{1,0:T(8,128)(2,1)S(1)}, bf16[144,512]{1,0:T(8,128)(2,1)S(1)}, u32[]{:S(2)}, u32[]{:S(2)}) collective-permute-start(bf16[144,512]{1,0:T(8,128)(2,1)S(1)} %get-tuple-element.121), channel_id=1, source_target_pairs={{0,3},{1,2},{2,1},{3,0},{4,7},{5,6},{6,5},{7,4},{8,11},{9,10},{10,... | collective-permute-start | bytes 442376 | tf_op jit(solution)/shard_map/ppermute | solution.py:726
  106.1 2.3 %collective-permute-done.36.refs_13_ = bf16[144,512]{1,0:T(8,128)(2,1)S(1)} collective-permute-done((bf16[144,512]{1,0:T(8,128)(2,1)S(1)}, bf16[144,512]{1,0:T(8,128)(2,1)S(1)}, u32[]{:S(2)}, u32[]{:S(2)}) %collective-permute-start.36) | collective-permute-done | bytes 147488 | tf_op jit(solution)/shard_map/ppermute | solution.py:726
  109.4 1.4 collective-permute-done.29.refs_8_
  111.4 2.5 %collective-permute-done.30.refs_9_ = bf16[144,512]{1,0:T(8,128)(2,1)S(1)} collective-permute-done((bf16[144,512]{1,0:T(8,128)(2,1)S(1)}, bf16[144,512]{1,0:T(8,128)(2,1)S(1)}, u32[]{:S(2)}, u32[]{:S(2)}) %collective-permute-start.30) | collective-permute-done | bytes 147488 | tf_op jit(solution)/shard_map/ppermute | solution.py:726
  114.3 2.6 %collective-permute-start.21 = (bf16[256,256]{1,0:T(8,128)(2,1)S(1)}, bf16[256,256]{1,0:T(8,128)(2,1)S(1)}, u32[]{:S(2)}, u32[]{:S(2)}) collective-permute-start(bf16[256,256]{1,0:T(8,128)(2,1)S(1)} %pad_maximum_fusion.2), channel_id=1, source_target_pairs={{0,16},{4,20},{8,24},{12,28},{16,0},{20,4},{24,8},{28,12},{1,17},{... | collective-permute-start | bytes 393224 | tf_op jit(solution)/shard_map/ppermute | solution.py:726
  116.9 7.1 %space_last.2 = (f32[2,256,2048]{2,1,0:T(8,128)}, bf16[4,128,256]{2,1,0:T(8,128)(2,1)S(1)}, bf16[4,128,256]{2,1,0:T(8,128)(2,1)S(1)}, f32[2,16,2048]{2,1,0:T(8,128)S(1)}) custom-call(s32[3]{0:T(128)S(1)} %copy-done.6, f32[2]{0:T(128)S(1)} %bitcast.59, bf16[256,2048]{1,0:T(8,128)(2,1)S(1)} %copy-done.1, bf16[2,16,128,128]{3,2,1,0:T(8,128)(2,1)S(1)} %bitcast.55, ...), custom_call_target="tpu_custom_call" | custom-call | flops 2097152000 | bytes 3145728 | tf_op jit(solution)/shard_map/space_last/pallas_call | solution.py:692
  124.1 1.6 collective-permute-done.22
  125.8 7.0 %space_last.3 = (f32[2,256,2048]{2,1,0:T(8,128)}, bf16[4,128,256]{2,1,0:T(8,128)(2,1)S(1)}, bf16[4,128,256]{2,1,0:T(8,128)(2,1)S(1)}) custom-call(s32[3]{0:T(128)S(1)} %copy-done.6, f32[2]{0:T(128)S(1)} %bitcast.60, bf16[256,2048]{1,0:T(8,128)(2,1)S(1)} %copy-done.1, bf16[2,16,128,128]{3,2,1,0:T(8,128)(2,1)S(1)} %bitcast.56, ...), custom_call_target="tpu_custom_call", output_to_operand_aliasing={{0}: (12, {})} | custom-call | flops 2097152000 | bytes 3145728 | tf_op jit(solution)/shard_map/space_last/pallas_call | solution.py:692
  133.7 1.9 %collective-permute-start.41 = (bf16[128,256]{1,0:T(8,128)(2,1)S(1)}, bf16[128,256]{1,0:T(8,128)(2,1)S(1)}, u32[]{:S(2)}, u32[]{:S(2)}) collective-permute-start(bf16[128,256]{1,0:T(8,128)(2,1)S(1)} %get-tuple-element.157), channel_id=1, source_target_pairs={{0,24},{4,28},{8,16},{12,20},{16,8},{20,12},{24,0},{28,4},{1,25},{... | collective-permute-start | bytes 196616 | tf_op jit(solution)/shard_map/ppermute | solution.py:726
  135.5 1.8 %collective-permute-start.40 = (bf16[128,256]{1,0:T(8,128)(2,1)S(1)}, bf16[128,256]{1,0:T(8,128)(2,1)S(1)}, u32[]{:S(2)}, u32[]{:S(2)}) collective-permute-start(bf16[128,256]{1,0:T(8,128)(2,1)S(1)} %get-tuple-element.158), channel_id=1, source_target_pairs={{0,16},{4,20},{8,24},{12,28},{16,0},{20,4},{24,8},{28,12},{1,17},{... | collective-permute-start | bytes 196616 | tf_op jit(solution)/shard_map/ppermute | solution.py:726
  138.5 1.5 collective-permute-start.48
  140.1 1.8 %collective-permute-start.47 = (bf16[128,256]{1,0:T(8,128)(2,1)S(1)}, bf16[128,256]{1,0:T(8,128)(2,1)S(1)}, u32[]{:S(2)}, u32[]{:S(2)}) collective-permute-start(bf16[128,256]{1,0:T(8,128)(2,1)S(1)} %get-tuple-element.161), channel_id=1, source_target_pairs={{0,16},{4,20},{8,24},{12,28},{16,0},{20,4},{24,8},{28,12},{1,17},{... | collective-permute-start | bytes 196616 | tf_op jit(solution)/shard_map/ppermute | solution.py:726
  144.0 3.9 %collective-permute-done.48 = bf16[128,256]{1,0:T(8,128)(2,1)S(1)} collective-permute-done((bf16[128,256]{1,0:T(8,128)(2,1)S(1)}, bf16[128,256]{1,0:T(8,128)(2,1)S(1)}, u32[]{:S(2)}, u32[]{:S(2)}) %collective-permute-start.48) | collective-permute-done | bytes 65568 | tf_op jit(solution)/shard_map/ppermute | solution.py:726
  150.5 3.9 %collective-permute-start.51 = (f32[2]{0:T(128)S(1)}, f32[2]{0:T(128)S(1)}, u32[]{:S(2)}, u32[]{:S(2)}) collective-permute-start(f32[2]{0:T(128)S(1)} %add.82), channel_id=1, source_target_pairs={{0,16},{4,20},{8,24},{12,28},{16,0},{20,4},{24,8},{28,12},{1,17},{... | collective-permute-start | bytes 32 | tf_op jit(solution)/shard_map/ppermute | solution.py:726
  154.4 1.5 collective-permute-done.51
  156.0 2.0 %collective-permute-done.50 = f32[2]{0:T(128)S(1)} collective-permute-done((f32[2]{0:T(128)S(1)}, f32[2]{0:T(128)S(1)}, u32[]{:S(2)}, u32[]{:S(2)}) %collective-permute-start.50) | collective-permute-done | bytes 40 | tf_op jit(solution)/shard_map/ppermute | solution.py:726
  158.0 1.6 collective-permute-start.55
  (129 shorter events, 30.5 us)
Async XLA Ops:
  5.0 26.3 %collective-permute-start = (bf16[128,1024]{1,0:T(8,128)(2,1)}, bf16[128,1024]{1,0:T(8,128)(2,1)S(1)}, u32[]{:S(2)}, u32[]{:S(2)}) collective-permute-start(bf16[128,1024]{1,0:T(8,128)(2,1)} %get-tuple-element.77), channel_id=1, source_target_pairs={{0,1},{1,0},{2,3},{3,2},{4,5},{5,4},{6,7},{7,6},{8,9},{9,8},{10,11... | collective-permute-start | bytes 786440 | tf_op jit(solution)/shard_map/ppermute | solution.py:726
  5.6 27.2 %collective-permute-start.1 = (bf16[128,1024]{1,0:T(8,128)(2,1)}, bf16[128,1024]{1,0:T(8,128)(2,1)S(1)}, u32[]{:S(2)}, u32[]{:S(2)}) collective-permute-start(bf16[128,1024]{1,0:T(8,128)(2,1)} %get-tuple-element.78), channel_id=1, source_target_pairs={{0,2},{1,3},{2,0},{3,1},{4,6},{5,7},{6,4},{7,5},{8,10},{9,11},{10,... | collective-permute-start | bytes 786440 | tf_op jit(solution)/shard_map/ppermute | solution.py:726
  7.1 25.6 %collective-permute-start.2 = (bf16[128,1024]{1,0:T(8,128)(2,1)}, bf16[128,1024]{1,0:T(8,128)(2,1)S(1)}, u32[]{:S(2)}, u32[]{:S(2)}) collective-permute-start(bf16[128,1024]{1,0:T(8,128)(2,1)} %get-tuple-element.79), channel_id=1, source_target_pairs={{0,3},{1,2},{2,1},{3,0},{4,7},{5,6},{6,5},{7,4},{8,11},{9,10},{10,... | collective-permute-start | bytes 786440 | tf_op jit(solution)/shard_map/ppermute | solution.py:726
  12.4 9.4 %collective-permute-start.3 = (bf16[128,512]{1,0:T(8,128)(2,1)}, bf16[128,512]{1,0:T(8,128)(2,1)S(1)}, u32[]{:S(2)}, u32[]{:S(2)}) collective-permute-start(bf16[128,512]{1,0:T(8,128)(2,1)} %get-tuple-element.80), channel_id=1, source_target_pairs={{0,1},{1,0},{2,3},{3,2},{4,5},{5,4},{6,7},{7,6},{8,9},{9,8},{10,11... | collective-permute-start | bytes 393224 | tf_op jit(solution)/shard_map/ppermute | solution.py:726
  13.0 16.2 %collective-permute-start.4 = (bf16[128,512]{1,0:T(8,128)(2,1)}, bf16[128,512]{1,0:T(8,128)(2,1)S(1)}, u32[]{:S(2)}, u32[]{:S(2)}) collective-permute-start(bf16[128,512]{1,0:T(8,128)(2,1)} %get-tuple-element.81), channel_id=1, source_target_pairs={{0,2},{1,3},{2,0},{3,1},{4,6},{5,7},{6,4},{7,5},{8,10},{9,11},{10,... | collective-permute-start | bytes 393224 | tf_op jit(solution)/shard_map/ppermute | solution.py:726
  21.8 9.0 %collective-permute-start.5 = (bf16[128,512]{1,0:T(8,128)(2,1)}, bf16[128,512]{1,0:T(8,128)(2,1)S(1)}, u32[]{:S(2)}, u32[]{:S(2)}) collective-permute-start(bf16[128,512]{1,0:T(8,128)(2,1)} %get-tuple-element.82), channel_id=1, source_target_pairs={{0,3},{1,2},{2,1},{3,0},{4,7},{5,6},{6,5},{7,4},{8,11},{9,10},{10,... | collective-permute-start | bytes 393224 | tf_op jit(solution)/shard_map/ppermute | solution.py:726
  29.2 8.5 %collective-permute-start.9 = (bf16[128,512]{1,0:T(8,128)(2,1)S(1)}, bf16[128,512]{1,0:T(8,128)(2,1)S(1)}, u32[]{:S(2)}, u32[]{:S(2)}) collective-permute-start(bf16[128,512]{1,0:T(8,128)(2,1)S(1)} %copy-done.14), channel_id=1, source_target_pairs={{0,1},{1,0},{2,3},{3,2},{4,5},{5,4},{6,7},{7,6},{8,9},{9,8},{10,11... | collective-permute-start | bytes 393224 | tf_op jit(solution)/shard_map/ppermute | solution.py:726
  30.8 8.4 %collective-permute-start.10 = (bf16[128,512]{1,0:T(8,128)(2,1)S(1)}, bf16[128,512]{1,0:T(8,128)(2,1)S(1)}, u32[]{:S(2)}, u32[]{:S(2)}) collective-permute-start(bf16[128,512]{1,0:T(8,128)(2,1)S(1)} %copy-done.13), channel_id=1, source_target_pairs={{0,2},{1,3},{2,0},{3,1},{4,6},{5,7},{6,4},{7,5},{8,10},{9,11},{10,... | collective-permute-start | bytes 393224 | tf_op jit(solution)/shard_map/ppermute | solution.py:726
  31.3 7.9 %collective-permute-start.11 = (bf16[128,512]{1,0:T(8,128)(2,1)S(1)}, bf16[128,512]{1,0:T(8,128)(2,1)S(1)}, u32[]{:S(2)}, u32[]{:S(2)}) collective-permute-start(bf16[128,512]{1,0:T(8,128)(2,1)S(1)} %copy-done.12), channel_id=1, source_target_pairs={{0,3},{1,2},{2,1},{3,0},{4,7},{5,6},{6,5},{7,4},{8,11},{9,10},{10,... | collective-permute-start | bytes 393224 | tf_op jit(solution)/shard_map/ppermute | solution.py:726
  35.6 8.6 %collective-permute-start.6 = (bf16[144,512]{1,0:T(8,128)(2,1)S(1)}, bf16[144,512]{1,0:T(8,128)(2,1)S(1)}, u32[]{:S(2)}, u32[]{:S(2)}) collective-permute-start(bf16[144,512]{1,0:T(8,128)(2,1)S(1)} %get-tuple-element.84), channel_id=1, source_target_pairs={{0,1},{1,0},{2,3},{3,2},{4,5},{5,4},{6,7},{7,6},{8,9},{9,8},{10,11... | collective-permute-start | bytes 442376 | tf_op jit(solution)/shard_map/ppermute | solution.py:726
  37.2 8.5 %collective-permute-start.7 = (bf16[144,512]{1,0:T(8,128)(2,1)S(1)}, bf16[144,512]{1,0:T(8,128)(2,1)S(1)}, u32[]{:S(2)}, u32[]{:S(2)}) collective-permute-start(bf16[144,512]{1,0:T(8,128)(2,1)S(1)} %get-tuple-element.85), channel_id=1, source_target_pairs={{0,2},{1,3},{2,0},{3,1},{4,6},{5,7},{6,4},{7,5},{8,10},{9,11},{10,... | collective-permute-start | bytes 442376 | tf_op jit(solution)/shard_map/ppermute | solution.py:726
  37.7 9.5 %collective-permute-start.8 = (bf16[144,512]{1,0:T(8,128)(2,1)S(1)}, bf16[144,512]{1,0:T(8,128)(2,1)S(1)}, u32[]{:S(2)}, u32[]{:S(2)}) collective-permute-start(bf16[144,512]{1,0:T(8,128)(2,1)S(1)} %get-tuple-element.86), channel_id=1, source_target_pairs={{0,3},{1,2},{2,1},{3,0},{4,7},{5,6},{6,5},{7,4},{8,11},{9,10},{10,... | collective-permute-start | bytes 442376 | tf_op jit(solution)/shard_map/ppermute | solution.py:726
  42.2 6.8 %collective-permute-start.12 = (bf16[144,512]{1,0:T(8,128)(2,1)S(1)}, bf16[144,512]{1,0:T(8,128)(2,1)S(1)}, u32[]{:S(2)}, u32[]{:S(2)}) collective-permute-start(bf16[144,512]{1,0:T(8,128)(2,1)S(1)} %get-tuple-element.97), channel_id=1, source_target_pairs={{0,1},{1,0},{2,3},{3,2},{4,5},{5,4},{6,7},{7,6},{8,9},{9,8},{10,11... | collective-permute-start | bytes 442376 | tf_op jit(solution)/shard_map/ppermute | solution.py:726
  43.7 8.6 %collective-permute-start.13 = (bf16[144,512]{1,0:T(8,128)(2,1)S(1)}, bf16[144,512]{1,0:T(8,128)(2,1)S(1)}, u32[]{:S(2)}, u32[]{:S(2)}) collective-permute-start(bf16[144,512]{1,0:T(8,128)(2,1)S(1)} %get-tuple-element.98), channel_id=1, source_target_pairs={{0,2},{1,3},{2,0},{3,1},{4,6},{5,7},{6,4},{7,5},{8,10},{9,11},{10,... | collective-permute-start | bytes 442376 | tf_op jit(solution)/shard_map/ppermute | solution.py:726
  44.2 8.1 %collective-permute-start.14 = (bf16[144,512]{1,0:T(8,128)(2,1)S(1)}, bf16[144,512]{1,0:T(8,128)(2,1)S(1)}, u32[]{:S(2)}, u32[]{:S(2)}) collective-permute-start(bf16[144,512]{1,0:T(8,128)(2,1)S(1)} %get-tuple-element.99), channel_id=1, source_target_pairs={{0,3},{1,2},{2,1},{3,0},{4,7},{5,6},{6,5},{7,4},{8,11},{9,10},{10,... | collective-permute-start | bytes 442376 | tf_op jit(solution)/shard_map/ppermute | solution.py:726
  45.7 12.0 %collective-permute-start.16 = (bf16[128,1024]{1,0:T(8,128)(2,1)S(1)}, bf16[128,1024]{1,0:T(8,128)(2,1)S(1)}, u32[]{:S(2)}, u32[]{:S(2)}) collective-permute-start(bf16[128,1024]{1,0:T(8,128)(2,1)S(1)} %get-tuple-element.103), channel_id=1, source_target_pairs={{0,1},{1,0},{2,3},{3,2},{4,5},{5,4},{6,7},{7,6},{8,9},{9,8},{10,11... | collective-permute-start | bytes 786440 | tf_op jit(solution)/shard_map/ppermute | solution.py:726
  47.2 14.6 %collective-permute-start.17 = (bf16[128,1024]{1,0:T(8,128)(2,1)S(1)}, bf16[128,1024]{1,0:T(8,128)(2,1)S(1)}, u32[]{:S(2)}, u32[]{:S(2)}) collective-permute-start(bf16[128,1024]{1,0:T(8,128)(2,1)S(1)} %get-tuple-element.104), channel_id=1, source_target_pairs={{0,2},{1,3},{2,0},{3,1},{4,6},{5,7},{6,4},{7,5},{8,10},{9,11},{10,... | collective-permute-start | bytes 786440 | tf_op jit(solution)/shard_map/ppermute | solution.py:726
  48.9 12.9 %collective-permute-start.18 = (bf16[128,1024]{1,0:T(8,128)(2,1)S(1)}, bf16[128,1024]{1,0:T(8,128)(2,1)S(1)}, u32[]{:S(2)}, u32[]{:S(2)}) collective-permute-start(bf16[128,1024]{1,0:T(8,128)(2,1)S(1)} %get-tuple-element.105), channel_id=1, source_target_pairs={{0,3},{1,2},{2,1},{3,0},{4,7},{5,6},{6,5},{7,4},{8,11},{9,10},{10,... | collective-permute-start | bytes 786440 | tf_op jit(solution)/shard_map/ppermute | solution.py:726
  66.8 6.4 %collective-permute-start.26 = (bf16[128,512]{1,0:T(8,128)(2,1)S(1)}, bf16[128,512]{1,0:T(8,128)(2,1)S(1)}, u32[]{:S(2)}, u32[]{:S(2)}) collective-permute-start(bf16[128,512]{1,0:T(8,128)(2,1)S(1)} %get-tuple-element.115), channel_id=1, source_target_pairs={{0,1},{1,0},{2,3},{3,2},{4,5},{5,4},{6,7},{7,6},{8,9},{9,8},{10,11... | collective-permute-start | bytes 393224 | tf_op jit(solution)/shard_map/ppermute | solution.py:726
  67.1 18.5 %collective-permute-start.23 = (bf16[128,1024]{1,0:T(8,128)(2,1)S(1)}, bf16[128,1024]{1,0:T(8,128)(2,1)S(1)}, u32[]{:S(2)}, u32[]{:S(2)}) collective-permute-start(bf16[128,1024]{1,0:T(8,128)(2,1)S(1)} %get-tuple-element.111), channel_id=1, source_target_pairs={{0,1},{1,0},{2,3},{3,2},{4,5},{5,4},{6,7},{7,6},{8,9},{9,8},{10,11... | collective-permute-start | bytes 786440 | tf_op jit(solution)/shard_map/ppermute | solution.py:726
  68.9 17.9 %collective-permute-start.24 = (bf16[128,1024]{1,0:T(8,128)(2,1)S(1)}, bf16[128,1024]{1,0:T(8,128)(2,1)S(1)}, u32[]{:S(2)}, u32[]{:S(2)}) collective-permute-start(bf16[128,1024]{1,0:T(8,128)(2,1)S(1)} %get-tuple-element.112), channel_id=1, source_target_pairs={{0,2},{1,3},{2,0},{3,1},{4,6},{5,7},{6,4},{7,5},{8,10},{9,11},{10,... | collective-permute-start | bytes 786440 | tf_op jit(solution)/shard_map/ppermute | solution.py:726
  69.9 18.8 %collective-permute-start.25 = (bf16[128,1024]{1,0:T(8,128)(2,1)S(1)}, bf16[128,1024]{1,0:T(8,128)(2,1)S(1)}, u32[]{:S(2)}, u32[]{:S(2)}) collective-permute-start(bf16[128,1024]{1,0:T(8,128)(2,1)S(1)} %get-tuple-element.113), channel_id=1, source_target_pairs={{0,3},{1,2},{2,1},{3,0},{4,7},{5,6},{6,5},{7,4},{8,11},{9,10},{10,... | collective-permute-start | bytes 786440 | tf_op jit(solution)/shard_map/ppermute | solution.py:726
  70.6 14.7 %collective-permute-start.27 = (bf16[128,512]{1,0:T(8,128)(2,1)S(1)}, bf16[128,512]{1,0:T(8,128)(2,1)S(1)}, u32[]{:S(2)}, u32[]{:S(2)}) collective-permute-start(bf16[128,512]{1,0:T(8,128)(2,1)S(1)} %get-tuple-element.116), channel_id=1, source_target_pairs={{0,2},{1,3},{2,0},{3,1},{4,6},{5,7},{6,4},{7,5},{8,10},{9,11},{10,... | collective-permute-start | bytes 393224 | tf_op jit(solution)/shard_map/ppermute | solution.py:726
  73.3 12.0 %collective-permute-start.28 = (bf16[128,512]{1,0:T(8,128)(2,1)S(1)}, bf16[128,512]{1,0:T(8,128)(2,1)S(1)}, u32[]{:S(2)}, u32[]{:S(2)}) collective-permute-start(bf16[128,512]{1,0:T(8,128)(2,1)S(1)} %get-tuple-element.117), channel_id=1, source_target_pairs={{0,3},{1,2},{2,1},{3,0},{4,7},{5,6},{6,5},{7,4},{8,11},{9,10},{10,... | collective-permute-start | bytes 393224 | tf_op jit(solution)/shard_map/ppermute | solution.py:726
  85.2 16.0 %collective-permute-start.15 = (bf16[4,128,256]{2,1,0:T(8,128)(2,1)S(1)}, bf16[4,128,256]{2,1,0:T(8,128)(2,1)S(1)}, u32[]{:S(2)}, u32[]{:S(2)}) collective-permute-start(bf16[4,128,256]{2,1,0:T(8,128)(2,1)S(1)} %get-tuple-element.101), channel_id=1, source_target_pairs={{0,4},{4,0},{8,12},{12,8},{16,20},{20,16},{24,28},{28,24},{1,5},{5... | collective-permute-start | bytes 786440 | tf_op jit(solution)/shard_map/ppermute | solution.py:726
  85.2 6.4 %collective-permute-start.32 = (bf16[128,512]{1,0:T(8,128)(2,1)S(1)}, bf16[128,512]{1,0:T(8,128)(2,1)S(1)}, u32[]{:S(2)}, u32[]{:S(2)}) collective-permute-start(bf16[128,512]{1,0:T(8,128)(2,1)S(1)} %get-tuple-element.124), channel_id=1, source_target_pairs={{0,1},{1,0},{2,3},{3,2},{4,5},{5,4},{6,7},{7,6},{8,9},{9,8},{10,11... | collective-permute-start | bytes 393224 | tf_op jit(solution)/shard_map/ppermute | solution.py:726
  85.6 6.0 %collective-permute-start.33 = (bf16[128,512]{1,0:T(8,128)(2,1)S(1)}, bf16[128,512]{1,0:T(8,128)(2,1)S(1)}, u32[]{:S(2)}, u32[]{:S(2)}) collective-permute-start(bf16[128,512]{1,0:T(8,128)(2,1)S(1)} %get-tuple-element.125), channel_id=1, source_target_pairs={{0,2},{1,3},{2,0},{3,1},{4,6},{5,7},{6,4},{7,5},{8,10},{9,11},{10,... | collective-permute-start | bytes 393224 | tf_op jit(solution)/shard_map/ppermute | solution.py:726
  86.8 7.8 %collective-permute-start.34 = (bf16[128,512]{1,0:T(8,128)(2,1)S(1)}, bf16[128,512]{1,0:T(8,128)(2,1)S(1)}, u32[]{:S(2)}, u32[]{:S(2)}) collective-permute-start(bf16[128,512]{1,0:T(8,128)(2,1)S(1)} %get-tuple-element.126), channel_id=1, source_target_pairs={{0,3},{1,2},{2,1},{3,0},{4,7},{5,6},{6,5},{7,4},{8,11},{9,10},{10,... | collective-permute-start | bytes 393224 | tf_op jit(solution)/shard_map/ppermute | solution.py:726
  88.7 13.7 %collective-permute-start.19 = (bf16[4,128,256]{2,1,0:T(8,128)(2,1)S(1)}, bf16[4,128,256]{2,1,0:T(8,128)(2,1)S(1)}, u32[]{:S(2)}, u32[]{:S(2)}) collective-permute-start(bf16[4,128,256]{2,1,0:T(8,128)(2,1)S(1)} %get-tuple-element.108), channel_id=1, source_target_pairs={{0,4},{4,0},{8,12},{12,8},{16,20},{20,16},{24,28},{28,24},{1,5},{5... | collective-permute-start | bytes 786440 | tf_op jit(solution)/shard_map/ppermute | solution.py:726
  97.7 6.8 %collective-permute-start.35 = (bf16[144,512]{1,0:T(8,128)(2,1)S(1)}, bf16[144,512]{1,0:T(8,128)(2,1)S(1)}, u32[]{:S(2)}, u32[]{:S(2)}) collective-permute-start(bf16[144,512]{1,0:T(8,128)(2,1)S(1)} %get-tuple-element.132), channel_id=1, source_target_pairs={{0,1},{1,0},{2,3},{3,2},{4,5},{5,4},{6,7},{7,6},{8,9},{9,8},{10,11... | collective-permute-start | bytes 442376 | tf_op jit(solution)/shard_map/ppermute | solution.py:726
  98.8 9.6 %collective-permute-start.36 = (bf16[144,512]{1,0:T(8,128)(2,1)S(1)}, bf16[144,512]{1,0:T(8,128)(2,1)S(1)}, u32[]{:S(2)}, u32[]{:S(2)}) collective-permute-start(bf16[144,512]{1,0:T(8,128)(2,1)S(1)} %get-tuple-element.133), channel_id=1, source_target_pairs={{0,2},{1,3},{2,0},{3,1},{4,6},{5,7},{6,4},{7,5},{8,10},{9,11},{10,... | collective-permute-start | bytes 442376 | tf_op jit(solution)/shard_map/ppermute | solution.py:726
  100.0 8.9 %collective-permute-start.37 = (bf16[144,512]{1,0:T(8,128)(2,1)S(1)}, bf16[144,512]{1,0:T(8,128)(2,1)S(1)}, u32[]{:S(2)}, u32[]{:S(2)}) collective-permute-start(bf16[144,512]{1,0:T(8,128)(2,1)S(1)} %get-tuple-element.134), channel_id=1, source_target_pairs={{0,3},{1,2},{2,1},{3,0},{4,7},{5,6},{6,5},{7,4},{8,11},{9,10},{10,... | collective-permute-start | bytes 442376 | tf_op jit(solution)/shard_map/ppermute | solution.py:726
  101.2 9.5 %collective-permute-start.29 = (bf16[144,512]{1,0:T(8,128)(2,1)S(1)}, bf16[144,512]{1,0:T(8,128)(2,1)S(1)}, u32[]{:S(2)}, u32[]{:S(2)}) collective-permute-start(bf16[144,512]{1,0:T(8,128)(2,1)S(1)} %get-tuple-element.119), channel_id=1, source_target_pairs={{0,1},{1,0},{2,3},{3,2},{4,5},{5,4},{6,7},{7,6},{8,9},{9,8},{10,11... | collective-permute-start | bytes 442376 | tf_op jit(solution)/shard_map/ppermute | solution.py:726
  102.4 11.5 %collective-permute-start.30 = (bf16[144,512]{1,0:T(8,128)(2,1)S(1)}, bf16[144,512]{1,0:T(8,128)(2,1)S(1)}, u32[]{:S(2)}, u32[]{:S(2)}) collective-permute-start(bf16[144,512]{1,0:T(8,128)(2,1)S(1)} %get-tuple-element.120), channel_id=1, source_target_pairs={{0,2},{1,3},{2,0},{3,1},{4,6},{5,7},{6,4},{7,5},{8,10},{9,11},{10,... | collective-permute-start | bytes 442376 | tf_op jit(solution)/shard_map/ppermute | solution.py:726
  104.4 9.9 %collective-permute-start.31 = (bf16[144,512]{1,0:T(8,128)(2,1)S(1)}, bf16[144,512]{1,0:T(8,128)(2,1)S(1)}, u32[]{:S(2)}, u32[]{:S(2)}) collective-permute-start(bf16[144,512]{1,0:T(8,128)(2,1)S(1)} %get-tuple-element.121), channel_id=1, source_target_pairs={{0,3},{1,2},{2,1},{3,0},{4,7},{5,6},{6,5},{7,4},{8,11},{9,10},{10,... | collective-permute-start | bytes 442376 | tf_op jit(solution)/shard_map/ppermute | solution.py:726
  108.4 8.5 %collective-permute-start.20 = (bf16[256,256]{1,0:T(8,128)(2,1)S(1)}, bf16[256,256]{1,0:T(8,128)(2,1)S(1)}, u32[]{:S(2)}, u32[]{:S(2)}) collective-permute-start(bf16[256,256]{1,0:T(8,128)(2,1)S(1)} %pad_maximum_fusion.1), channel_id=1, source_target_pairs={{0,8},{4,12},{8,0},{12,4},{16,24},{20,28},{24,16},{28,20},{1,9},{5... | collective-permute-start | bytes 393224 | tf_op jit(solution)/shard_map/ppermute | solution.py:726
  108.9 16.8 %collective-permute-start.42 = (bf16[128,1024]{1,0:T(8,128)(2,1)S(1)}, bf16[128,1024]{1,0:T(8,128)(2,1)S(1)}, u32[]{:S(2)}, u32[]{:S(2)}) collective-permute-start(bf16[128,1024]{1,0:T(8,128)(2,1)S(1)} %get-tuple-element.138), channel_id=1, source_target_pairs={{0,1},{1,0},{2,3},{3,2},{4,5},{5,4},{6,7},{7,6},{8,9},{9,8},{10,11... | collective-permute-start | bytes 786440 | tf_op jit(solution)/shard_map/ppermute | solution.py:726
  110.8 15.0 %collective-permute-start.43 = (bf16[128,1024]{1,0:T(8,128)(2,1)S(1)}, bf16[128,1024]{1,0:T(8,128)(2,1)S(1)}, u32[]{:S(2)}, u32[]{:S(2)}) collective-permute-start(bf16[128,1024]{1,0:T(8,128)(2,1)S(1)} %get-tuple-element.139), channel_id=1, source_target_pairs={{0,2},{1,3},{2,0},{3,1},{4,6},{5,7},{6,4},{7,5},{8,10},{9,11},{10,... | collective-permute-start | bytes 786440 | tf_op jit(solution)/shard_map/ppermute | solution.py:726
  113.9 11.8 %collective-permute-start.44 = (bf16[128,1024]{1,0:T(8,128)(2,1)S(1)}, bf16[128,1024]{1,0:T(8,128)(2,1)S(1)}, u32[]{:S(2)}, u32[]{:S(2)}) collective-permute-start(bf16[128,1024]{1,0:T(8,128)(2,1)S(1)} %get-tuple-element.140), channel_id=1, source_target_pairs={{0,3},{1,2},{2,1},{3,0},{4,7},{5,6},{6,5},{7,4},{8,11},{9,10},{10,... | collective-permute-start | bytes 786440 | tf_op jit(solution)/shard_map/ppermute | solution.py:726
  114.3 9.7 %collective-permute-start.21 = (bf16[256,256]{1,0:T(8,128)(2,1)S(1)}, bf16[256,256]{1,0:T(8,128)(2,1)S(1)}, u32[]{:S(2)}, u32[]{:S(2)}) collective-permute-start(bf16[256,256]{1,0:T(8,128)(2,1)S(1)} %pad_maximum_fusion.2), channel_id=1, source_target_pairs={{0,16},{4,20},{8,24},{12,28},{16,0},{20,4},{24,8},{28,12},{1,17},{... | collective-permute-start | bytes 393224 | tf_op jit(solution)/shard_map/ppermute | solution.py:726
  116.9 8.8 %collective-permute-start.22 = (bf16[256,256]{1,0:T(8,128)(2,1)S(1)}, bf16[256,256]{1,0:T(8,128)(2,1)S(1)}, u32[]{:S(2)}, u32[]{:S(2)}) collective-permute-start(bf16[256,256]{1,0:T(8,128)(2,1)S(1)} %pad_maximum_fusion.3), channel_id=1, source_target_pairs={{0,24},{4,28},{8,16},{12,20},{16,8},{20,12},{24,0},{28,4},{1,25},{... | collective-permute-start | bytes 393224 | tf_op jit(solution)/shard_map/ppermute | solution.py:726
  124.0 8.8 %collective-permute-start.38 = (bf16[4,128,256]{2,1,0:T(8,128)(2,1)S(1)}, bf16[4,128,256]{2,1,0:T(8,128)(2,1)S(1)}, u32[]{:S(2)}, u32[]{:S(2)}) collective-permute-start(bf16[4,128,256]{2,1,0:T(8,128)(2,1)S(1)} %get-tuple-element.136), channel_id=1, source_target_pairs={{0,4},{4,0},{8,12},{12,8},{16,20},{20,16},{24,28},{28,24},{1,5},{5... | collective-permute-start | bytes 786440 | tf_op jit(solution)/shard_map/ppermute | solution.py:726
  132.9 7.2 %collective-permute-start.39 = (bf16[128,256]{1,0:T(8,128)(2,1)S(1)}, bf16[128,256]{1,0:T(8,128)(2,1)S(1)}, u32[]{:S(2)}, u32[]{:S(2)}) collective-permute-start(bf16[128,256]{1,0:T(8,128)(2,1)S(1)} %get-tuple-element.156), channel_id=1, source_target_pairs={{0,8},{4,12},{8,0},{12,4},{16,24},{20,28},{24,16},{28,20},{1,9},{5... | collective-permute-start | bytes 196616 | tf_op jit(solution)/shard_map/ppermute | solution.py:726
  133.7 8.3 %collective-permute-start.41 = (bf16[128,256]{1,0:T(8,128)(2,1)S(1)}, bf16[128,256]{1,0:T(8,128)(2,1)S(1)}, u32[]{:S(2)}, u32[]{:S(2)}) collective-permute-start(bf16[128,256]{1,0:T(8,128)(2,1)S(1)} %get-tuple-element.157), channel_id=1, source_target_pairs={{0,24},{4,28},{8,16},{12,20},{16,8},{20,12},{24,0},{28,4},{1,25},{... | collective-permute-start | bytes 196616 | tf_op jit(solution)/shard_map/ppermute | solution.py:726
  135.5 7.1 %collective-permute-start.40 = (bf16[128,256]{1,0:T(8,128)(2,1)S(1)}, bf16[128,256]{1,0:T(8,128)(2,1)S(1)}, u32[]{:S(2)}, u32[]{:S(2)}) collective-permute-start(bf16[128,256]{1,0:T(8,128)(2,1)S(1)} %get-tuple-element.158), channel_id=1, source_target_pairs={{0,16},{4,20},{8,24},{12,28},{16,0},{20,4},{24,8},{28,12},{1,17},{... | collective-permute-start | bytes 196616 | tf_op jit(solution)/shard_map/ppermute | solution.py:726
  137.5 6.5 %collective-permute-start.46 = (bf16[128,256]{1,0:T(8,128)(2,1)S(1)}, bf16[128,256]{1,0:T(8,128)(2,1)S(1)}, u32[]{:S(2)}, u32[]{:S(2)}) collective-permute-start(bf16[128,256]{1,0:T(8,128)(2,1)S(1)} %get-tuple-element.159), channel_id=1, source_target_pairs={{0,8},{4,12},{8,0},{12,4},{16,24},{20,28},{24,16},{28,20},{1,9},{5... | collective-permute-start | bytes 196616 | tf_op jit(solution)/shard_map/ppermute | solution.py:726
  138.5 9.4 %collective-permute-start.48 = (bf16[128,256]{1,0:T(8,128)(2,1)S(1)}, bf16[128,256]{1,0:T(8,128)(2,1)S(1)}, u32[]{:S(2)}, u32[]{:S(2)}) collective-permute-start(bf16[128,256]{1,0:T(8,128)(2,1)S(1)} %get-tuple-element.160), channel_id=1, source_target_pairs={{0,24},{4,28},{8,16},{12,20},{16,8},{20,12},{24,0},{28,4},{1,25},{... | collective-permute-start | bytes 196616 | tf_op jit(solution)/shard_map/ppermute | solution.py:726
  140.1 7.8 %collective-permute-start.47 = (bf16[128,256]{1,0:T(8,128)(2,1)S(1)}, bf16[128,256]{1,0:T(8,128)(2,1)S(1)}, u32[]{:S(2)}, u32[]{:S(2)}) collective-permute-start(bf16[128,256]{1,0:T(8,128)(2,1)S(1)} %get-tuple-element.161), channel_id=1, source_target_pairs={{0,16},{4,20},{8,24},{12,28},{16,0},{20,4},{24,8},{28,12},{1,17},{... | collective-permute-start | bytes 196616 | tf_op jit(solution)/shard_map/ppermute | solution.py:726
  (24 other events, 183.0 us)

commit v3 on v2

--- a/solution.py
+++ b/solution.py
@@ -76,9 +76,8 @@
     count = height // lane
     a = np.arange(lane)
     forward, inverse = [], []
-    for k in range(count):
-        j = a if 2 * k <= count else lane - 1 - a
-        ky = count * j + k
+    for k in range(count // 2 + 1):
+        ky = count * a + k
         table = np.exp(-2j * np.pi * np.outer(ky, a) / height)
         forward.append(np.block([[table.real, -table.imag], [table.imag, table.real]]))
         back = np.conj(table.T) / height
@@ -145,8 +144,8 @@
 
 
 def first_kernel(*refs, lane, per_device, chunk, parts):
-    me_ref, field_hbm, twist_hbm, table_hbm, _ = refs[:5]
-    outs = refs[5:-5]
+    field_hbm, twist_hbm, table_hbm, _ = refs[:4]
+    outs = refs[4:-5]
     field_ref, left_ref, twist_ref, table_ref, sem = refs[-5:]
     rows, width = field_ref.shape[1], field_ref.shape[2]
     tile = rows // parts
@@ -173,10 +172,10 @@
 
         forward_lanes(load, tile, width // lane, lane, twist_ref, left_ref, t * tile)
     table_in.wait()
-    store_slots(outs, left_ref, table_ref, me_ref[0], per_device, lane)
-
-
-def forward_x(me, field, tables, lane, devices, chunk, chunks, pieces, after):
+    store_slots(outs, left_ref, table_ref, lax.axis_index("rows"), per_device, lane)
+
+
+def forward_x(field, tables, lane, devices, chunk, chunks, pieces, after):
     _, rows, width = field.shape
     blocks = width // lane
     per_device = blocks // devices
@@ -187,7 +186,7 @@
         functools.partial(
             first_kernel, lane=lane, per_device=per_device, chunk=chunk, parts=parts
         ),
-        in_specs=[SMEM, ANY, ANY, ANY, pl.BlockSpec(memory_space=pl.ANY)],
+        in_specs=[ANY, ANY, ANY, pl.BlockSpec(memory_space=pl.ANY)],
         out_specs=[FULL] * (devices * pieces),
         out_shape=[shape] * (devices * pieces),
         scratch_shapes=[
@@ -200,7 +199,7 @@
         compiler_params=params(60 * 1024 * 1024),
         cost_estimate=cost(rows * width * 4000, rows * width * 12),
         name="forward_x",
-    )(me, field, tables[2], tables[0], after)
+    )(field, tables[2], tables[0], after)
     return [made[p * devices : (p + 1) * devices] for p in range(pieces)]
 
 
@@ -385,20 +384,25 @@
             )
             for k in range(count):
                 x_ref[k, pl.ds(at, sub), here] = real[k].astype(BF16)
-                x_ref[k, pl.ds(lane + at, sub), here] = imag[k].astype(BF16)
+                value = -imag[k] if 2 * k > count else imag[k]
+                x_ref[k, pl.ds(lane + at, sub), here] = value.astype(BF16)
             return carry
 
         lax.fori_loop(0, lane // sub, load_body, 0)
 
     for k in range(count):
         same = k if 2 * k <= count else count - k
-        y = dot(forward_ref[k], x_ref[k])
+        y = dot(forward_ref[same], x_ref[k])
         yr, yi = y[:lane], y[lane:]
         ur, ui = u_ref[same, 0:lane, :], u_ref[same, lane:pair, :]
-        z_ref[k, 0:lane, :] = (yr * ur - yi * ui).astype(BF16)
-        z_ref[k, lane:pair, :] = (yr * ui + yi * ur).astype(BF16)
+        if same == k:
+            z_ref[k, 0:lane, :] = (yr * ur - yi * ui).astype(BF16)
+            z_ref[k, lane:pair, :] = (yr * ui + yi * ur).astype(BF16)
+        else:
+            z_ref[k, 0:lane, :] = (yr * ur + yi * ui).astype(BF16)
+            z_ref[k, lane:pair, :] = (yi * ur - yr * ui).astype(BF16)
     for k in range(count):
-        w_ref[k] = dot(inverse_ref[k], z_ref[k])
+        w_ref[k] = dot(inverse_ref[k if 2 * k <= count else count - k], z_ref[k])
 
     for c in range(columns):
         here = slice(c * lane, (c + 1) * lane)
@@ -407,6 +411,7 @@
             at = pl.multiple_of(i * sub, sub)
             real = [w_ref[k, pl.ds(at, sub), here] for k in range(count)]
             imag = [w_ref[k, pl.ds(lane + at, sub), here] for k in range(count)]
+            imag = [-im if 2 * k > count else im for k, im in enumerate(imag)]
             real, imag = small_dft(real, imag, 1)
             leave(
                 at,
@@ -572,9 +577,9 @@
     gr, gi = factor_ref[0], factor_ref[1]
     sub = 16
 
-    def correct(i, carry):
+    def correct(i, carry, group):
         at = pl.multiple_of(i * sub, sub)
-        for b in range(blocks):
+        for b in group:
             here = slice(b * lane, (b + 1) * lane)
             weight = coef_ref[pl.ds(at, sub), here].astype(F32)
             centre, curve = [], []
@@ -591,9 +596,6 @@
             left_ref[b, pl.ds(at, sub), lane:pair] = im.astype(BF16)
         return carry
 
-    lax.fori_loop(0, rows // sub, correct, 0)
-    block_copy.wait()
-    leaving = []
     half, _, share = kept_ref.shape
     stride = share // lane
     if stride:
@@ -603,45 +605,54 @@
         ]
     else:
         order = list(range(blocks))
-    even = None
-    for b in order:
-        here = slice(b * lane, (b + 1) * lane)
-        br, bi = block_ref[0, b], block_ref[1, b]
-        square = jnp.concatenate(
-            [jnp.concatenate([br, bi], axis=1), jnp.concatenate([-bi, br], axis=1)], axis=0
-        )
-        change = dot(left_ref[b], square)
-        re = p_ref[0, :, here] + change[:, 0:lane]
-        im = p_ref[1, :, here] + change[:, lane:pair]
-        if not stride:
-            per_tile = lane // share
-            for piece in range(per_tile):
-                owner = b * per_tile + piece
-                value = re[:, piece * share : (piece + 1) * share].astype(BF16)
-                place = lax.bitwise_xor(jnp.int32(owner // 2), me_ref[2])
-
-                @pl.when(me_ref[1] == owner % 2)
-                def _(place=place, value=value):
-                    kept_ref[place] = value
-
-                @pl.when(me_ref[1] != owner % 2)
-                def _(place=place, value=value):
-                    sent_ref[place] = value
-        elif (b // stride) % 2 == 0:
-            even = re
-        else:
-            place = lax.bitwise_xor(jnp.int32(b // stride // 2), me_ref[2])
-            cols = slice((b % stride) * lane, (b % stride + 1) * lane)
-            kept_ref[place, :, cols] = jnp.where(me_ref[1] == 0, even, re).astype(BF16)
-            sent_ref[place, :, cols] = jnp.where(me_ref[1] == 0, re, even).astype(BF16)
-        p_ref[0, :, here] = re
-        p_ref[1, :, here] = im
+    steps = 2 if last and stride and half % 2 == 0 else 1
+    leaving = []
+    for step in range(steps):
+        group = order[step * blocks // steps : (step + 1) * blocks // steps]
+        lax.fori_loop(0, rows // sub, functools.partial(correct, group=group), 0)
+        if step == 0:
+            block_copy.wait()
+        even = None
+        for b in group:
+            here = slice(b * lane, (b + 1) * lane)
+            br, bi = block_ref[0, b], block_ref[1, b]
+            square = jnp.concatenate(
+                [jnp.concatenate([br, bi], axis=1), jnp.concatenate([-bi, br], axis=1)], axis=0
+            )
+            change = dot(left_ref[b], square)
+            re = p_ref[0, :, here] + change[:, 0:lane]
+            im = p_ref[1, :, here] + change[:, lane:pair]
+            if not stride:
+                per_tile = lane // share
+                for piece in range(per_tile):
+                    owner = b * per_tile + piece
+                    value = re[:, piece * share : (piece + 1) * share].astype(BF16)
+                    place = lax.bitwise_xor(jnp.int32(owner // 2), me_ref[2])
+
+                    @pl.when(me_ref[1] == owner % 2)
+                    def _(place=place, value=value):
+                        kept_ref[place] = value
+
+                    @pl.when(me_ref[1] != owner % 2)
+                    def _(place=place, value=value):
+                        sent_ref[place] = value
+            elif (b // stride) % 2 == 0:
+                even = re
+            else:
+                place = lax.bitwise_xor(jnp.int32(b // stride // 2), me_ref[2])
+                cols = slice((b % stride) * lane, (b % stride + 1) * lane)
+                mine = me_ref[1] == 0
+                kept_ref[place, :, cols] = jnp.where(mine, even, re).astype(BF16)
+                sent_ref[place, :, cols] = jnp.where(mine, re, even).astype(BF16)
+            p_ref[0, :, here] = re
+            p_ref[1, :, here] = im
         if last:
+            lanes = pl.ds(step * width // steps, width // steps)
             leaving.append(
                 pltpu.make_async_copy(
-                    p_ref.at[:, :, pl.ds(b * lane, lane)],
-                    outs[0].at[:, pl.ds(chunk * rows, rows), pl.ds(b * lane, lane)],
-                    out_sem.at[b],
+                    p_ref.at[:, :, lanes],
+                    outs[0].at[:, pl.ds(chunk * rows, rows), lanes],
+                    out_sem.at[step],
                 )
             )
             leaving[-1].start()
@@ -769,12 +780,11 @@
     fields = []
     for f in range(freq_local):
         factor = correction_factor[:, f]
-        made, behind = [], me
+        made, behind = [], slowness
         for h in range(chunks):
             made.append(
                 forward_x(
-                    me, wavefield[:, f], x_tables, lane, devices, h, chunks, parts if h else 1,
-                    behind,
+                    wavefield[:, f], x_tables, lane, devices, h, chunks, parts if h else 1, behind
                 )
             )
             behind = made[-1][0][0]

time: 167 us -> 164 us (0.982)
  Pallas kernels: 48.2 us -> 43 us
  waiting for transfers between devices: 51 us -> 53.5 us
    pallas_call x4, Pallas kernels: 24.1 us -> 20.2 us  [space(): pl.pallas_call(functools.partial(space_kernel, lane=lane, devices=devices...]
    ppermute x56, waiting for transfers between devices: 51 us -> 53.5 us  [swap(): return lax.ppermute(value, axis, [(i, i ^ distance) for i in range(count)])]
  transfers between devices with their start and end apart: 56 -> 56, of which waited for: 23 -> 23; matrix products, arithmetic and copies ran while one was open for 0% -> 0% of each run, Pallas kernels for 24% -> 22%
where the time goes in v3:
time: 164 us; the launch traced here: 162 us
  starting transfers between devices  60.8 us (37%)
  waiting for transfers between devices  53.5 us (33%)
  Pallas kernels  43 us (26%)
  between operations  1.74 us (1%)
    ppermute x56, starting transfers between devices, swap(): return lax.ppermute(value, axis, [(i, i ^ distance) for i in range(count)])  60.8 us
    ppermute x56, waiting for transfers between devices, swap(): return lax.ppermute(value, axis, [(i, i ^ distance) for i in range(count)])  53.5 us
    pallas_call x4, Pallas kernels, space(): pl.pallas_call(functools.partial(space_kernel, lane=lane, devices=devices...  20.2 us
    pallas_call x4, Pallas kernels, spectral(): pl.pallas_call(functools.partial(spectral_kernel, lane=lane, width=width,...  11.7 us
    pallas_call x2, Pallas kernels, forward_x(): pl.pallas_call(functools.partial(first_kernel, lane=lane, per_device=per_...  6.16 us
    pallas_call x1, Pallas kernels, waves(): pl.pallas_call(functools.partial(wave_kernel, lane=lane, width=width, hei...  4.93 us
  transfers between devices with their start and end apart: 56, of which 23 were waited for; matrix products, arithmetic and copies ran while one was open for 0% of the time, Pallas kernels for 22%

profile of v3, /device:TPU:10, one launch (start us, length us, event | category | flops | bytes accessed | tf_op | source)
XLA Modules:
  0.0 161.7 jit_solution(15412101865566568895)
XLA Ops:
  0.6 3.1 %forward_x.2 = (bf16[128,1024]{1,0:T(8,128)(2,1)}, bf16[128,1024]{1,0:T(8,128)(2,1)}, bf16[128,1024]{1,0:T(8,128)(2,1)}, bf16[128,1024]{1,0:T(8,128)(2,1)}) custom-call(f32[2,256,2048]{2,1,0:T(8,128)} %bitcast.61, f32[2,16,128]{2,1,0:T(8,128)} %constant.53.clone.refs_1_.refs_4_, bf16[256,256]{1,0:T(8,128)(2,1)} %constant.51.clone.refs_2_.refs_6_, f32[2]{0:T(128)} %refs_3_.5), custom_call_target="tpu_custom_call" | custom-call | flops 1048576000 | bytes 3145728 | tf_op jit(solution)/shard_map/forward_x/pallas_call | solution.py:185
  4.3 1.5 collective-permute-start.1
  5.9 1.4 collective-permute-start.2
  7.3 3.1 %forward_x.3 = (bf16[128,512]{1,0:T(8,128)(2,1)}, bf16[128,512]{1,0:T(8,128)(2,1)}, bf16[128,512]{1,0:T(8,128)(2,1)}, bf16[128,512]{1,0:T(8,128)(2,1)}, bf16[128...) custom-call(f32[2,256,2048]{2,1,0:T(8,128)} %bitcast.62, ...), custom_call_target="tpu_custom_call" | custom-call | flops 1048576000 | bytes 3145728 | tf_op jit(solution)/shard_map/forward_x/pallas_call | solution.py:185
  11.0 1.5 collective-permute-start.4
  13.2 7.3 %collective-permute-done.3.refs_9_ = bf16[128,512]{1,0:T(8,128)(2,1)S(1)} collective-permute-done((bf16[128,512]{1,0:T(8,128)(2,1)}, bf16[128,512]{1,0:T(8,128)(2,1)S(1)}, u32[]{:S(2)}, u32[]{:S(2)}) %collective-permute-start.3) | collective-permute-done | bytes 131104 | tf_op jit(solution)/shard_map/ppermute | solution.py:737
  20.5 1.5 collective-permute-start.5
  23.0 4.9 %waves.1 = (f32[5,256,256]{2,1,0:T(8,128)S(1)}, f32[5,256,256]{2,1,0:T(8,128)S(1)}, f32[5,256,256]{2,1,0:T(8,128)S(1)}, f32[5,256,256]{2,1,0:T(8,128)S(1)}) custom-call(s32[3]{0:T(128)S(1)} %pad_add_fusion.me_ref.refs_0_, f32[2]{0:T(128)S(1)} %multiply_multiply_fusion.squared_ref, bf16[128,512]{1,0:T(8,128)(2,1)S(1)} %copy-done.8), custom_call_target="tpu_custom_call" | custom-call | flops 4194304000 | bytes 8388608 | tf_op jit(solution)/shard_map/waves/pallas_call | solution.py:274
  27.9 1.6 collective-permute-start.9
  30.0 1.5 collective-permute-start.11
  31.5 2.8 %spectral.4 = (bf16[144,512]{1,0:T(8,128)(2,1)S(1)}, bf16[144,512]{1,0:T(8,128)(2,1)S(1)}, bf16[144,512]{1,0:T(8,128)(2,1)S(1)}, bf16[144,512]{1,0:T(8,128)(2,1)...) custom-call(s32[3]{0:T(128)S(1)} %pad_add_fusion.me_ref.refs_0_, ...), custom_call_target="tpu_custom_call" | custom-call | flops 2097152000 | bytes 4194304 | tf_op jit(solution)/shard_map/spectral/pallas_call | solution.py:481
  34.4 1.6 collective-permute-start.6
  36.5 1.5 collective-permute-start.8
  38.0 2.9 %spectral.5 = (bf16[144,512]{1,0:T(8,128)(2,1)S(1)}, bf16[144,512]{1,0:T(8,128)(2,1)S(1)}, bf16[144,512]{1,0:T(8,128)(2,1)S(1)}, bf16[144,512]{1,0:T(8,128)(2,1)...) custom-call(s32[3]{0:T(128)S(1)} %pad_add_fusion.me_ref.refs_0_, ...), custom_call_target="tpu_custom_call" | custom-call | flops 2097152000 | bytes 4194304 | tf_op jit(solution)/shard_map/spectral/pallas_call | solution.py:481
  41.0 1.6 collective-permute-start.12
  43.0 1.5 collective-permute-start.14
  44.5 1.5 collective-permute-start.16
  47.7 1.4 collective-permute-start.18
  49.2 1.9 %collective-permute-done.13.refs_13_ = bf16[144,512]{1,0:T(8,128)(2,1)S(1)} collective-permute-done((bf16[144,512]{1,0:T(8,128)(2,1)S(1)}, bf16[144,512]{1,0:T(8,128)(2,1)S(1)}, u32[]{:S(2)}, u32[]{:S(2)}) %collective-permute-start.13) | collective-permute-done | bytes 147488 | tf_op jit(solution)/shard_map/ppermute | solution.py:737
  51.1 5.1 %space.2 = (bf16[128,1024]{1,0:T(8,128)(2,1)S(1)}, bf16[128,1024]{1,0:T(8,128)(2,1)S(1)}, bf16[128,1024]{1,0:T(8,128)(2,1)S(1)}, bf16[128,1024]{1,0:T(8,128)(2,1...) custom-call(s32[3]{0:T(128)S(1)} %pad_add_fusion.me_ref.refs_0_, ...), custom_call_target="tpu_custom_call" | custom-call | flops 2097152000 | bytes 3145728 | tf_op jit(solution)/shard_map/space/pallas_call | solution.py:703
  56.5 4.0 %collective-permute-done.17.refs_9_ = bf16[128,1024]{1,0:T(8,128)(2,1)S(1)} collective-permute-done((bf16[128,1024]{1,0:T(8,128)(2,1)S(1)}, bf16[128,1024]{1,0:T(8,128)(2,1)S(1)}, u32[]{:S(2)}, u32[]{:S(2)}) %collective-permute-start.17) | collective-permute-done | bytes 262176 | tf_op jit(solution)/shard_map/ppermute | solution.py:737
  60.5 5.0 %space.3 = (bf16[128,512]{1,0:T(8,128)(2,1)S(1)}, bf16[128,512]{1,0:T(8,128)(2,1)S(1)}, bf16[128,512]{1,0:T(8,128)(2,1)S(1)}, bf16[128,512]{1,0:T(8,128)(2,1)S(1...) custom-call(s32[3]{0:T(128)S(1)} %pad_add_fusion.me_ref.refs_0_, ...), custom_call_target="tpu_custom_call" | custom-call | flops 2097152000 | bytes 3145728 | tf_op jit(solution)/shard_map/space/pallas_call | solution.py:703
  65.8 1.8 %collective-permute-start.23 = (bf16[128,1024]{1,0:T(8,128)(2,1)S(1)}, bf16[128,1024]{1,0:T(8,128)(2,1)S(1)}, u32[]{:S(2)}, u32[]{:S(2)}) collective-permute-start(bf16[128,1024]{1,0:T(8,128)(2,1)S(1)} %get-tuple-element.111), channel_id=1, source_target_pairs={{0,1},{1,0},{2,3},{3,2},{4,5},{5,4},{6,7},{7,6},{8,9},{9,8},{10,11... | collective-permute-start | bytes 786440 | tf_op jit(solution)/shard_map/ppermute | solution.py:737
  69.3 1.4 collective-permute-start.27
  73.0 10.9 %collective-permute-done.27.refs_10_ = bf16[128,512]{1,0:T(8,128)(2,1)S(1)} collective-permute-done((bf16[128,512]{1,0:T(8,128)(2,1)S(1)}, bf16[128,512]{1,0:T(8,128)(2,1)S(1)}, u32[]{:S(2)}, u32[]{:S(2)}) %collective-permute-start.27) | collective-permute-done | bytes 131104 | tf_op jit(solution)/shard_map/ppermute | solution.py:737
  85.5 1.9 %collective-permute-start.34 = (bf16[128,512]{1,0:T(8,128)(2,1)S(1)}, bf16[128,512]{1,0:T(8,128)(2,1)S(1)}, u32[]{:S(2)}, u32[]{:S(2)}) collective-permute-start(bf16[128,512]{1,0:T(8,128)(2,1)S(1)} %get-tuple-element.126), channel_id=1, source_target_pairs={{0,3},{1,2},{2,1},{3,0},{4,7},{5,6},{6,5},{7,4},{8,11},{9,10},{10,... | collective-permute-start | bytes 393224 | tf_op jit(solution)/shard_map/ppermute | solution.py:737
  87.5 2.8 %spectral.6 = (bf16[144,512]{1,0:T(8,128)(2,1)S(1)}, bf16[144,512]{1,0:T(8,128)(2,1)S(1)}, bf16[144,512]{1,0:T(8,128)(2,1)S(1)}, bf16[144,512]{1,0:T(8,128)(2,1)...) custom-call(s32[3]{0:T(128)S(1)} %pad_add_fusion.me_ref.refs_0_, ...), custom_call_target="tpu_custom_call" | custom-call | flops 2097152000 | bytes 4194304 | tf_op jit(solution)/shard_map/spectral/pallas_call | solution.py:481
  90.3 3.0 %collective-permute-done.34.refs_11_ = bf16[128,512]{1,0:T(8,128)(2,1)S(1)} collective-permute-done((bf16[128,512]{1,0:T(8,128)(2,1)S(1)}, bf16[128,512]{1,0:T(8,128)(2,1)S(1)}, u32[]{:S(2)}, u32[]{:S(2)}) %collective-permute-start.34) | collective-permute-done | bytes 131104 | tf_op jit(solution)/shard_map/ppermute | solution.py:737
  93.3 3.1 %spectral.7 = (bf16[144,512]{1,0:T(8,128)(2,1)S(1)}, bf16[144,512]{1,0:T(8,128)(2,1)S(1)}, bf16[144,512]{1,0:T(8,128)(2,1)S(1)}, bf16[144,512]{1,0:T(8,128)(2,1)...) custom-call(s32[3]{0:T(128)S(1)} %pad_add_fusion.me_ref.refs_0_, ...), custom_call_target="tpu_custom_call" | custom-call | flops 2097152000 | bytes 4194304 | tf_op jit(solution)/shard_map/spectral/pallas_call | solution.py:481
  101.2 1.3 collective-permute-start.30
  103.2 1.6 %collective-permute-start.31 = (bf16[144,512]{1,0:T(8,128)(2,1)S(1)}, bf16[144,512]{1,0:T(8,128)(2,1)S(1)}, u32[]{:S(2)}, u32[]{:S(2)}) collective-permute-start(bf16[144,512]{1,0:T(8,128)(2,1)S(1)} %get-tuple-element.121), channel_id=1, source_target_pairs={{0,3},{1,2},{2,1},{3,0},{4,7},{5,6},{6,5},{7,4},{8,11},{9,10},{10,... | collective-permute-start | bytes 442376 | tf_op jit(solution)/shard_map/ppermute | solution.py:737
  104.8 2.4 %collective-permute-done.36.refs_13_ = bf16[144,512]{1,0:T(8,128)(2,1)S(1)} collective-permute-done((bf16[144,512]{1,0:T(8,128)(2,1)S(1)}, bf16[144,512]{1,0:T(8,128)(2,1)S(1)}, u32[]{:S(2)}, u32[]{:S(2)}) %collective-permute-start.36) | collective-permute-done | bytes 147488 | tf_op jit(solution)/shard_map/ppermute | solution.py:737
  108.2 1.3 collective-permute-done.29.refs_8_
  110.2 2.5 %collective-permute-done.30.refs_9_ = bf16[144,512]{1,0:T(8,128)(2,1)S(1)} collective-permute-done((bf16[144,512]{1,0:T(8,128)(2,1)S(1)}, bf16[144,512]{1,0:T(8,128)(2,1)S(1)}, u32[]{:S(2)}, u32[]{:S(2)}) %collective-permute-start.30) | collective-permute-done | bytes 147488 | tf_op jit(solution)/shard_map/ppermute | solution.py:737
  113.1 2.6 %collective-permute-start.21 = (bf16[256,256]{1,0:T(8,128)(2,1)S(1)}, bf16[256,256]{1,0:T(8,128)(2,1)S(1)}, u32[]{:S(2)}, u32[]{:S(2)}) collective-permute-start(bf16[256,256]{1,0:T(8,128)(2,1)S(1)} %pad_maximum_fusion.2), channel_id=1, source_target_pairs={{0,16},{4,20},{8,24},{12,28},{16,0},{20,4},{24,8},{28,12},{1,17},{... | collective-permute-start | bytes 393224 | tf_op jit(solution)/shard_map/ppermute | solution.py:737
  115.7 5.1 %space_last.2 = (f32[2,256,2048]{2,1,0:T(8,128)}, bf16[4,128,256]{2,1,0:T(8,128)(2,1)S(1)}, bf16[4,128,256]{2,1,0:T(8,128)(2,1)S(1)}, f32[2,16,2048]{2,1,0:T(8,128)S(1)}) custom-call(s32[3]{0:T(128)S(1)} %pad_add_fusion.me_ref.refs_0_, f32[2]{0:T(128)S(1)} %bitcast.59, bf16[256,2048]{1,0:T(8,128)(2,1)S(1)} %copy-done.1, ...), custom_call_target="tpu_custom_call" | custom-call | flops 2097152000 | bytes 3145728 | tf_op jit(solution)/shard_map/space_last/pallas_call | solution.py:703
  120.8 1.6 collective-permute-done.21
  122.3 2.1 %collective-permute-done.22 = bf16[256,256]{1,0:T(8,128)(2,1)S(1)} collective-permute-done((bf16[256,256]{1,0:T(8,128)(2,1)S(1)}, bf16[256,256]{1,0:T(8,128)(2,1)S(1)}, u32[]{:S(2)}, u32[]{:S(2)}) %collective-permute-start.22) | collective-permute-done | bytes 131104 | tf_op jit(solution)/shard_map/ppermute | solution.py:737
  124.6 5.0 %space_last.3 = (f32[2,256,2048]{2,1,0:T(8,128)}, bf16[4,128,256]{2,1,0:T(8,128)(2,1)S(1)}, bf16[4,128,256]{2,1,0:T(8,128)(2,1)S(1)}) custom-call(s32[3]{0:T(128)S(1)} %pad_add_fusion.me_ref.refs_0_, f32[2]{0:T(128)S(1)} %bitcast.60, bf16[256,2048]{1,0:T(8,128)(2,1)S(1)} %copy-done.1, ...), custom_call_target="tpu_custom_call", output_to_operand_aliasing={{0}: (12, {})} | custom-call | flops 2097152000 | bytes 3145728 | tf_op jit(solution)/shard_map/space_last/pallas_call | solution.py:703
  130.4 2.0 %collective-permute-start.41 = (bf16[128,256]{1,0:T(8,128)(2,1)S(1)}, bf16[128,256]{1,0:T(8,128)(2,1)S(1)}, u32[]{:S(2)}, u32[]{:S(2)}) collective-permute-start(bf16[128,256]{1,0:T(8,128)(2,1)S(1)} %get-tuple-element.157), channel_id=1, source_target_pairs={{0,24},{4,28},{8,16},{12,20},{16,8},{20,12},{24,0},{28,4},{1,25},{... | collective-permute-start | bytes 196616 | tf_op jit(solution)/shard_map/ppermute | solution.py:737
  132.4 1.8 %collective-permute-start.40 = (bf16[128,256]{1,0:T(8,128)(2,1)S(1)}, bf16[128,256]{1,0:T(8,128)(2,1)S(1)}, u32[]{:S(2)}, u32[]{:S(2)}) collective-permute-start(bf16[128,256]{1,0:T(8,128)(2,1)S(1)} %get-tuple-element.158), channel_id=1, source_target_pairs={{0,16},{4,20},{8,24},{12,28},{16,0},{20,4},{24,8},{28,12},{1,17},{... | collective-permute-start | bytes 196616 | tf_op jit(solution)/shard_map/ppermute | solution.py:737
  135.4 1.5 collective-permute-start.48
  137.0 1.8 %collective-permute-start.47 = (bf16[128,256]{1,0:T(8,128)(2,1)S(1)}, bf16[128,256]{1,0:T(8,128)(2,1)S(1)}, u32[]{:S(2)}, u32[]{:S(2)}) collective-permute-start(bf16[128,256]{1,0:T(8,128)(2,1)S(1)} %get-tuple-element.161), channel_id=1, source_target_pairs={{0,16},{4,20},{8,24},{12,28},{16,0},{20,4},{24,8},{28,12},{1,17},{... | collective-permute-start | bytes 196616 | tf_op jit(solution)/shard_map/ppermute | solution.py:737
  140.8 3.9 %collective-permute-done.48 = bf16[128,256]{1,0:T(8,128)(2,1)S(1)} collective-permute-done((bf16[128,256]{1,0:T(8,128)(2,1)S(1)}, bf16[128,256]{1,0:T(8,128)(2,1)S(1)}, u32[]{:S(2)}, u32[]{:S(2)}) %collective-permute-start.48) | collective-permute-done | bytes 65568 | tf_op jit(solution)/shard_map/ppermute | solution.py:737
  147.4 3.9 %collective-permute-start.51 = (f32[2]{0:T(128)S(1)}, f32[2]{0:T(128)S(1)}, u32[]{:S(2)}, u32[]{:S(2)}) collective-permute-start(f32[2]{0:T(128)S(1)} %add.82), channel_id=1, source_target_pairs={{0,16},{4,20},{8,24},{12,28},{16,0},{20,4},{24,8},{28,12},{1,17},{... | collective-permute-start | bytes 32 | tf_op jit(solution)/shard_map/ppermute | solution.py:737
  151.3 1.5 collective-permute-done.51
  152.9 2.0 %collective-permute-done.50 = f32[2]{0:T(128)S(1)} collective-permute-done((f32[2]{0:T(128)S(1)}, f32[2]{0:T(128)S(1)}, u32[]{:S(2)}, u32[]{:S(2)}) %collective-permute-start.50) | collective-permute-done | bytes 40 | tf_op jit(solution)/shard_map/ppermute | solution.py:737
  154.9 1.6 collective-permute-start.55
  (127 shorter events, 31.2 us)
Async XLA Ops:
  3.7 26.3 %collective-permute-start = (bf16[128,1024]{1,0:T(8,128)(2,1)}, bf16[128,1024]{1,0:T(8,128)(2,1)S(1)}, u32[]{:S(2)}, u32[]{:S(2)}) collective-permute-start(bf16[128,1024]{1,0:T(8,128)(2,1)} %get-tuple-element.77), channel_id=1, source_target_pairs={{0,1},{1,0},{2,3},{3,2},{4,5},{5,4},{6,7},{7,6},{8,9},{9,8},{10,11... | collective-permute-start | bytes 786440 | tf_op jit(solution)/shard_map/ppermute | solution.py:737
  4.3 27.2 %collective-permute-start.1 = (bf16[128,1024]{1,0:T(8,128)(2,1)}, bf16[128,1024]{1,0:T(8,128)(2,1)S(1)}, u32[]{:S(2)}, u32[]{:S(2)}) collective-permute-start(bf16[128,1024]{1,0:T(8,128)(2,1)} %get-tuple-element.78), channel_id=1, source_target_pairs={{0,2},{1,3},{2,0},{3,1},{4,6},{5,7},{6,4},{7,5},{8,10},{9,11},{10,... | collective-permute-start | bytes 786440 | tf_op jit(solution)/shard_map/ppermute | solution.py:737
  5.9 25.6 %collective-permute-start.2 = (bf16[128,1024]{1,0:T(8,128)(2,1)}, bf16[128,1024]{1,0:T(8,128)(2,1)S(1)}, u32[]{:S(2)}, u32[]{:S(2)}) collective-permute-start(bf16[128,1024]{1,0:T(8,128)(2,1)} %get-tuple-element.79), channel_id=1, source_target_pairs={{0,3},{1,2},{2,1},{3,0},{4,7},{5,6},{6,5},{7,4},{8,11},{9,10},{10,... | collective-permute-start | bytes 786440 | tf_op jit(solution)/shard_map/ppermute | solution.py:737
  10.4 10.2 %collective-permute-start.3 = (bf16[128,512]{1,0:T(8,128)(2,1)}, bf16[128,512]{1,0:T(8,128)(2,1)S(1)}, u32[]{:S(2)}, u32[]{:S(2)}) collective-permute-start(bf16[128,512]{1,0:T(8,128)(2,1)} %get-tuple-element.80), channel_id=1, source_target_pairs={{0,1},{1,0},{2,3},{3,2},{4,5},{5,4},{6,7},{7,6},{8,9},{9,8},{10,11... | collective-permute-start | bytes 393224 | tf_op jit(solution)/shard_map/ppermute | solution.py:737
  11.0 17.0 %collective-permute-start.4 = (bf16[128,512]{1,0:T(8,128)(2,1)}, bf16[128,512]{1,0:T(8,128)(2,1)S(1)}, u32[]{:S(2)}, u32[]{:S(2)}) collective-permute-start(bf16[128,512]{1,0:T(8,128)(2,1)} %get-tuple-element.81), channel_id=1, source_target_pairs={{0,2},{1,3},{2,0},{3,1},{4,6},{5,7},{6,4},{7,5},{8,10},{9,11},{10,... | collective-permute-start | bytes 393224 | tf_op jit(solution)/shard_map/ppermute | solution.py:737
  20.5 9.0 %collective-permute-start.5 = (bf16[128,512]{1,0:T(8,128)(2,1)}, bf16[128,512]{1,0:T(8,128)(2,1)S(1)}, u32[]{:S(2)}, u32[]{:S(2)}) collective-permute-start(bf16[128,512]{1,0:T(8,128)(2,1)} %get-tuple-element.82), channel_id=1, source_target_pairs={{0,3},{1,2},{2,1},{3,0},{4,7},{5,6},{6,5},{7,4},{8,11},{9,10},{10,... | collective-permute-start | bytes 393224 | tf_op jit(solution)/shard_map/ppermute | solution.py:737
  27.9 8.5 %collective-permute-start.9 = (bf16[128,512]{1,0:T(8,128)(2,1)S(1)}, bf16[128,512]{1,0:T(8,128)(2,1)S(1)}, u32[]{:S(2)}, u32[]{:S(2)}) collective-permute-start(bf16[128,512]{1,0:T(8,128)(2,1)S(1)} %copy-done.14), channel_id=1, source_target_pairs={{0,1},{1,0},{2,3},{3,2},{4,5},{5,4},{6,7},{7,6},{8,9},{9,8},{10,11... | collective-permute-start | bytes 393224 | tf_op jit(solution)/shard_map/ppermute | solution.py:737
  29.5 8.5 %collective-permute-start.10 = (bf16[128,512]{1,0:T(8,128)(2,1)S(1)}, bf16[128,512]{1,0:T(8,128)(2,1)S(1)}, u32[]{:S(2)}, u32[]{:S(2)}) collective-permute-start(bf16[128,512]{1,0:T(8,128)(2,1)S(1)} %copy-done.13), channel_id=1, source_target_pairs={{0,2},{1,3},{2,0},{3,1},{4,6},{5,7},{6,4},{7,5},{8,10},{9,11},{10,... | collective-permute-start | bytes 393224 | tf_op jit(solution)/shard_map/ppermute | solution.py:737
  30.0 7.9 %collective-permute-start.11 = (bf16[128,512]{1,0:T(8,128)(2,1)S(1)}, bf16[128,512]{1,0:T(8,128)(2,1)S(1)}, u32[]{:S(2)}, u32[]{:S(2)}) collective-permute-start(bf16[128,512]{1,0:T(8,128)(2,1)S(1)} %copy-done.12), channel_id=1, source_target_pairs={{0,3},{1,2},{2,1},{3,0},{4,7},{5,6},{6,5},{7,4},{8,11},{9,10},{10,... | collective-permute-start | bytes 393224 | tf_op jit(solution)/shard_map/ppermute | solution.py:737
  34.4 8.6 %collective-permute-start.6 = (bf16[144,512]{1,0:T(8,128)(2,1)S(1)}, bf16[144,512]{1,0:T(8,128)(2,1)S(1)}, u32[]{:S(2)}, u32[]{:S(2)}) collective-permute-start(bf16[144,512]{1,0:T(8,128)(2,1)S(1)} %get-tuple-element.84), channel_id=1, source_target_pairs={{0,1},{1,0},{2,3},{3,2},{4,5},{5,4},{6,7},{7,6},{8,9},{9,8},{10,11... | collective-permute-start | bytes 442376 | tf_op jit(solution)/shard_map/ppermute | solution.py:737
  35.9 8.6 %collective-permute-start.7 = (bf16[144,512]{1,0:T(8,128)(2,1)S(1)}, bf16[144,512]{1,0:T(8,128)(2,1)S(1)}, u32[]{:S(2)}, u32[]{:S(2)}) collective-permute-start(bf16[144,512]{1,0:T(8,128)(2,1)S(1)} %get-tuple-element.85), channel_id=1, source_target_pairs={{0,2},{1,3},{2,0},{3,1},{4,6},{5,7},{6,4},{7,5},{8,10},{9,11},{10,... | collective-permute-start | bytes 442376 | tf_op jit(solution)/shard_map/ppermute | solution.py:737
  36.5 9.5 %collective-permute-start.8 = (bf16[144,512]{1,0:T(8,128)(2,1)S(1)}, bf16[144,512]{1,0:T(8,128)(2,1)S(1)}, u32[]{:S(2)}, u32[]{:S(2)}) collective-permute-start(bf16[144,512]{1,0:T(8,128)(2,1)S(1)} %get-tuple-element.86), channel_id=1, source_target_pairs={{0,3},{1,2},{2,1},{3,0},{4,7},{5,6},{6,5},{7,4},{8,11},{9,10},{10,... | collective-permute-start | bytes 442376 | tf_op jit(solution)/shard_map/ppermute | solution.py:737
  41.0 6.8 %collective-permute-start.12 = (bf16[144,512]{1,0:T(8,128)(2,1)S(1)}, bf16[144,512]{1,0:T(8,128)(2,1)S(1)}, u32[]{:S(2)}, u32[]{:S(2)}) collective-permute-start(bf16[144,512]{1,0:T(8,128)(2,1)S(1)} %get-tuple-element.97), channel_id=1, source_target_pairs={{0,1},{1,0},{2,3},{3,2},{4,5},{5,4},{6,7},{7,6},{8,9},{9,8},{10,11... | collective-permute-start | bytes 442376 | tf_op jit(solution)/shard_map/ppermute | solution.py:737
  42.5 8.6 %collective-permute-start.13 = (bf16[144,512]{1,0:T(8,128)(2,1)S(1)}, bf16[144,512]{1,0:T(8,128)(2,1)S(1)}, u32[]{:S(2)}, u32[]{:S(2)}) collective-permute-start(bf16[144,512]{1,0:T(8,128)(2,1)S(1)} %get-tuple-element.98), channel_id=1, source_target_pairs={{0,2},{1,3},{2,0},{3,1},{4,6},{5,7},{6,4},{7,5},{8,10},{9,11},{10,... | collective-permute-start | bytes 442376 | tf_op jit(solution)/shard_map/ppermute | solution.py:737
  43.0 8.0 %collective-permute-start.14 = (bf16[144,512]{1,0:T(8,128)(2,1)S(1)}, bf16[144,512]{1,0:T(8,128)(2,1)S(1)}, u32[]{:S(2)}, u32[]{:S(2)}) collective-permute-start(bf16[144,512]{1,0:T(8,128)(2,1)S(1)} %get-tuple-element.99), channel_id=1, source_target_pairs={{0,3},{1,2},{2,1},{3,0},{4,7},{5,6},{6,5},{7,4},{8,11},{9,10},{10,... | collective-permute-start | bytes 442376 | tf_op jit(solution)/shard_map/ppermute | solution.py:737
  44.5 12.0 %collective-permute-start.16 = (bf16[128,1024]{1,0:T(8,128)(2,1)S(1)}, bf16[128,1024]{1,0:T(8,128)(2,1)S(1)}, u32[]{:S(2)}, u32[]{:S(2)}) collective-permute-start(bf16[128,1024]{1,0:T(8,128)(2,1)S(1)} %get-tuple-element.103), channel_id=1, source_target_pairs={{0,1},{1,0},{2,3},{3,2},{4,5},{5,4},{6,7},{7,6},{8,9},{9,8},{10,11... | collective-permute-start | bytes 786440 | tf_op jit(solution)/shard_map/ppermute | solution.py:737
  46.0 14.5 %collective-permute-start.17 = (bf16[128,1024]{1,0:T(8,128)(2,1)S(1)}, bf16[128,1024]{1,0:T(8,128)(2,1)S(1)}, u32[]{:S(2)}, u32[]{:S(2)}) collective-permute-start(bf16[128,1024]{1,0:T(8,128)(2,1)S(1)} %get-tuple-element.104), channel_id=1, source_target_pairs={{0,2},{1,3},{2,0},{3,1},{4,6},{5,7},{6,4},{7,5},{8,10},{9,11},{10,... | collective-permute-start | bytes 786440 | tf_op jit(solution)/shard_map/ppermute | solution.py:737
  47.7 12.8 %collective-permute-start.18 = (bf16[128,1024]{1,0:T(8,128)(2,1)S(1)}, bf16[128,1024]{1,0:T(8,128)(2,1)S(1)}, u32[]{:S(2)}, u32[]{:S(2)}) collective-permute-start(bf16[128,1024]{1,0:T(8,128)(2,1)S(1)} %get-tuple-element.105), channel_id=1, source_target_pairs={{0,3},{1,2},{2,1},{3,0},{4,7},{5,6},{6,5},{7,4},{8,11},{9,10},{10,... | collective-permute-start | bytes 786440 | tf_op jit(solution)/shard_map/ppermute | solution.py:737
  65.5 6.4 %collective-permute-start.26 = (bf16[128,512]{1,0:T(8,128)(2,1)S(1)}, bf16[128,512]{1,0:T(8,128)(2,1)S(1)}, u32[]{:S(2)}, u32[]{:S(2)}) collective-permute-start(bf16[128,512]{1,0:T(8,128)(2,1)S(1)} %get-tuple-element.115), channel_id=1, source_target_pairs={{0,1},{1,0},{2,3},{3,2},{4,5},{5,4},{6,7},{7,6},{8,9},{9,8},{10,11... | collective-permute-start | bytes 393224 | tf_op jit(solution)/shard_map/ppermute | solution.py:737
  65.8 18.5 %collective-permute-start.23 = (bf16[128,1024]{1,0:T(8,128)(2,1)S(1)}, bf16[128,1024]{1,0:T(8,128)(2,1)S(1)}, u32[]{:S(2)}, u32[]{:S(2)}) collective-permute-start(bf16[128,1024]{1,0:T(8,128)(2,1)S(1)} %get-tuple-element.111), channel_id=1, source_target_pairs={{0,1},{1,0},{2,3},{3,2},{4,5},{5,4},{6,7},{7,6},{8,9},{9,8},{10,11... | collective-permute-start | bytes 786440 | tf_op jit(solution)/shard_map/ppermute | solution.py:737
  67.6 17.9 %collective-permute-start.24 = (bf16[128,1024]{1,0:T(8,128)(2,1)S(1)}, bf16[128,1024]{1,0:T(8,128)(2,1)S(1)}, u32[]{:S(2)}, u32[]{:S(2)}) collective-permute-start(bf16[128,1024]{1,0:T(8,128)(2,1)S(1)} %get-tuple-element.112), channel_id=1, source_target_pairs={{0,2},{1,3},{2,0},{3,1},{4,6},{5,7},{6,4},{7,5},{8,10},{9,11},{10,... | collective-permute-start | bytes 786440 | tf_op jit(solution)/shard_map/ppermute | solution.py:737
  68.6 18.8 %collective-permute-start.25 = (bf16[128,1024]{1,0:T(8,128)(2,1)S(1)}, bf16[128,1024]{1,0:T(8,128)(2,1)S(1)}, u32[]{:S(2)}, u32[]{:S(2)}) collective-permute-start(bf16[128,1024]{1,0:T(8,128)(2,1)S(1)} %get-tuple-element.113), channel_id=1, source_target_pairs={{0,3},{1,2},{2,1},{3,0},{4,7},{5,6},{6,5},{7,4},{8,11},{9,10},{10,... | collective-permute-start | bytes 786440 | tf_op jit(solution)/shard_map/ppermute | solution.py:737
  69.3 14.6 %collective-permute-start.27 = (bf16[128,512]{1,0:T(8,128)(2,1)S(1)}, bf16[128,512]{1,0:T(8,128)(2,1)S(1)}, u32[]{:S(2)}, u32[]{:S(2)}) collective-permute-start(bf16[128,512]{1,0:T(8,128)(2,1)S(1)} %get-tuple-element.116), channel_id=1, source_target_pairs={{0,2},{1,3},{2,0},{3,1},{4,6},{5,7},{6,4},{7,5},{8,10},{9,11},{10,... | collective-permute-start | bytes 393224 | tf_op jit(solution)/shard_map/ppermute | solution.py:737
  72.0 12.0 %collective-permute-start.28 = (bf16[128,512]{1,0:T(8,128)(2,1)S(1)}, bf16[128,512]{1,0:T(8,128)(2,1)S(1)}, u32[]{:S(2)}, u32[]{:S(2)}) collective-permute-start(bf16[128,512]{1,0:T(8,128)(2,1)S(1)} %get-tuple-element.117), channel_id=1, source_target_pairs={{0,3},{1,2},{2,1},{3,0},{4,7},{5,6},{6,5},{7,4},{8,11},{9,10},{10,... | collective-permute-start | bytes 393224 | tf_op jit(solution)/shard_map/ppermute | solution.py:737
  83.9 16.0 %collective-permute-start.15 = (bf16[4,128,256]{2,1,0:T(8,128)(2,1)S(1)}, bf16[4,128,256]{2,1,0:T(8,128)(2,1)S(1)}, u32[]{:S(2)}, u32[]{:S(2)}) collective-permute-start(bf16[4,128,256]{2,1,0:T(8,128)(2,1)S(1)} %get-tuple-element.101), channel_id=1, source_target_pairs={{0,4},{4,0},{8,12},{12,8},{16,20},{20,16},{24,28},{28,24},{1,5},{5... | collective-permute-start | bytes 786440 | tf_op jit(solution)/shard_map/ppermute | solution.py:737
  84.0 6.4 %collective-permute-start.32 = (bf16[128,512]{1,0:T(8,128)(2,1)S(1)}, bf16[128,512]{1,0:T(8,128)(2,1)S(1)}, u32[]{:S(2)}, u32[]{:S(2)}) collective-permute-start(bf16[128,512]{1,0:T(8,128)(2,1)S(1)} %get-tuple-element.124), channel_id=1, source_target_pairs={{0,1},{1,0},{2,3},{3,2},{4,5},{5,4},{6,7},{7,6},{8,9},{9,8},{10,11... | collective-permute-start | bytes 393224 | tf_op jit(solution)/shard_map/ppermute | solution.py:737
  84.3 6.0 %collective-permute-start.33 = (bf16[128,512]{1,0:T(8,128)(2,1)S(1)}, bf16[128,512]{1,0:T(8,128)(2,1)S(1)}, u32[]{:S(2)}, u32[]{:S(2)}) collective-permute-start(bf16[128,512]{1,0:T(8,128)(2,1)S(1)} %get-tuple-element.125), channel_id=1, source_target_pairs={{0,2},{1,3},{2,0},{3,1},{4,6},{5,7},{6,4},{7,5},{8,10},{9,11},{10,... | collective-permute-start | bytes 393224 | tf_op jit(solution)/shard_map/ppermute | solution.py:737
  85.5 7.8 %collective-permute-start.34 = (bf16[128,512]{1,0:T(8,128)(2,1)S(1)}, bf16[128,512]{1,0:T(8,128)(2,1)S(1)}, u32[]{:S(2)}, u32[]{:S(2)}) collective-permute-start(bf16[128,512]{1,0:T(8,128)(2,1)S(1)} %get-tuple-element.126), channel_id=1, source_target_pairs={{0,3},{1,2},{2,1},{3,0},{4,7},{5,6},{6,5},{7,4},{8,11},{9,10},{10,... | collective-permute-start | bytes 393224 | tf_op jit(solution)/shard_map/ppermute | solution.py:737
  87.5 13.7 %collective-permute-start.19 = (bf16[4,128,256]{2,1,0:T(8,128)(2,1)S(1)}, bf16[4,128,256]{2,1,0:T(8,128)(2,1)S(1)}, u32[]{:S(2)}, u32[]{:S(2)}) collective-permute-start(bf16[4,128,256]{2,1,0:T(8,128)(2,1)S(1)} %get-tuple-element.108), channel_id=1, source_target_pairs={{0,4},{4,0},{8,12},{12,8},{16,20},{20,16},{24,28},{28,24},{1,5},{5... | collective-permute-start | bytes 786440 | tf_op jit(solution)/shard_map/ppermute | solution.py:737
  96.4 6.8 %collective-permute-start.35 = (bf16[144,512]{1,0:T(8,128)(2,1)S(1)}, bf16[144,512]{1,0:T(8,128)(2,1)S(1)}, u32[]{:S(2)}, u32[]{:S(2)}) collective-permute-start(bf16[144,512]{1,0:T(8,128)(2,1)S(1)} %get-tuple-element.132), channel_id=1, source_target_pairs={{0,1},{1,0},{2,3},{3,2},{4,5},{5,4},{6,7},{7,6},{8,9},{9,8},{10,11... | collective-permute-start | bytes 442376 | tf_op jit(solution)/shard_map/ppermute | solution.py:737
  97.6 9.6 %collective-permute-start.36 = (bf16[144,512]{1,0:T(8,128)(2,1)S(1)}, bf16[144,512]{1,0:T(8,128)(2,1)S(1)}, u32[]{:S(2)}, u32[]{:S(2)}) collective-permute-start(bf16[144,512]{1,0:T(8,128)(2,1)S(1)} %get-tuple-element.133), channel_id=1, source_target_pairs={{0,2},{1,3},{2,0},{3,1},{4,6},{5,7},{6,4},{7,5},{8,10},{9,11},{10,... | collective-permute-start | bytes 442376 | tf_op jit(solution)/shard_map/ppermute | solution.py:737
  98.8 9.0 %collective-permute-start.37 = (bf16[144,512]{1,0:T(8,128)(2,1)S(1)}, bf16[144,512]{1,0:T(8,128)(2,1)S(1)}, u32[]{:S(2)}, u32[]{:S(2)}) collective-permute-start(bf16[144,512]{1,0:T(8,128)(2,1)S(1)} %get-tuple-element.134), channel_id=1, source_target_pairs={{0,3},{1,2},{2,1},{3,0},{4,7},{5,6},{6,5},{7,4},{8,11},{9,10},{10,... | collective-permute-start | bytes 442376 | tf_op jit(solution)/shard_map/ppermute | solution.py:737
  100.0 9.5 %collective-permute-start.29 = (bf16[144,512]{1,0:T(8,128)(2,1)S(1)}, bf16[144,512]{1,0:T(8,128)(2,1)S(1)}, u32[]{:S(2)}, u32[]{:S(2)}) collective-permute-start(bf16[144,512]{1,0:T(8,128)(2,1)S(1)} %get-tuple-element.119), channel_id=1, source_target_pairs={{0,1},{1,0},{2,3},{3,2},{4,5},{5,4},{6,7},{7,6},{8,9},{9,8},{10,11... | collective-permute-start | bytes 442376 | tf_op jit(solution)/shard_map/ppermute | solution.py:737
  101.2 11.5 %collective-permute-start.30 = (bf16[144,512]{1,0:T(8,128)(2,1)S(1)}, bf16[144,512]{1,0:T(8,128)(2,1)S(1)}, u32[]{:S(2)}, u32[]{:S(2)}) collective-permute-start(bf16[144,512]{1,0:T(8,128)(2,1)S(1)} %get-tuple-element.120), channel_id=1, source_target_pairs={{0,2},{1,3},{2,0},{3,1},{4,6},{5,7},{6,4},{7,5},{8,10},{9,11},{10,... | collective-permute-start | bytes 442376 | tf_op jit(solution)/shard_map/ppermute | solution.py:737
  103.2 9.9 %collective-permute-start.31 = (bf16[144,512]{1,0:T(8,128)(2,1)S(1)}, bf16[144,512]{1,0:T(8,128)(2,1)S(1)}, u32[]{:S(2)}, u32[]{:S(2)}) collective-permute-start(bf16[144,512]{1,0:T(8,128)(2,1)S(1)} %get-tuple-element.121), channel_id=1, source_target_pairs={{0,3},{1,2},{2,1},{3,0},{4,7},{5,6},{6,5},{7,4},{8,11},{9,10},{10,... | collective-permute-start | bytes 442376 | tf_op jit(solution)/shard_map/ppermute | solution.py:737
  107.2 8.5 %collective-permute-start.20 = (bf16[256,256]{1,0:T(8,128)(2,1)S(1)}, bf16[256,256]{1,0:T(8,128)(2,1)S(1)}, u32[]{:S(2)}, u32[]{:S(2)}) collective-permute-start(bf16[256,256]{1,0:T(8,128)(2,1)S(1)} %pad_maximum_fusion.1), channel_id=1, source_target_pairs={{0,8},{4,12},{8,0},{12,4},{16,24},{20,28},{24,16},{28,20},{1,9},{5... | collective-permute-start | bytes 393224 | tf_op jit(solution)/shard_map/ppermute | solution.py:737
  107.7 16.8 %collective-permute-start.42 = (bf16[128,1024]{1,0:T(8,128)(2,1)S(1)}, bf16[128,1024]{1,0:T(8,128)(2,1)S(1)}, u32[]{:S(2)}, u32[]{:S(2)}) collective-permute-start(bf16[128,1024]{1,0:T(8,128)(2,1)S(1)} %get-tuple-element.138), channel_id=1, source_target_pairs={{0,1},{1,0},{2,3},{3,2},{4,5},{5,4},{6,7},{7,6},{8,9},{9,8},{10,11... | collective-permute-start | bytes 786440 | tf_op jit(solution)/shard_map/ppermute | solution.py:737
  109.5 15.1 %collective-permute-start.43 = (bf16[128,1024]{1,0:T(8,128)(2,1)S(1)}, bf16[128,1024]{1,0:T(8,128)(2,1)S(1)}, u32[]{:S(2)}, u32[]{:S(2)}) collective-permute-start(bf16[128,1024]{1,0:T(8,128)(2,1)S(1)} %get-tuple-element.139), channel_id=1, source_target_pairs={{0,2},{1,3},{2,0},{3,1},{4,6},{5,7},{6,4},{7,5},{8,10},{9,11},{10,... | collective-permute-start | bytes 786440 | tf_op jit(solution)/shard_map/ppermute | solution.py:737
  112.6 11.9 %collective-permute-start.44 = (bf16[128,1024]{1,0:T(8,128)(2,1)S(1)}, bf16[128,1024]{1,0:T(8,128)(2,1)S(1)}, u32[]{:S(2)}, u32[]{:S(2)}) collective-permute-start(bf16[128,1024]{1,0:T(8,128)(2,1)S(1)} %get-tuple-element.140), channel_id=1, source_target_pairs={{0,3},{1,2},{2,1},{3,0},{4,7},{5,6},{6,5},{7,4},{8,11},{9,10},{10,... | collective-permute-start | bytes 786440 | tf_op jit(solution)/shard_map/ppermute | solution.py:737
  113.1 9.3 %collective-permute-start.21 = (bf16[256,256]{1,0:T(8,128)(2,1)S(1)}, bf16[256,256]{1,0:T(8,128)(2,1)S(1)}, u32[]{:S(2)}, u32[]{:S(2)}) collective-permute-start(bf16[256,256]{1,0:T(8,128)(2,1)S(1)} %pad_maximum_fusion.2), channel_id=1, source_target_pairs={{0,16},{4,20},{8,24},{12,28},{16,0},{20,4},{24,8},{28,12},{1,17},{... | collective-permute-start | bytes 393224 | tf_op jit(solution)/shard_map/ppermute | solution.py:737
  115.7 8.8 %collective-permute-start.22 = (bf16[256,256]{1,0:T(8,128)(2,1)S(1)}, bf16[256,256]{1,0:T(8,128)(2,1)S(1)}, u32[]{:S(2)}, u32[]{:S(2)}) collective-permute-start(bf16[256,256]{1,0:T(8,128)(2,1)S(1)} %pad_maximum_fusion.3), channel_id=1, source_target_pairs={{0,24},{4,28},{8,16},{12,20},{16,8},{20,12},{24,0},{28,4},{1,25},{... | collective-permute-start | bytes 393224 | tf_op jit(solution)/shard_map/ppermute | solution.py:737
  122.3 7.3 %collective-permute-start.38 = (bf16[4,128,256]{2,1,0:T(8,128)(2,1)S(1)}, bf16[4,128,256]{2,1,0:T(8,128)(2,1)S(1)}, u32[]{:S(2)}, u32[]{:S(2)}) collective-permute-start(bf16[4,128,256]{2,1,0:T(8,128)(2,1)S(1)} %get-tuple-element.136), channel_id=1, source_target_pairs={{0,4},{4,0},{8,12},{12,8},{16,20},{20,16},{24,28},{28,24},{1,5},{5... | collective-permute-start | bytes 786440 | tf_op jit(solution)/shard_map/ppermute | solution.py:737
  129.8 7.2 %collective-permute-start.39 = (bf16[128,256]{1,0:T(8,128)(2,1)S(1)}, bf16[128,256]{1,0:T(8,128)(2,1)S(1)}, u32[]{:S(2)}, u32[]{:S(2)}) collective-permute-start(bf16[128,256]{1,0:T(8,128)(2,1)S(1)} %get-tuple-element.156), channel_id=1, source_target_pairs={{0,8},{4,12},{8,0},{12,4},{16,24},{20,28},{24,16},{28,20},{1,9},{5... | collective-permute-start | bytes 196616 | tf_op jit(solution)/shard_map/ppermute | solution.py:737
  130.4 8.4 %collective-permute-start.41 = (bf16[128,256]{1,0:T(8,128)(2,1)S(1)}, bf16[128,256]{1,0:T(8,128)(2,1)S(1)}, u32[]{:S(2)}, u32[]{:S(2)}) collective-permute-start(bf16[128,256]{1,0:T(8,128)(2,1)S(1)} %get-tuple-element.157), channel_id=1, source_target_pairs={{0,24},{4,28},{8,16},{12,20},{16,8},{20,12},{24,0},{28,4},{1,25},{... | collective-permute-start | bytes 196616 | tf_op jit(solution)/shard_map/ppermute | solution.py:737
  132.4 7.1 %collective-permute-start.40 = (bf16[128,256]{1,0:T(8,128)(2,1)S(1)}, bf16[128,256]{1,0:T(8,128)(2,1)S(1)}, u32[]{:S(2)}, u32[]{:S(2)}) collective-permute-start(bf16[128,256]{1,0:T(8,128)(2,1)S(1)} %get-tuple-element.158), channel_id=1, source_target_pairs={{0,16},{4,20},{8,24},{12,28},{16,0},{20,4},{24,8},{28,12},{1,17},{... | collective-permute-start | bytes 196616 | tf_op jit(solution)/shard_map/ppermute | solution.py:737
  134.3 6.5 %collective-permute-start.46 = (bf16[128,256]{1,0:T(8,128)(2,1)S(1)}, bf16[128,256]{1,0:T(8,128)(2,1)S(1)}, u32[]{:S(2)}, u32[]{:S(2)}) collective-permute-start(bf16[128,256]{1,0:T(8,128)(2,1)S(1)} %get-tuple-element.159), channel_id=1, source_target_pairs={{0,8},{4,12},{8,0},{12,4},{16,24},{20,28},{24,16},{28,20},{1,9},{5... | collective-permute-start | bytes 196616 | tf_op jit(solution)/shard_map/ppermute | solution.py:737
  135.4 9.4 %collective-permute-start.48 = (bf16[128,256]{1,0:T(8,128)(2,1)S(1)}, bf16[128,256]{1,0:T(8,128)(2,1)S(1)}, u32[]{:S(2)}, u32[]{:S(2)}) collective-permute-start(bf16[128,256]{1,0:T(8,128)(2,1)S(1)} %get-tuple-element.160), channel_id=1, source_target_pairs={{0,24},{4,28},{8,16},{12,20},{16,8},{20,12},{24,0},{28,4},{1,25},{... | collective-permute-start | bytes 196616 | tf_op jit(solution)/shard_map/ppermute | solution.py:737
  137.0 7.8 %collective-permute-start.47 = (bf16[128,256]{1,0:T(8,128)(2,1)S(1)}, bf16[128,256]{1,0:T(8,128)(2,1)S(1)}, u32[]{:S(2)}, u32[]{:S(2)}) collective-permute-start(bf16[128,256]{1,0:T(8,128)(2,1)S(1)} %get-tuple-element.161), channel_id=1, source_target_pairs={{0,16},{4,20},{8,24},{12,28},{16,0},{20,4},{24,8},{28,12},{1,17},{... | collective-permute-start | bytes 196616 | tf_op jit(solution)/shard_map/ppermute | solution.py:737
  (23 other events, 167.6 us)
